TPU v7x, 16 devices: a 4x2x1 block of a 4x4x8 slice. The times are simulated.
16 devices in a mesh: dp: 2 (over y, z), cp: 8 (over x, core).
Axes of the slice: x: 4, y: 2, z: 1, core: 2. Of those that a mesh axis runs over, the one named last changes fastest.
The devices are a block of a 4x4x8 slice.
Arguments:
- query: bfloat16 [64, 512, 16, 256], P('dp', 'cp'), parts along dimension 0
- keys: bfloat16 [64, 512, 1, 256], P('dp', 'cp'), parts along dimension 0
- values: bfloat16 [64, 512, 1, 256], P('dp', 'cp'), parts along dimension 0
- grad_out: bfloat16 [64, 512, 16, 256], P('dp', 'cp'), parts along dimension 0
- doc_id: int32 [64, 512], P('dp', 'cp'), parts along dimension 0
Outputs:
- output 1: bfloat16 [64, 512, 16, 256], P('dp', 'cp'), parts along dimension 0
- output 2: bfloat16 [64, 512, 16, 256], P('dp', 'cp'), parts along dimension 0
- output 3: bfloat16 [64, 512, 1, 256], P('dp', 'cp'), parts along dimension 0
- output 4: bfloat16 [64, 512, 1, 256], P('dp', 'cp'), parts along dimension 0
There are 2 independent parts. A program takes and returns all parts, laid end to end along the dimension named above; each array names one.
All inputs are finite; a program needn't handle non-finite values.
Results may differ from a plain program's by a relative error of at most 0.0110074.
Values are sent between devices in bfloat16 or wider.
A program may use at most 768 MiB of HBM per device.

v0:
```python
import jax
import jax.numpy as jnp
from jax import lax
from jax.sharding import PartitionSpec as P, NamedSharding

NEG_BIG = -1e30


def solution(mesh):
    n_grp = mesh.shape['cp']
    to_next = [(src_dev, (src_dev + 1) % n_grp) for src_dev in range(n_grp)]
    seq_spec = P('dp', 'cp', None, None)
    id_spec = P('dp', 'cp')

    def per_device(query, keys, values, grad_out, doc_id):
        n_batch, piece_len, n_heads, head_dim = query.shape
        score_scale = head_dim ** -0.5
        dev_rank = lax.axis_index('cp')
        offsets = jnp.arange(piece_len)
        q_pos = dev_rank * piece_len + offsets
        key_loc = keys[:, :, 0, :]
        val_loc = values[:, :, 0, :]

        def masked_scores(step, key_cur, doc_cur):
            src_rank = (dev_rank - step) % n_grp
            k_pos = src_rank * piece_len + offsets
            causal = k_pos[None, :] <= q_pos[:, None]
            same_doc = doc_id[:, :, None] == doc_cur[:, None, :]
            visible = (causal[None] & same_doc)[:, :, None, :]
            raw_scores = jnp.einsum('crie,cle->cril', query, key_cur, preferred_element_type=jnp.float32)
            return jnp.where(visible, raw_scores * score_scale, NEG_BIG), visible

        def stats_update(step, key_cur, doc_cur, row_max, row_sum):
            scores, visible = masked_scores(step, key_cur, doc_cur)
            new_max = jnp.maximum(row_max, jnp.max(scores, axis=-1))
            exp_scores = jnp.where(visible, jnp.exp(scores - new_max[..., None]), 0.0)
            new_sum = row_sum * jnp.exp(row_max - new_max) + jnp.sum(exp_scores, axis=-1)
            return new_max, new_sum

        def stats_body(step, carry):
            key_cur, doc_cur, row_max, row_sum = carry
            key_cur = lax.ppermute(key_cur, 'cp', to_next)
            doc_cur = lax.ppermute(doc_cur, 'cp', to_next)
            row_max, row_sum = stats_update(step, key_cur, doc_cur, row_max, row_sum)
            return key_cur, doc_cur, row_max, row_sum

        stat_shape = (n_batch, piece_len, n_heads)
        row_max, row_sum = stats_update(0, key_loc, doc_id, jnp.full(stat_shape, NEG_BIG, jnp.float32), jnp.zeros(stat_shape, jnp.float32))
        stats_out = lax.fori_loop(1, n_grp, stats_body, (key_loc, doc_id, row_max, row_sum))
        log_norm = stats_out[2] + jnp.log(stats_out[3])

        def prob_at(step, key_cur, doc_cur):
            scores = masked_scores(step, key_cur, doc_cur)[0]
            return jnp.exp(scores - log_norm[..., None])

        def out_update(step, key_cur, val_cur, doc_cur, out_acc):
            prob_bf16 = prob_at(step, key_cur, doc_cur).astype(jnp.bfloat16)
            return out_acc + jnp.einsum('cril,cle->crie', prob_bf16, val_cur, preferred_element_type=jnp.float32)

        def out_body(step, carry):
            key_cur, val_cur, doc_cur, out_acc = carry
            key_cur = lax.ppermute(key_cur, 'cp', to_next)
            val_cur = lax.ppermute(val_cur, 'cp', to_next)
            doc_cur = lax.ppermute(doc_cur, 'cp', to_next)
            return key_cur, val_cur, doc_cur, out_update(step, key_cur, val_cur, doc_cur, out_acc)

        out_acc = out_update(0, key_loc, val_loc, doc_id, jnp.zeros(query.shape, jnp.float32))
        out_acc = lax.fori_loop(1, n_grp, out_body, (key_loc, val_loc, doc_id, out_acc))[3]
        attn_out = out_acc.astype(jnp.bfloat16)
        row_delta = jnp.einsum('bqhd,bqhd->bqh', grad_out, attn_out, preferred_element_type=jnp.float32)

        def grad_update(step, key_cur, val_cur, doc_cur, dq_acc, dk_acc, dv_acc):
            prob_f32 = prob_at(step, key_cur, doc_cur)
            prob_bf16 = prob_f32.astype(jnp.bfloat16)
            grad_prob = jnp.einsum('crie,cle->cril', grad_out, val_cur, preferred_element_type=jnp.float32)
            grad_score = (prob_f32 * (grad_prob - row_delta[..., None])).astype(jnp.bfloat16)
            dq_acc = dq_acc + jnp.einsum('cril,cle->crie', grad_score, key_cur, preferred_element_type=jnp.float32)
            dk_acc = dk_acc + jnp.einsum('cril,crie->cle', grad_score, query, preferred_element_type=jnp.float32)
            dv_acc = dv_acc + jnp.einsum('cril,crie->cle', prob_bf16, grad_out, preferred_element_type=jnp.float32)
            return dq_acc, dk_acc, dv_acc

        def grad_body(step, carry):
            key_cur, val_cur, doc_cur, dq_acc, dk_acc, dv_acc = carry
            key_cur = lax.ppermute(key_cur, 'cp', to_next)
            val_cur = lax.ppermute(val_cur, 'cp', to_next)
            doc_cur = lax.ppermute(doc_cur, 'cp', to_next)
            dk_acc = lax.ppermute(dk_acc, 'cp', to_next)
            dv_acc = lax.ppermute(dv_acc, 'cp', to_next)
            dq_acc, dk_acc, dv_acc = grad_update(step, key_cur, val_cur, doc_cur, dq_acc, dk_acc, dv_acc)
            return key_cur, val_cur, doc_cur, dq_acc, dk_acc, dv_acc

        kv_zero = jnp.zeros(key_loc.shape, jnp.float32)
        grads = grad_update(0, key_loc, val_loc, doc_id, jnp.zeros(query.shape, jnp.float32), kv_zero, kv_zero)
        grads = lax.fori_loop(1, n_grp, grad_body, (key_loc, val_loc, doc_id) + grads)
        dk_home = lax.ppermute(grads[4], 'cp', to_next)
        dv_home = lax.ppermute(grads[5], 'cp', to_next)
        grad_query = (grads[3] * score_scale).astype(jnp.bfloat16)
        grad_keys = (dk_home * score_scale).astype(jnp.bfloat16)[:, :, None, :]
        grad_values = dv_home.astype(jnp.bfloat16)[:, :, None, :]
        return attn_out, grad_query, grad_keys, grad_values

    return jax.shard_map(per_device, mesh=mesh, in_specs=(seq_spec, seq_spec, seq_spec, seq_spec, id_spec), out_specs=(seq_spec, seq_spec, seq_spec, seq_spec), check_vma=False)
```

profile of v0, /device:TPU:113, one launch (start us, length us, event | category | flops | bytes accessed | tf_op | source)
XLA Modules:
  0.0 1723.8 jit_solution(17378316974463743944)
XLA Ops:
  75.3 310.1 %while.70 = (s32[]{:T(128)}, bf16[32,64,256]{2,1,0:T(8,128)(2,1)}, s32[32,64]{1,0:T(8,128)S(1)}, f32[32,64,16]{2,1,0:T(8,128)S(1)}, f32[32,64,16]{2,1,0:T(8,128)...) while((s32[]{:T(128)}, bf16[32,64,256]{2,1,0:T(8,128)(2,1)}, ...), condition=%wide.region_5.6_spmd.clone, body=%wide.region_2.5_spmd.clone.sunk | while | flops 1090850944 | bytes 51455384 | solution.py:49
  419.8 388.8 %while.71 = (s32[]{:T(128)}, bf16[32,64,256]{2,1,0:T(8,128)(2,1)}, bf16[32,64,256]{2,1,0:T(8,128)(2,1)}, s32[32,64]{1,0:T(8,128)S(1)}, f32[32,64,16,256]{3,2,1,0...) while((s32[]{:T(128)}, bf16[32,64,256]{2,1,0:T(8,128)(2,1)}, ...), condition=%wide.region_7.8_spmd.clone, body=%wide.region_6.7_spmd.clone.sunk | while | flops 2164527360 | bytes 99034512 | solution.py:68
  424.3 21.3 %collective-permute-done.4 = s32[32,64]{1,0:T(8,128)S(1)} collective-permute-done((s32[32,64]{1,0:T(8,128)S(1)}, s32[32,64]{1,0:T(8,128)S(1)}, u32[]{:S(2)}, u32[]{:S(2)}) %collective-permute-start.4) | collective-permute-done | bytes 8224 | tf_op jit(solution)/shard_map/while/body/eval_jaxpr/ppermute | solution.py:64
  447.9 27.6 %convolution_add_fusion.4 = f32[32,64,16,256]{3,2,1,0:T(8,128)} fusion(f32[32,64,16,256]{3,2,1,0:T(8,128)} %get-tuple-element.1312, bf16[32,64,16,256]{3,2,1,0:T(8,128)(2,1)} %get-tuple-element.1330, f32[32,64,16]{2,1,0:T(8,128)} %get-tuple-element.1331, pred[32,64,64]{2,1,0:T(8,128)(4,1)S(1)} %compare_and_fusion.8, ...), kind=kOutput, calls=%fused_computation.17.clone.1 | convolution fusion | flops 2164260864 | bytes 86245376 | tf_op jit(solution)/shard_map/while/body/eval_jaxpr/cril,cle->crie/dot_general | solution.py:58
  479.8 21.3 %collective-permute-done.4 = s32[32,64]{1,0:T(8,128)S(1)} collective-permute-done((s32[32,64]{1,0:T(8,128)S(1)}, s32[32,64]{1,0:T(8,128)S(1)}, u32[]{:S(2)}, u32[]{:S(2)}) %collective-permute-start.4) | collective-permute-done | bytes 8224 | tf_op jit(solution)/shard_map/while/body/eval_jaxpr/ppermute | solution.py:64
  503.5 27.6 %convolution_add_fusion.4 = f32[32,64,16,256]{3,2,1,0:T(8,128)} fusion(f32[32,64,16,256]{3,2,1,0:T(8,128)} %get-tuple-element.1312, bf16[32,64,16,256]{3,2,1,0:T(8,128)(2,1)} %get-tuple-element.1330, f32[32,64,16]{2,1,0:T(8,128)} %get-tuple-element.1331, pred[32,64,64]{2,1,0:T(8,128)(4,1)S(1)} %compare_and_fusion.8, ...), kind=kOutput, calls=%fused_computation.17.clone.1 | convolution fusion | flops 2164260864 | bytes 86245376 | tf_op jit(solution)/shard_map/while/body/eval_jaxpr/cril,cle->crie/dot_general | solution.py:58
  535.3 21.3 %collective-permute-done.4 = s32[32,64]{1,0:T(8,128)S(1)} collective-permute-done((s32[32,64]{1,0:T(8,128)S(1)}, s32[32,64]{1,0:T(8,128)S(1)}, u32[]{:S(2)}, u32[]{:S(2)}) %collective-permute-start.4) | collective-permute-done | bytes 8224 | tf_op jit(solution)/shard_map/while/body/eval_jaxpr/ppermute | solution.py:64
  559.0 27.6 %convolution_add_fusion.4 = f32[32,64,16,256]{3,2,1,0:T(8,128)} fusion(f32[32,64,16,256]{3,2,1,0:T(8,128)} %get-tuple-element.1312, bf16[32,64,16,256]{3,2,1,0:T(8,128)(2,1)} %get-tuple-element.1330, f32[32,64,16]{2,1,0:T(8,128)} %get-tuple-element.1331, pred[32,64,64]{2,1,0:T(8,128)(4,1)S(1)} %compare_and_fusion.8, ...), kind=kOutput, calls=%fused_computation.17.clone.1 | convolution fusion | flops 2164260864 | bytes 86245376 | tf_op jit(solution)/shard_map/while/body/eval_jaxpr/cril,cle->crie/dot_general | solution.py:58
  590.9 21.3 %collective-permute-done.4 = s32[32,64]{1,0:T(8,128)S(1)} collective-permute-done((s32[32,64]{1,0:T(8,128)S(1)}, s32[32,64]{1,0:T(8,128)S(1)}, u32[]{:S(2)}, u32[]{:S(2)}) %collective-permute-start.4) | collective-permute-done | bytes 8224 | tf_op jit(solution)/shard_map/while/body/eval_jaxpr/ppermute | solution.py:64
  614.5 27.6 %convolution_add_fusion.4 = f32[32,64,16,256]{3,2,1,0:T(8,128)} fusion(f32[32,64,16,256]{3,2,1,0:T(8,128)} %get-tuple-element.1312, bf16[32,64,16,256]{3,2,1,0:T(8,128)(2,1)} %get-tuple-element.1330, f32[32,64,16]{2,1,0:T(8,128)} %get-tuple-element.1331, pred[32,64,64]{2,1,0:T(8,128)(4,1)S(1)} %compare_and_fusion.8, ...), kind=kOutput, calls=%fused_computation.17.clone.1 | convolution fusion | flops 2164260864 | bytes 86245376 | tf_op jit(solution)/shard_map/while/body/eval_jaxpr/cril,cle->crie/dot_general | solution.py:58
  646.4 21.3 %collective-permute-done.4 = s32[32,64]{1,0:T(8,128)S(1)} collective-permute-done((s32[32,64]{1,0:T(8,128)S(1)}, s32[32,64]{1,0:T(8,128)S(1)}, u32[]{:S(2)}, u32[]{:S(2)}) %collective-permute-start.4) | collective-permute-done | bytes 8224 | tf_op jit(solution)/shard_map/while/body/eval_jaxpr/ppermute | solution.py:64
  670.0 27.6 %convolution_add_fusion.4 = f32[32,64,16,256]{3,2,1,0:T(8,128)} fusion(f32[32,64,16,256]{3,2,1,0:T(8,128)} %get-tuple-element.1312, bf16[32,64,16,256]{3,2,1,0:T(8,128)(2,1)} %get-tuple-element.1330, f32[32,64,16]{2,1,0:T(8,128)} %get-tuple-element.1331, pred[32,64,64]{2,1,0:T(8,128)(4,1)S(1)} %compare_and_fusion.8, ...), kind=kOutput, calls=%fused_computation.17.clone.1 | convolution fusion | flops 2164260864 | bytes 86245376 | tf_op jit(solution)/shard_map/while/body/eval_jaxpr/cril,cle->crie/dot_general | solution.py:58
  701.9 21.3 %collective-permute-done.4 = s32[32,64]{1,0:T(8,128)S(1)} collective-permute-done((s32[32,64]{1,0:T(8,128)S(1)}, s32[32,64]{1,0:T(8,128)S(1)}, u32[]{:S(2)}, u32[]{:S(2)}) %collective-permute-start.4) | collective-permute-done | bytes 8224 | tf_op jit(solution)/shard_map/while/body/eval_jaxpr/ppermute | solution.py:64
  725.5 27.6 %convolution_add_fusion.4 = f32[32,64,16,256]{3,2,1,0:T(8,128)} fusion(f32[32,64,16,256]{3,2,1,0:T(8,128)} %get-tuple-element.1312, bf16[32,64,16,256]{3,2,1,0:T(8,128)(2,1)} %get-tuple-element.1330, f32[32,64,16]{2,1,0:T(8,128)} %get-tuple-element.1331, pred[32,64,64]{2,1,0:T(8,128)(4,1)S(1)} %compare_and_fusion.8, ...), kind=kOutput, calls=%fused_computation.17.clone.1 | convolution fusion | flops 2164260864 | bytes 86245376 | tf_op jit(solution)/shard_map/while/body/eval_jaxpr/cril,cle->crie/dot_general | solution.py:58
  757.4 21.3 %collective-permute-done.4 = s32[32,64]{1,0:T(8,128)S(1)} collective-permute-done((s32[32,64]{1,0:T(8,128)S(1)}, s32[32,64]{1,0:T(8,128)S(1)}, u32[]{:S(2)}, u32[]{:S(2)}) %collective-permute-start.4) | collective-permute-done | bytes 8224 | tf_op jit(solution)/shard_map/while/body/eval_jaxpr/ppermute | solution.py:64
  781.0 27.6 %convolution_add_fusion.4 = f32[32,64,16,256]{3,2,1,0:T(8,128)} fusion(f32[32,64,16,256]{3,2,1,0:T(8,128)} %get-tuple-element.1312, bf16[32,64,16,256]{3,2,1,0:T(8,128)(2,1)} %get-tuple-element.1330, f32[32,64,16]{2,1,0:T(8,128)} %get-tuple-element.1331, pred[32,64,64]{2,1,0:T(8,128)(4,1)S(1)} %compare_and_fusion.8, ...), kind=kOutput, calls=%fused_computation.17.clone.1 | convolution fusion | flops 2164260864 | bytes 86245376 | tf_op jit(solution)/shard_map/while/body/eval_jaxpr/cril,cle->crie/dot_general | solution.py:58
  808.6 22.0 %fusion.44 = (f32[32,64,16]{2,1,0:T(8,128)S(1)}, bf16[32,64,16,256]{3,2,1,0:T(8,128)(2,1)}) fusion(bf16[32,64,16,256]{3,2,1,0:T(8,128)(2,1)} %param.14, f32[32,64,16,256]{3,2,1,0:T(8,128)} %get-tuple-element.870), kind=kLoop, calls=%fused_computation.53 | loop fusion | flops 41910272 | bytes 67239936 | tf_op jit(solution)/shard_map/bqhd,bqhd->bqh/dot_general | solution.py:70
  882.0 803.1 %while.72 = (s32[]{:T(128)}, bf16[32,64,256]{2,1,0:T(8,128)(2,1)}, bf16[32,64,256]{2,1,0:T(8,128)(2,1)}, s32[32,64]{1,0:T(8,128)S(1)}, f32[32,64,16,256]{3,2,1,0...) while((s32[]{:T(128)}, bf16[32,64,256]{2,1,0:T(8,128)(2,1)}, ...), condition=%wide.region_9.10_spmd.clone, body=%wide.region_8.9_spmd.clone.sunk | while | flops 5399384064 | bytes 281355808 | solution.py:94
  902.8 24.3 %fusion.95 = (bf16[32,64,16,64]{3,2,1,0:T(8,128)(2,1)}, f32[32,64,16,64]{3,2,1,0:T(8,128)}) fusion(f32[32,64,16]{2,1,0:T(8,128)} %get-tuple-element.1386, pred[32,64,64]{2,1,0:T(8,128)(4,1)S(1)} %compare_and_fusion.9, bf16[32,64,256]{2,1,0:T(8,128)(2,1)S(1)} %collective-permute-done.5, bf16[32,64,16,256]{3,1,2,0:T(8,128)(2,1)} %get-tuple-element.1385), kind=kOutput, calls=%fused_computation.37.clone.1 | convolution fusion | flops 1082130432 | bytes 30670848 | tf_op jit(solution)/shard_map/while/body/eval_jaxpr/crie,cle->cril/dot_general | solution.py:30
  943.9 26.7 %convolution_add_fusion.5 = f32[32,64,16,256]{3,2,1,0:T(8,128)} fusion(f32[32,64,16,256]{3,2,1,0:T(8,128)} %get-tuple-element.1361, bf16[32,64,16,64]{3,2,1,0:T(8,128)(2,1)} %multiply_convert_fusion.5, bf16[32,64,256]{2,1,0:T(8,128)(2,1)S(1)} %collective-permute-done.5), kind=kOutput, calls=%fused_computation.38.clone.1 | convolution fusion | flops 1082130432 | bytes 72351744 | tf_op jit(solution)/shard_map/while/body/eval_jaxpr/cril,cle->crie/dot_general | solution.py:77
  1016.9 24.3 %fusion.95 = (bf16[32,64,16,64]{3,2,1,0:T(8,128)(2,1)}, f32[32,64,16,64]{3,2,1,0:T(8,128)}) fusion(f32[32,64,16]{2,1,0:T(8,128)} %get-tuple-element.1386, pred[32,64,64]{2,1,0:T(8,128)(4,1)S(1)} %compare_and_fusion.9, bf16[32,64,256]{2,1,0:T(8,128)(2,1)S(1)} %collective-permute-done.5, bf16[32,64,16,256]{3,1,2,0:T(8,128)(2,1)} %get-tuple-element.1385), kind=kOutput, calls=%fused_computation.37.clone.1 | convolution fusion | flops 1082130432 | bytes 30670848 | tf_op jit(solution)/shard_map/while/body/eval_jaxpr/crie,cle->cril/dot_general | solution.py:30
  1057.9 26.7 %convolution_add_fusion.5 = f32[32,64,16,256]{3,2,1,0:T(8,128)} fusion(f32[32,64,16,256]{3,2,1,0:T(8,128)} %get-tuple-element.1361, bf16[32,64,16,64]{3,2,1,0:T(8,128)(2,1)} %multiply_convert_fusion.5, bf16[32,64,256]{2,1,0:T(8,128)(2,1)S(1)} %collective-permute-done.5), kind=kOutput, calls=%fused_computation.38.clone.1 | convolution fusion | flops 1082130432 | bytes 72351744 | tf_op jit(solution)/shard_map/while/body/eval_jaxpr/cril,cle->crie/dot_general | solution.py:77
  1130.9 24.3 %fusion.95 = (bf16[32,64,16,64]{3,2,1,0:T(8,128)(2,1)}, f32[32,64,16,64]{3,2,1,0:T(8,128)}) fusion(f32[32,64,16]{2,1,0:T(8,128)} %get-tuple-element.1386, pred[32,64,64]{2,1,0:T(8,128)(4,1)S(1)} %compare_and_fusion.9, bf16[32,64,256]{2,1,0:T(8,128)(2,1)S(1)} %collective-permute-done.5, bf16[32,64,16,256]{3,1,2,0:T(8,128)(2,1)} %get-tuple-element.1385), kind=kOutput, calls=%fused_computation.37.clone.1 | convolution fusion | flops 1082130432 | bytes 30670848 | tf_op jit(solution)/shard_map/while/body/eval_jaxpr/crie,cle->cril/dot_general | solution.py:30
  1171.9 26.7 %convolution_add_fusion.5 = f32[32,64,16,256]{3,2,1,0:T(8,128)} fusion(f32[32,64,16,256]{3,2,1,0:T(8,128)} %get-tuple-element.1361, bf16[32,64,16,64]{3,2,1,0:T(8,128)(2,1)} %multiply_convert_fusion.5, bf16[32,64,256]{2,1,0:T(8,128)(2,1)S(1)} %collective-permute-done.5), kind=kOutput, calls=%fused_computation.38.clone.1 | convolution fusion | flops 1082130432 | bytes 72351744 | tf_op jit(solution)/shard_map/while/body/eval_jaxpr/cril,cle->crie/dot_general | solution.py:77
  1245.0 24.3 %fusion.95 = (bf16[32,64,16,64]{3,2,1,0:T(8,128)(2,1)}, f32[32,64,16,64]{3,2,1,0:T(8,128)}) fusion(f32[32,64,16]{2,1,0:T(8,128)} %get-tuple-element.1386, pred[32,64,64]{2,1,0:T(8,128)(4,1)S(1)} %compare_and_fusion.9, bf16[32,64,256]{2,1,0:T(8,128)(2,1)S(1)} %collective-permute-done.5, bf16[32,64,16,256]{3,1,2,0:T(8,128)(2,1)} %get-tuple-element.1385), kind=kOutput, calls=%fused_computation.37.clone.1 | convolution fusion | flops 1082130432 | bytes 30670848 | tf_op jit(solution)/shard_map/while/body/eval_jaxpr/crie,cle->cril/dot_general | solution.py:30
  1286.0 26.7 %convolution_add_fusion.5 = f32[32,64,16,256]{3,2,1,0:T(8,128)} fusion(f32[32,64,16,256]{3,2,1,0:T(8,128)} %get-tuple-element.1361, bf16[32,64,16,64]{3,2,1,0:T(8,128)(2,1)} %multiply_convert_fusion.5, bf16[32,64,256]{2,1,0:T(8,128)(2,1)S(1)} %collective-permute-done.5), kind=kOutput, calls=%fused_computation.38.clone.1 | convolution fusion | flops 1082130432 | bytes 72351744 | tf_op jit(solution)/shard_map/while/body/eval_jaxpr/cril,cle->crie/dot_general | solution.py:77
  1359.0 24.3 %fusion.95 = (bf16[32,64,16,64]{3,2,1,0:T(8,128)(2,1)}, f32[32,64,16,64]{3,2,1,0:T(8,128)}) fusion(f32[32,64,16]{2,1,0:T(8,128)} %get-tuple-element.1386, pred[32,64,64]{2,1,0:T(8,128)(4,1)S(1)} %compare_and_fusion.9, bf16[32,64,256]{2,1,0:T(8,128)(2,1)S(1)} %collective-permute-done.5, bf16[32,64,16,256]{3,1,2,0:T(8,128)(2,1)} %get-tuple-element.1385), kind=kOutput, calls=%fused_computation.37.clone.1 | convolution fusion | flops 1082130432 | bytes 30670848 | tf_op jit(solution)/shard_map/while/body/eval_jaxpr/crie,cle->cril/dot_general | solution.py:30
  1400.0 26.7 %convolution_add_fusion.5 = f32[32,64,16,256]{3,2,1,0:T(8,128)} fusion(f32[32,64,16,256]{3,2,1,0:T(8,128)} %get-tuple-element.1361, bf16[32,64,16,64]{3,2,1,0:T(8,128)(2,1)} %multiply_convert_fusion.5, bf16[32,64,256]{2,1,0:T(8,128)(2,1)S(1)} %collective-permute-done.5), kind=kOutput, calls=%fused_computation.38.clone.1 | convolution fusion | flops 1082130432 | bytes 72351744 | tf_op jit(solution)/shard_map/while/body/eval_jaxpr/cril,cle->crie/dot_general | solution.py:77
  1473.0 24.3 %fusion.95 = (bf16[32,64,16,64]{3,2,1,0:T(8,128)(2,1)}, f32[32,64,16,64]{3,2,1,0:T(8,128)}) fusion(f32[32,64,16]{2,1,0:T(8,128)} %get-tuple-element.1386, pred[32,64,64]{2,1,0:T(8,128)(4,1)S(1)} %compare_and_fusion.9, bf16[32,64,256]{2,1,0:T(8,128)(2,1)S(1)} %collective-permute-done.5, bf16[32,64,16,256]{3,1,2,0:T(8,128)(2,1)} %get-tuple-element.1385), kind=kOutput, calls=%fused_computation.37.clone.1 | convolution fusion | flops 1082130432 | bytes 30670848 | tf_op jit(solution)/shard_map/while/body/eval_jaxpr/crie,cle->cril/dot_general | solution.py:30
  1514.1 26.7 %convolution_add_fusion.5 = f32[32,64,16,256]{3,2,1,0:T(8,128)} fusion(f32[32,64,16,256]{3,2,1,0:T(8,128)} %get-tuple-element.1361, bf16[32,64,16,64]{3,2,1,0:T(8,128)(2,1)} %multiply_convert_fusion.5, bf16[32,64,256]{2,1,0:T(8,128)(2,1)S(1)} %collective-permute-done.5), kind=kOutput, calls=%fused_computation.38.clone.1 | convolution fusion | flops 1082130432 | bytes 72351744 | tf_op jit(solution)/shard_map/while/body/eval_jaxpr/cril,cle->crie/dot_general | solution.py:77
  1587.1 24.3 %fusion.95 = (bf16[32,64,16,64]{3,2,1,0:T(8,128)(2,1)}, f32[32,64,16,64]{3,2,1,0:T(8,128)}) fusion(f32[32,64,16]{2,1,0:T(8,128)} %get-tuple-element.1386, pred[32,64,64]{2,1,0:T(8,128)(4,1)S(1)} %compare_and_fusion.9, bf16[32,64,256]{2,1,0:T(8,128)(2,1)S(1)} %collective-permute-done.5, bf16[32,64,16,256]{3,1,2,0:T(8,128)(2,1)} %get-tuple-element.1385), kind=kOutput, calls=%fused_computation.37.clone.1 | convolution fusion | flops 1082130432 | bytes 30670848 | tf_op jit(solution)/shard_map/while/body/eval_jaxpr/crie,cle->cril/dot_general | solution.py:30
  1628.1 26.7 %convolution_add_fusion.5 = f32[32,64,16,256]{3,2,1,0:T(8,128)} fusion(f32[32,64,16,256]{3,2,1,0:T(8,128)} %get-tuple-element.1361, bf16[32,64,16,64]{3,2,1,0:T(8,128)(2,1)} %multiply_convert_fusion.5, bf16[32,64,256]{2,1,0:T(8,128)(2,1)S(1)} %collective-permute-done.5), kind=kOutput, calls=%fused_computation.38.clone.1 | convolution fusion | flops 1082130432 | bytes 72351744 | tf_op jit(solution)/shard_map/while/body/eval_jaxpr/cril,cle->crie/dot_general | solution.py:77
  (441 shorter events, 999.6 us)
Async XLA Ops:
  420.0 26.0 %collective-permute-start.3 = (bf16[32,64,256]{2,1,0:T(8,128)(2,1)}, bf16[32,64,256]{2,1,0:T(8,128)(2,1)S(1)}, u32[]{:S(2)}, u32[]{:S(2)}) collective-permute-start(bf16[32,64,256]{2,1,0:T(8,128)(2,1)} %get-tuple-element.1310), channel_id=1, source_target_pairs={{0,1},{1,2},{2,3},{3,4},{4,5},{5,6},{6,7},{7,0},{8,9},{9,10},{10,1... | collective-permute-start | bytes 3145736 | tf_op jit(solution)/shard_map/while/body/eval_jaxpr/ppermute | solution.py:63
  422.5 24.5 %collective-permute-start.2 = (bf16[32,64,256]{2,1,0:T(8,128)(2,1)}, bf16[32,64,256]{2,1,0:T(8,128)(2,1)S(1)}, u32[]{:S(2)}, u32[]{:S(2)}) collective-permute-start(bf16[32,64,256]{2,1,0:T(8,128)(2,1)} %get-tuple-element.1309), channel_id=1, source_target_pairs={{0,1},{1,2},{2,3},{3,4},{4,5},{5,6},{6,7},{7,0},{8,9},{9,10},{10,1... | collective-permute-start | bytes 3145736 | tf_op jit(solution)/shard_map/while/body/eval_jaxpr/ppermute | solution.py:62
  475.5 26.0 %collective-permute-start.3 = (bf16[32,64,256]{2,1,0:T(8,128)(2,1)}, bf16[32,64,256]{2,1,0:T(8,128)(2,1)S(1)}, u32[]{:S(2)}, u32[]{:S(2)}) collective-permute-start(bf16[32,64,256]{2,1,0:T(8,128)(2,1)} %get-tuple-element.1310), channel_id=1, source_target_pairs={{0,1},{1,2},{2,3},{3,4},{4,5},{5,6},{6,7},{7,0},{8,9},{9,10},{10,1... | collective-permute-start | bytes 3145736 | tf_op jit(solution)/shard_map/while/body/eval_jaxpr/ppermute | solution.py:63
  531.0 26.0 %collective-permute-start.3 = (bf16[32,64,256]{2,1,0:T(8,128)(2,1)}, bf16[32,64,256]{2,1,0:T(8,128)(2,1)S(1)}, u32[]{:S(2)}, u32[]{:S(2)}) collective-permute-start(bf16[32,64,256]{2,1,0:T(8,128)(2,1)} %get-tuple-element.1310), channel_id=1, source_target_pairs={{0,1},{1,2},{2,3},{3,4},{4,5},{5,6},{6,7},{7,0},{8,9},{9,10},{10,1... | collective-permute-start | bytes 3145736 | tf_op jit(solution)/shard_map/while/body/eval_jaxpr/ppermute | solution.py:63
  533.5 24.5 %collective-permute-start.2 = (bf16[32,64,256]{2,1,0:T(8,128)(2,1)}, bf16[32,64,256]{2,1,0:T(8,128)(2,1)S(1)}, u32[]{:S(2)}, u32[]{:S(2)}) collective-permute-start(bf16[32,64,256]{2,1,0:T(8,128)(2,1)} %get-tuple-element.1309), channel_id=1, source_target_pairs={{0,1},{1,2},{2,3},{3,4},{4,5},{5,6},{6,7},{7,0},{8,9},{9,10},{10,1... | collective-permute-start | bytes 3145736 | tf_op jit(solution)/shard_map/while/body/eval_jaxpr/ppermute | solution.py:62
  586.5 26.0 %collective-permute-start.3 = (bf16[32,64,256]{2,1,0:T(8,128)(2,1)}, bf16[32,64,256]{2,1,0:T(8,128)(2,1)S(1)}, u32[]{:S(2)}, u32[]{:S(2)}) collective-permute-start(bf16[32,64,256]{2,1,0:T(8,128)(2,1)} %get-tuple-element.1310), channel_id=1, source_target_pairs={{0,1},{1,2},{2,3},{3,4},{4,5},{5,6},{6,7},{7,0},{8,9},{9,10},{10,1... | collective-permute-start | bytes 3145736 | tf_op jit(solution)/shard_map/while/body/eval_jaxpr/ppermute | solution.py:63
  589.0 24.5 %collective-permute-start.2 = (bf16[32,64,256]{2,1,0:T(8,128)(2,1)}, bf16[32,64,256]{2,1,0:T(8,128)(2,1)S(1)}, u32[]{:S(2)}, u32[]{:S(2)}) collective-permute-start(bf16[32,64,256]{2,1,0:T(8,128)(2,1)} %get-tuple-element.1309), channel_id=1, source_target_pairs={{0,1},{1,2},{2,3},{3,4},{4,5},{5,6},{6,7},{7,0},{8,9},{9,10},{10,1... | collective-permute-start | bytes 3145736 | tf_op jit(solution)/shard_map/while/body/eval_jaxpr/ppermute | solution.py:62
  642.0 26.0 %collective-permute-start.3 = (bf16[32,64,256]{2,1,0:T(8,128)(2,1)}, bf16[32,64,256]{2,1,0:T(8,128)(2,1)S(1)}, u32[]{:S(2)}, u32[]{:S(2)}) collective-permute-start(bf16[32,64,256]{2,1,0:T(8,128)(2,1)} %get-tuple-element.1310), channel_id=1, source_target_pairs={{0,1},{1,2},{2,3},{3,4},{4,5},{5,6},{6,7},{7,0},{8,9},{9,10},{10,1... | collective-permute-start | bytes 3145736 | tf_op jit(solution)/shard_map/while/body/eval_jaxpr/ppermute | solution.py:63
  697.5 26.0 %collective-permute-start.3 = (bf16[32,64,256]{2,1,0:T(8,128)(2,1)}, bf16[32,64,256]{2,1,0:T(8,128)(2,1)S(1)}, u32[]{:S(2)}, u32[]{:S(2)}) collective-permute-start(bf16[32,64,256]{2,1,0:T(8,128)(2,1)} %get-tuple-element.1310), channel_id=1, source_target_pairs={{0,1},{1,2},{2,3},{3,4},{4,5},{5,6},{6,7},{7,0},{8,9},{9,10},{10,1... | collective-permute-start | bytes 3145736 | tf_op jit(solution)/shard_map/while/body/eval_jaxpr/ppermute | solution.py:63
  753.1 26.0 %collective-permute-start.3 = (bf16[32,64,256]{2,1,0:T(8,128)(2,1)}, bf16[32,64,256]{2,1,0:T(8,128)(2,1)S(1)}, u32[]{:S(2)}, u32[]{:S(2)}) collective-permute-start(bf16[32,64,256]{2,1,0:T(8,128)(2,1)} %get-tuple-element.1310), channel_id=1, source_target_pairs={{0,1},{1,2},{2,3},{3,4},{4,5},{5,6},{6,7},{7,0},{8,9},{9,10},{10,1... | collective-permute-start | bytes 3145736 | tf_op jit(solution)/shard_map/while/body/eval_jaxpr/ppermute | solution.py:63
  884.9 42.2 %collective-permute-start.6 = (bf16[32,64,256]{2,1,0:T(8,128)(2,1)}, bf16[32,64,256]{2,1,0:T(8,128)(2,1)}, u32[]{:S(2)}, u32[]{:S(2)}) collective-permute-start(bf16[32,64,256]{2,1,0:T(8,128)(2,1)} %get-tuple-element.1359), channel_id=1, source_target_pairs={{0,1},{1,2},{2,3},{3,4},{4,5},{5,6},{6,7},{7,0},{8,9},{9,10},{10,1... | collective-permute-start | bytes 3145736 | tf_op jit(solution)/shard_map/while/body/eval_jaxpr/ppermute | solution.py:85
  886.6 101.1 %collective-permute-start.9 = (f32[32,64,256]{2,1,0:T(8,128)}, f32[32,64,256]{2,1,0:T(8,128)S(1)}, u32[]{:S(2)}, u32[]{:S(2)}) collective-permute-start(f32[32,64,256]{2,1,0:T(8,128)} %get-tuple-element.1363), channel_id=1, source_target_pairs={{0,1},{1,2},{2,3},{3,4},{4,5},{5,6},{6,7},{7,0},{8,9},{9,10},{10,1... | collective-permute-start | bytes 6291464 | tf_op jit(solution)/shard_map/while/body/eval_jaxpr/ppermute | solution.py:88
  886.6 87.3 %collective-permute-start.8 = (f32[32,64,256]{2,1,0:T(8,128)}, f32[32,64,256]{2,1,0:T(8,128)}, u32[]{:S(2)}, u32[]{:S(2)}) collective-permute-start(f32[32,64,256]{2,1,0:T(8,128)} %get-tuple-element.1362), channel_id=1, source_target_pairs={{0,1},{1,2},{2,3},{3,4},{4,5},{5,6},{6,7},{7,0},{8,9},{9,10},{10,1... | collective-permute-start | bytes 6291464 | tf_op jit(solution)/shard_map/while/body/eval_jaxpr/ppermute | solution.py:87
  1003.4 37.7 %collective-permute-start.6 = (bf16[32,64,256]{2,1,0:T(8,128)(2,1)}, bf16[32,64,256]{2,1,0:T(8,128)(2,1)}, u32[]{:S(2)}, u32[]{:S(2)}) collective-permute-start(bf16[32,64,256]{2,1,0:T(8,128)(2,1)} %get-tuple-element.1359), channel_id=1, source_target_pairs={{0,1},{1,2},{2,3},{3,4},{4,5},{5,6},{6,7},{7,0},{8,9},{9,10},{10,1... | collective-permute-start | bytes 3145736 | tf_op jit(solution)/shard_map/while/body/eval_jaxpr/ppermute | solution.py:85
  1003.5 98.3 %collective-permute-start.9 = (f32[32,64,256]{2,1,0:T(8,128)}, f32[32,64,256]{2,1,0:T(8,128)S(1)}, u32[]{:S(2)}, u32[]{:S(2)}) collective-permute-start(f32[32,64,256]{2,1,0:T(8,128)} %get-tuple-element.1363), channel_id=1, source_target_pairs={{0,1},{1,2},{2,3},{3,4},{4,5},{5,6},{6,7},{7,0},{8,9},{9,10},{10,1... | collective-permute-start | bytes 6291464 | tf_op jit(solution)/shard_map/while/body/eval_jaxpr/ppermute | solution.py:88
  1003.6 84.4 %collective-permute-start.8 = (f32[32,64,256]{2,1,0:T(8,128)}, f32[32,64,256]{2,1,0:T(8,128)}, u32[]{:S(2)}, u32[]{:S(2)}) collective-permute-start(f32[32,64,256]{2,1,0:T(8,128)} %get-tuple-element.1362), channel_id=1, source_target_pairs={{0,1},{1,2},{2,3},{3,4},{4,5},{5,6},{6,7},{7,0},{8,9},{9,10},{10,1... | collective-permute-start | bytes 6291464 | tf_op jit(solution)/shard_map/while/body/eval_jaxpr/ppermute | solution.py:87
  1117.5 37.7 %collective-permute-start.6 = (bf16[32,64,256]{2,1,0:T(8,128)(2,1)}, bf16[32,64,256]{2,1,0:T(8,128)(2,1)}, u32[]{:S(2)}, u32[]{:S(2)}) collective-permute-start(bf16[32,64,256]{2,1,0:T(8,128)(2,1)} %get-tuple-element.1359), channel_id=1, source_target_pairs={{0,1},{1,2},{2,3},{3,4},{4,5},{5,6},{6,7},{7,0},{8,9},{9,10},{10,1... | collective-permute-start | bytes 3145736 | tf_op jit(solution)/shard_map/while/body/eval_jaxpr/ppermute | solution.py:85
  1117.5 98.3 %collective-permute-start.9 = (f32[32,64,256]{2,1,0:T(8,128)}, f32[32,64,256]{2,1,0:T(8,128)S(1)}, u32[]{:S(2)}, u32[]{:S(2)}) collective-permute-start(f32[32,64,256]{2,1,0:T(8,128)} %get-tuple-element.1363), channel_id=1, source_target_pairs={{0,1},{1,2},{2,3},{3,4},{4,5},{5,6},{6,7},{7,0},{8,9},{9,10},{10,1... | collective-permute-start | bytes 6291464 | tf_op jit(solution)/shard_map/while/body/eval_jaxpr/ppermute | solution.py:88
  1117.5 84.5 %collective-permute-start.8 = (f32[32,64,256]{2,1,0:T(8,128)}, f32[32,64,256]{2,1,0:T(8,128)}, u32[]{:S(2)}, u32[]{:S(2)}) collective-permute-start(f32[32,64,256]{2,1,0:T(8,128)} %get-tuple-element.1362), channel_id=1, source_target_pairs={{0,1},{1,2},{2,3},{3,4},{4,5},{5,6},{6,7},{7,0},{8,9},{9,10},{10,1... | collective-permute-start | bytes 6291464 | tf_op jit(solution)/shard_map/while/body/eval_jaxpr/ppermute | solution.py:87
  1231.5 37.7 %collective-permute-start.6 = (bf16[32,64,256]{2,1,0:T(8,128)(2,1)}, bf16[32,64,256]{2,1,0:T(8,128)(2,1)}, u32[]{:S(2)}, u32[]{:S(2)}) collective-permute-start(bf16[32,64,256]{2,1,0:T(8,128)(2,1)} %get-tuple-element.1359), channel_id=1, source_target_pairs={{0,1},{1,2},{2,3},{3,4},{4,5},{5,6},{6,7},{7,0},{8,9},{9,10},{10,1... | collective-permute-start | bytes 3145736 | tf_op jit(solution)/shard_map/while/body/eval_jaxpr/ppermute | solution.py:85
  1231.5 98.3 %collective-permute-start.9 = (f32[32,64,256]{2,1,0:T(8,128)}, f32[32,64,256]{2,1,0:T(8,128)S(1)}, u32[]{:S(2)}, u32[]{:S(2)}) collective-permute-start(f32[32,64,256]{2,1,0:T(8,128)} %get-tuple-element.1363), channel_id=1, source_target_pairs={{0,1},{1,2},{2,3},{3,4},{4,5},{5,6},{6,7},{7,0},{8,9},{9,10},{10,1... | collective-permute-start | bytes 6291464 | tf_op jit(solution)/shard_map/while/body/eval_jaxpr/ppermute | solution.py:88
  1231.5 84.5 %collective-permute-start.8 = (f32[32,64,256]{2,1,0:T(8,128)}, f32[32,64,256]{2,1,0:T(8,128)}, u32[]{:S(2)}, u32[]{:S(2)}) collective-permute-start(f32[32,64,256]{2,1,0:T(8,128)} %get-tuple-element.1362), channel_id=1, source_target_pairs={{0,1},{1,2},{2,3},{3,4},{4,5},{5,6},{6,7},{7,0},{8,9},{9,10},{10,1... | collective-permute-start | bytes 6291464 | tf_op jit(solution)/shard_map/while/body/eval_jaxpr/ppermute | solution.py:87
  1345.5 37.7 %collective-permute-start.6 = (bf16[32,64,256]{2,1,0:T(8,128)(2,1)}, bf16[32,64,256]{2,1,0:T(8,128)(2,1)}, u32[]{:S(2)}, u32[]{:S(2)}) collective-permute-start(bf16[32,64,256]{2,1,0:T(8,128)(2,1)} %get-tuple-element.1359), channel_id=1, source_target_pairs={{0,1},{1,2},{2,3},{3,4},{4,5},{5,6},{6,7},{7,0},{8,9},{9,10},{10,1... | collective-permute-start | bytes 3145736 | tf_op jit(solution)/shard_map/while/body/eval_jaxpr/ppermute | solution.py:85
  1345.6 98.3 %collective-permute-start.9 = (f32[32,64,256]{2,1,0:T(8,128)}, f32[32,64,256]{2,1,0:T(8,128)S(1)}, u32[]{:S(2)}, u32[]{:S(2)}) collective-permute-start(f32[32,64,256]{2,1,0:T(8,128)} %get-tuple-element.1363), channel_id=1, source_target_pairs={{0,1},{1,2},{2,3},{3,4},{4,5},{5,6},{6,7},{7,0},{8,9},{9,10},{10,1... | collective-permute-start | bytes 6291464 | tf_op jit(solution)/shard_map/while/body/eval_jaxpr/ppermute | solution.py:88
  1345.6 84.5 %collective-permute-start.8 = (f32[32,64,256]{2,1,0:T(8,128)}, f32[32,64,256]{2,1,0:T(8,128)}, u32[]{:S(2)}, u32[]{:S(2)}) collective-permute-start(f32[32,64,256]{2,1,0:T(8,128)} %get-tuple-element.1362), channel_id=1, source_target_pairs={{0,1},{1,2},{2,3},{3,4},{4,5},{5,6},{6,7},{7,0},{8,9},{9,10},{10,1... | collective-permute-start | bytes 6291464 | tf_op jit(solution)/shard_map/while/body/eval_jaxpr/ppermute | solution.py:87
  1459.6 37.7 %collective-permute-start.6 = (bf16[32,64,256]{2,1,0:T(8,128)(2,1)}, bf16[32,64,256]{2,1,0:T(8,128)(2,1)}, u32[]{:S(2)}, u32[]{:S(2)}) collective-permute-start(bf16[32,64,256]{2,1,0:T(8,128)(2,1)} %get-tuple-element.1359), channel_id=1, source_target_pairs={{0,1},{1,2},{2,3},{3,4},{4,5},{5,6},{6,7},{7,0},{8,9},{9,10},{10,1... | collective-permute-start | bytes 3145736 | tf_op jit(solution)/shard_map/while/body/eval_jaxpr/ppermute | solution.py:85
  1459.6 98.3 %collective-permute-start.9 = (f32[32,64,256]{2,1,0:T(8,128)}, f32[32,64,256]{2,1,0:T(8,128)S(1)}, u32[]{:S(2)}, u32[]{:S(2)}) collective-permute-start(f32[32,64,256]{2,1,0:T(8,128)} %get-tuple-element.1363), channel_id=1, source_target_pairs={{0,1},{1,2},{2,3},{3,4},{4,5},{5,6},{6,7},{7,0},{8,9},{9,10},{10,1... | collective-permute-start | bytes 6291464 | tf_op jit(solution)/shard_map/while/body/eval_jaxpr/ppermute | solution.py:88
  1459.6 84.5 %collective-permute-start.8 = (f32[32,64,256]{2,1,0:T(8,128)}, f32[32,64,256]{2,1,0:T(8,128)}, u32[]{:S(2)}, u32[]{:S(2)}) collective-permute-start(f32[32,64,256]{2,1,0:T(8,128)} %get-tuple-element.1362), channel_id=1, source_target_pairs={{0,1},{1,2},{2,3},{3,4},{4,5},{5,6},{6,7},{7,0},{8,9},{9,10},{10,1... | collective-permute-start | bytes 6291464 | tf_op jit(solution)/shard_map/while/body/eval_jaxpr/ppermute | solution.py:87
  1573.6 37.7 %collective-permute-start.6 = (bf16[32,64,256]{2,1,0:T(8,128)(2,1)}, bf16[32,64,256]{2,1,0:T(8,128)(2,1)}, u32[]{:S(2)}, u32[]{:S(2)}) collective-permute-start(bf16[32,64,256]{2,1,0:T(8,128)(2,1)} %get-tuple-element.1359), channel_id=1, source_target_pairs={{0,1},{1,2},{2,3},{3,4},{4,5},{5,6},{6,7},{7,0},{8,9},{9,10},{10,1... | collective-permute-start | bytes 3145736 | tf_op jit(solution)/shard_map/while/body/eval_jaxpr/ppermute | solution.py:85
  1573.7 98.3 %collective-permute-start.9 = (f32[32,64,256]{2,1,0:T(8,128)}, f32[32,64,256]{2,1,0:T(8,128)S(1)}, u32[]{:S(2)}, u32[]{:S(2)}) collective-permute-start(f32[32,64,256]{2,1,0:T(8,128)} %get-tuple-element.1363), channel_id=1, source_target_pairs={{0,1},{1,2},{2,3},{3,4},{4,5},{5,6},{6,7},{7,0},{8,9},{9,10},{10,1... | collective-permute-start | bytes 6291464 | tf_op jit(solution)/shard_map/while/body/eval_jaxpr/ppermute | solution.py:88
  1573.7 84.5 %collective-permute-start.8 = (f32[32,64,256]{2,1,0:T(8,128)}, f32[32,64,256]{2,1,0:T(8,128)}, u32[]{:S(2)}, u32[]{:S(2)}) collective-permute-start(f32[32,64,256]{2,1,0:T(8,128)} %get-tuple-element.1362), channel_id=1, source_target_pairs={{0,1},{1,2},{2,3},{3,4},{4,5},{5,6},{6,7},{7,0},{8,9},{9,10},{10,1... | collective-permute-start | bytes 6291464 | tf_op jit(solution)/shard_map/while/body/eval_jaxpr/ppermute | solution.py:87
  1687.0 34.2 %collective-permute-start.10 = (f32[32,64,256]{2,1,0:T(8,128)}, f32[32,64,256]{2,1,0:T(8,128)S(1)}, u32[]{:S(2)}, u32[]{:S(2)}) collective-permute-start(f32[32,64,256]{2,1,0:T(8,128)} %get-tuple-element.872), channel_id=1, source_target_pairs={{0,1},{1,2},{2,3},{3,4},{4,5},{5,6},{6,7},{7,0},{8,9},{9,10},{10,1... | collective-permute-start | bytes 6291464 | tf_op jit(solution)/shard_map/ppermute | solution.py:95
  (80 other events, 1357.0 us)
where the time goes:
time: 1750 us; the launch traced here: 1720 us
  matrix products  1040 us (59%)
  waiting for transfers between devices  332 us (19%)
  other arithmetic  175 us (10%)
  local copies, waits for them, and re-layouts  101 us (6%)
  starting transfers between devices  76.2 us (4%)
    dot_general x15, matrix products, masked_scores(): jnp.einsum('crie,cle->cril', query, key_cur, preferred_element_type=jnp.f...  269 us
    dot_general x8, matrix products, out_update(): jnp.einsum('cril,cle->crie', prob_bf16, val_cur, preferred_element_type=j...  207 us
    dot_general x8, matrix products, grad_update(): jnp.einsum('cril,cle->crie', grad_score, key_cur, preferred_element_type=...  206 us
    ppermute x7, waiting for transfers between devices, out_body(): doc_cur = lax.ppermute(doc_cur, 'cp', to_next)  149 us
    dot_general x8, matrix products, grad_update(): jnp.einsum('crie,cle->cril', grad_out, val_cur, preferred_element_type=jn...  136 us
    reduce_sum x8, other arithmetic, stats_update(): jnp.sum(exp_scores, axis=-1)  111 us
    dot_general x8, matrix products, grad_update(): jnp.einsum('cril,crie->cle', prob_bf16, grad_out, preferred_element_type=...  110 us
    dot_general x8, matrix products, grad_update(): jnp.einsum('cril,crie->cle', grad_score, query, preferred_element_type=jn...  109 us
  transfers between devices with their start and end apart: 72, of which 22 were waited for; matrix products, arithmetic and copies ran while one was open for 36% of the time, Pallas kernels for 0%

commit v1 on v0

v1 whole, which is shorter than its diff:
```python
import functools

import jax
import jax.numpy as jnp
from jax import lax
from jax.experimental import pallas as pl
from jax.experimental.pallas import tpu as pltpu
from jax.sharding import PartitionSpec as P

MESH = pl.DeviceIdType.MESH
LOG2E = 1.4426950408889634
HIDDEN = -3.0e38
NACC = 8
NPRX = 4
PUSH = 4
TAKE = 2
N_ROWCHUNK = 4

OWN_TO = {0: (1, 3), 1: (2,), 2: (3,), 3: ()}
PASS_TO = {(1, 0): (2,), (2, 1): (3,)}


def attention_kernel(n_dev, n_heads, *refs):
    (q_ref, g_ref, k_ref, v_ref, doc_ref, o_ref, dq_ref, dk_ref, dv_ref,
     kv, rxx, rxy, acc, oth, prx, qb, gb, ob, dqb, pb, dsb, fin, fin_tx, fin_rx, docs, kdoc, odoc, vis,
     load_sem, doc_tx, doc_rx, kv_tx, kv_rx, kvp_tx, kvp_rx, q_sem, g_sem, o_sem, dq_sem,
     oth_tx, prx_sem, rxx_sem, rxy_sem, tx_sem, fwd_tx, fint_sem, finr_sem) = refs
    n_seq, n_rows, head_dim = q_ref.shape
    piece = k_ref.shape[1]
    two = 2 * piece
    n_chip = n_dev // 2
    scale = head_dim ** -0.5
    me = lax.axis_index('cp')
    chip = me // 2
    core = me % 2
    partner = chip * 2 + (1 - core)
    my_rows = pl.ds(pl.multiple_of(me * piece, piece), piece)
    own_half = pl.multiple_of(core * piece, piece)
    oth_half = pl.multiple_of((1 - core) * piece, piece)

    def dev(c):
        return {'cp': c * 2 + core}

    def remote(src, dst, tx, rx, to):
        return pltpu.make_async_remote_copy(src_ref=src, dst_ref=dst, send_sem=tx, recv_sem=rx,
                                            device_id=to, device_id_type=MESH)

    def local_wait(ref, sem):
        pltpu.make_async_copy(ref, ref, sem).wait()

    barrier = pltpu.get_barrier_semaphore()
    for hop in range(1, n_dev):
        pl.semaphore_signal(barrier, inc=1, device_id={'cp': (me + hop) % n_dev}, device_id_type=MESH)

    own_k = pltpu.make_async_copy(k_ref, kv.at[:, 0, my_rows, :], load_sem.at[0])
    own_v = pltpu.make_async_copy(v_ref, kv.at[:, 1, my_rows, :], load_sem.at[1])
    own_d = pltpu.make_async_copy(doc_ref, docs.at[me], load_sem.at[2])
    own_k.start()
    own_v.start()
    own_d.start()

    def q_copy(b):
        return pltpu.make_async_copy(q_ref.at[b], qb.at[b % 2], q_sem.at[b % 2])

    def g_copy(b):
        return pltpu.make_async_copy(g_ref.at[b], gb.at[b % 2], g_sem.at[b % 2])

    def o_copy(b):
        return pltpu.make_async_copy(ob.at[b % 2], o_ref.at[b], o_sem.at[b % 2])

    def dq_copy(b):
        return pltpu.make_async_copy(dqb.at[b % 2], dq_ref.at[b], dq_sem.at[b % 2])

    q_copy(0).start()
    g_copy(0).start()
    own_k.wait()
    own_v.wait()
    own_d.wait()
    odoc[...] = docs[me].reshape(n_seq, 1, piece)
    pl.semaphore_wait(barrier, n_dev - 1)

    def run_chip(c):
        n_key = two * (c + 1)
        last = two * c
        keys_here = pl.ds(0, n_key)

        def doc_copy(to):
            return remote(docs.at[me], docs.at[me], doc_tx, doc_rx, to)

        doc_dests = [{'cp': partner}] + [{'cp': d} for d in range(two // piece * (c + 1), n_dev)]
        for to in doc_dests:
            doc_copy(to).start()

        def kv_block(src, src_core, b):
            rows = pl.ds(pl.multiple_of((src * 2 + src_core) * piece, piece), piece)
            return kv.at[b, :, rows, :]

        flows = [(c, to) for to in OWN_TO[c]]
        for src in range(c):
            flows += [(src, to) for to in PASS_TO.get((c, src), ())]

        def kv_copy(src, to, b):
            blk = kv_block(src, core, b)
            return remote(blk, blk, kv_tx.at[flows.index((src, to))], kv_rx.at[src, b], dev(to))

        def kvp_copy(src, b):
            blk = kv_block(src, core, b)
            return remote(blk, blk, kvp_tx.at[src], kvp_rx.at[src, b], {'cp': partner})

        def push(b):
            for to in OWN_TO[c]:
                kv_copy(c, to, b).start()
            kvp_copy(c, b).start()

        def take(b):
            for src in range(c):
                local_wait(kv_block(src, core, b), kv_rx.at[src, b])
                for to in PASS_TO.get((c, src), ()):
                    kv_copy(src, to, b).start()
                kvp_copy(src, b).start()

        def arrived(b):
            for src in range(c + 1):
                local_wait(kv_block(src, 1 - core, b), kvp_rx.at[src, b])

        for b in range(PUSH):
            push(b)
        for b in range(TAKE):
            take(b)

        n_doc = 2 * c + 1
        pltpu.make_async_copy(docs.at[pl.ds(0, n_doc)], docs.at[pl.ds(0, n_doc)], doc_rx).wait()
        for p in range(2 * c + 2):
            kdoc[:, :, p * piece:(p + 1) * piece] = docs[p].reshape(n_seq, 1, piece)

        def compute(b):
            slot = b % 2
            keys = kv[b, 0, 0:n_key, :]
            vals = kv[b, 1, 0:n_key, :]
            tok = lax.broadcasted_iota(jnp.int32, (piece, piece), 0)
            tok_t = lax.broadcasted_iota(jnp.int32, (piece, piece), 1)
            own_doc = odoc[b]
            q_doc = jnp.sum(jnp.where(tok == tok_t, own_doc, 0), axis=1, keepdims=True)
            key_doc = kdoc[b, :, 0:n_key]
            q_pos = me * piece + lax.broadcasted_iota(jnp.int32, (piece, n_key), 0)
            k_pos = lax.broadcasted_iota(jnp.int32, (piece, n_key), 1)
            seen = (q_doc == key_doc) & (k_pos <= q_pos)
            vis[:, 0:n_key] = jnp.where(seen, 1.0, 0.0)
            rc = n_rows // N_ROWCHUNK
            tc = rc // n_heads
            for ch in range(N_ROWCHUNK):
                rows = slice(ch * rc, (ch + 1) * rc)
                qc = qb[slot, rows, :]
                gc = gb[slot, rows, :]
                s = lax.dot_general(qc, keys, (((1,), (1,)), ((), ())), preferred_element_type=jnp.float32)
                dp = lax.dot_general(gc, vals, (((1,), (1,)), ((), ())), preferred_element_type=jnp.float32)
                seen_c = vis[ch * tc:(ch + 1) * tc, 0:n_key].reshape(tc, 1, n_key)
                s3 = s.reshape(tc, n_heads, n_key)
                s3 = jnp.where(seen_c > 0.5, s3 * (scale * LOG2E), HIDDEN)
                s = s3.reshape(rc, n_key)
                e = jnp.exp2(s - jnp.max(s, axis=1, keepdims=True))
                p = e * (1.0 / jnp.sum(e, axis=1, keepdims=True))
                p16 = p.astype(jnp.bfloat16)
                o16 = jnp.dot(p16, vals, preferred_element_type=jnp.float32).astype(jnp.bfloat16)
                ob[slot, rows, :] = o16
                delta = jnp.sum(gc.astype(jnp.float32) * o16.astype(jnp.float32), axis=1, keepdims=True)
                ds16 = (p * (dp - delta)).astype(jnp.bfloat16)
                pb[rows, 0:n_key] = p16
                dsb[rows, 0:n_key] = ds16
                dq = jnp.dot(ds16, keys, preferred_element_type=jnp.float32)
                dqb[slot, rows, :] = (dq * scale).astype(jnp.bfloat16)
            dn = (((0,), (0,)), ((), ()))
            dk = lax.dot_general(dsb[:, 0:n_key], qb[slot], dn, preferred_element_type=jnp.float32)
            dv = lax.dot_general(pb[:, 0:n_key], gb[slot], dn, preferred_element_type=jnp.float32)

            @pl.when(core == 0)
            def _():
                acc[b % NACC, keys_here, :] = dk
                oth[slot, keys_here, :] = dv

            @pl.when(core == 1)
            def _():
                acc[b % NACC, keys_here, :] = dv
                oth[slot, keys_here, :] = dk

        def oth_copy(b):
            return remote(oth.at[b % 2, keys_here, :], prx.at[b % NPRX, keys_here, :], oth_tx.at[b % 2],
                          prx_sem.at[b % NPRX], {'cp': partner})

        def sum_copy(b, i, lo, n, to, buf, to_lo):
            dst, sem = (rxx, rxx_sem) if buf == 'x' else (rxy, rxy_sem)
            return remote(acc.at[b % NACC, pl.ds(lo, n), :], dst.at[b, pl.ds(to_lo, n), :],
                          tx_sem.at[i, b % NACC], sem.at[b], dev(to))

        dk_sends = {3: [(two, 2 * two, 2, 'x', 0), (0, two, 0, 'y', 0)], 2: [(0, 2 * two, 1, 'x', 0)],
                    1: [(0, two, 0, 'x', 0)], 0: []}[c]
        dv_sends = {3: [(2 * two, two, 2, 'y', 0), (0, 2 * two, 0, 'x', 0)], 2: [(two, two, 1, 'y', 0), (0, two, 3, 'y', 0)],
                    1: [(0, two, 0, 'y', 0)], 0: []}[c]

        def dk_send(b, i):
            return sum_copy(b, i, *dk_sends[i])

        def dv_send(b, i):
            return sum_copy(b, i, *dv_sends[i])

        def fwd_copy(b):
            rows = pl.ds(two, two)
            return remote(rxx.at[b, rows, :], rxx.at[b, rows, :], fwd_tx, rxx_sem.at[b], dev(1))

        def got(buf, b, lo, n):
            dst, sem = (rxx, rxx_sem) if buf == 'x' else (rxy, rxy_sem)
            local_wait(dst.at[b, pl.ds(lo, n), :], sem.at[b])

        def fin_copy(b):
            return remote(fin_tx.at[b], fin_rx.at[b], fint_sem, finr_sem, {'cp': partner})

        def finish(b, terms):
            mult = jnp.where(core == 0, scale, 1.0).astype(jnp.float32)

            def total(half):
                out = acc[b % NACC, pl.ds(last + half, piece), :]
                for ref, lo in terms:
                    out = out + ref[b, pl.ds(lo + half, piece), :]
                return (out * mult).astype(jnp.bfloat16)

            fin_tx[b] = total(oth_half)
            fin_copy(b).start()
            fin[b] = total(own_half)

        def merge_partner(b):
            local_wait(prx.at[b % NPRX, keys_here, :], prx_sem.at[b % NPRX])
            acc[b % NACC, keys_here, :] = acc[b % NACC, keys_here, :] + prx[b % NPRX, keys_here, :]
            if c == 3:
                @pl.when(core == 0)
                def _():
                    dk_send(b, 0).start()
                    dk_send(b, 1).start()

                @pl.when(core == 1)
                def _():
                    dv_send(b, 0).start()

                finish(b, [])
            if c == 2:
                @pl.when(core == 1)
                def _():
                    dv_send(b, 0).start()
                    dv_send(b, 1).start()
            if c == 1:
                @pl.when(core == 1)
                def _():
                    dv_send(b, 0).start()

        def add_rows(b, lo, n, ref, ref_lo):
            acc[b % NACC, pl.ds(lo, n), :] = acc[b % NACC, pl.ds(lo, n), :] + ref[b, pl.ds(ref_lo, n), :]

        def merge_dk(b):
            if c == 2:
                got('x', b, 0, 2 * two)
                add_rows(b, two, two, rxx, 0)
                dk_send(b, 0).start()
                finish(b, [(rxx, two)])
            if c == 1:
                got('x', b, 0, 2 * two)
                add_rows(b, 0, two, rxx, 0)
                dk_send(b, 0).start()
                finish(b, [(rxx, two)])
            if c == 0:
                got('x', b, 0, two)
                got('y', b, 0, two)
                finish(b, [(rxx, 0), (rxy, 0)])

        def merge_dv(b):
            if c == 3:
                got('y', b, 0, two)
                add_rows(b, 0, two, rxy, 0)
                dv_send(b, 1).start()
            if c == 2:
                got('y', b, 0, two)
                finish(b, [(rxy, 0)])
            if c == 0:
                got('x', b, 0, 2 * two)
                fwd_copy(b).start()
                got('y', b, 0, two)
                finish(b, [(rxx, 0), (rxy, 0)])
            if c == 1:
                got('x', b, two, two)
                got('y', b, 0, two)
                finish(b, [(rxx, two), (rxy, 0)])

        lag_dk = {3: None, 2: 3, 1: 5, 0: 7}[c]
        lag_dv = {3: 3, 2: 3, 1: 7, 0: 5}[c]
        n_step = n_seq + 7

        def when_seq(b, fn):
            pl.when((b >= 0) & (b < n_seq))(lambda: fn(b))

        def step(t, carry):
            @pl.when(t < n_seq)
            def _():
                when_seq(t + PUSH, push)
                when_seq(t + TAKE, take)

                @pl.when(t + 1 < n_seq)
                def _():
                    q_copy(t + 1).start()
                    g_copy(t + 1).start()

                @pl.when(t >= 2)
                def _():
                    o_copy(t - 2).wait()
                    dq_copy(t - 2).wait()
                    oth_copy(t - 2).wait_send()

                @pl.when((t >= NACC) & (core == 0))
                def _():
                    for i in range(len(dk_sends)):
                        dk_send(t - NACC, i).wait_send()

                @pl.when((t >= NACC) & (core == 1))
                def _():
                    for i in range(len(dv_sends)):
                        dv_send(t - NACC, i).wait_send()

                arrived(t)
                q_copy(t).wait()
                g_copy(t).wait()
                compute(t)
                o_copy(t).start()
                dq_copy(t).start()
                oth_copy(t).start()

            when_seq(t - 1, merge_partner)

            if lag_dk is not None:
                @pl.when(core == 0)
                def _():
                    when_seq(t - lag_dk, merge_dk)

            @pl.when(core == 1)
            def _():
                when_seq(t - lag_dv, merge_dv)
            return carry

        lax.fori_loop(0, n_step, step, 0)

        for b in (n_seq - 2, n_seq - 1):
            o_copy(b).wait()
            dq_copy(b).wait()
            oth_copy(b).wait_send()
        for b in range(n_seq - NACC, n_seq):
            @pl.when(core == 0)
            def _():
                for i in range(len(dk_sends)):
                    dk_send(b, i).wait_send()

            @pl.when(core == 1)
            def _():
                for i in range(len(dv_sends)):
                    dv_send(b, i).wait_send()
        whole = kv.at[:, :, pl.ds(0, piece), :]
        for i in range(len(flows)):
            local_wait(whole, kv_tx.at[i])
        for src in range(c + 1):
            local_wait(whole, kvp_tx.at[src])
        for to in doc_dests:
            doc_copy(to).wait_send()
        if c == 0:
            @pl.when(core == 1)
            def _():
                local_wait(rxx.at[:, pl.ds(0, two), :], fwd_tx)
        local_wait(fin_tx, fint_sem)
        local_wait(fin_rx, finr_sem)

    for c in range(n_chip):
        pl.when(chip == c)(functools.partial(run_chip, c))

    @pl.when(core == 0)
    def _():
        a = pltpu.make_async_copy(fin, dk_ref, load_sem.at[0])
        b = pltpu.make_async_copy(fin_rx, dv_ref, load_sem.at[1])
        a.start()
        b.start()
        a.wait()
        b.wait()

    @pl.when(core == 1)
    def _():
        a = pltpu.make_async_copy(fin, dv_ref, load_sem.at[0])
        b = pltpu.make_async_copy(fin_rx, dk_ref, load_sem.at[1])
        a.start()
        b.start()
        a.wait()
        b.wait()


def solution(mesh):
    n_dev = mesh.shape['cp']
    seq_spec = P('dp', 'cp', None, None)

    def per_device(query, keys, values, grad_out, doc_id):
        n_seq, piece, n_heads, head_dim = query.shape
        n_rows = piece * n_heads
        n_key = piece * n_dev
        two = 2 * piece
        rows_shape = (n_seq, n_rows, head_dim)
        kv_shape = (n_seq, piece, head_dim)
        bf16, f32, i32 = jnp.bfloat16, jnp.float32, jnp.int32
        dma = pltpu.SemaphoreType.DMA
        any_spec = pl.BlockSpec(memory_space=pl.ANY)
        n_chip = n_dev // 2
        out = pl.pallas_call(
            functools.partial(attention_kernel, n_dev, n_heads),
            name='attention',
            out_shape=[jax.ShapeDtypeStruct(rows_shape, bf16)] * 2 + [jax.ShapeDtypeStruct(kv_shape, bf16)] * 2,
            in_specs=[any_spec] * 5,
            out_specs=[any_spec] * 4,
            scratch_shapes=[
                pltpu.VMEM((n_seq, 2, n_key, head_dim), bf16),
                pltpu.VMEM((n_seq, 2 * two, head_dim), f32),
                pltpu.VMEM((n_seq, two, head_dim), f32),
                pltpu.VMEM((NACC, n_key, head_dim), f32),
                pltpu.VMEM((2, n_key, head_dim), f32),
                pltpu.VMEM((NPRX, n_key, head_dim), f32),
                pltpu.VMEM((2, n_rows, head_dim), bf16),
                pltpu.VMEM((2, n_rows, head_dim), bf16),
                pltpu.VMEM((2, n_rows, head_dim), bf16),
                pltpu.VMEM((2, n_rows, head_dim), bf16),
                pltpu.VMEM((n_rows, n_key), bf16),
                pltpu.VMEM((n_rows, n_key), bf16),
                pltpu.VMEM(kv_shape, bf16),
                pltpu.VMEM(kv_shape, bf16),
                pltpu.VMEM(kv_shape, bf16),
                pltpu.VMEM((n_dev, n_seq, piece), i32),
                pltpu.VMEM((n_seq, 1, n_key), i32),
                pltpu.VMEM((n_seq, 1, piece), i32),
                pltpu.VMEM((piece, n_key), f32),
                dma((3,)), dma, dma,
                dma((2,)), dma((n_chip, n_seq)), dma((n_chip,)), dma((n_chip, n_seq)),
                dma((2,)), dma((2,)), dma((2,)), dma((2,)),
                dma((2,)), dma((NPRX,)), dma((n_seq,)), dma((n_seq,)), dma((2, NACC)), dma, dma, dma,
            ],
            compiler_params=pltpu.CompilerParams(collective_id=0, has_side_effects=True, vmem_limit_bytes=63 * 1024 * 1024),
        )(query.reshape(rows_shape), grad_out.reshape(rows_shape), keys.reshape(kv_shape), values.reshape(kv_shape), doc_id)
        attn_out, grad_query, grad_keys, grad_values = out
        return (attn_out.reshape(query.shape), grad_query.reshape(query.shape),
                grad_keys.reshape(keys.shape), grad_values.reshape(values.shape))

    return jax.shard_map(per_device, mesh=mesh, in_specs=(seq_spec,) * 4 + (P('dp', 'cp'),), out_specs=(seq_spec,) * 4, check_vma=False)
```

time: 1750 us -> 236 us (0.13); the launches traced: 1720 us -> 236 us
  matrix products: 1040 us -> 0 us
  waiting for transfers between devices: 332 us -> 0 us
  Pallas kernels: 0 us -> 210 us
  other arithmetic: 175 us -> 0 us
  starting transfers between devices: 76.2 us -> 0 us
  local copies, waits for them, and re-layouts: 101 us -> 25.1 us
    dot_general x55 -> x0, matrix products: 1040 us -> none  [the longest x15 269 us: masked_scores(): jnp.einsum('crie,cle->cril', query, key_cur, preferred_element_type=jnp.f...]
    ppermute x72 -> x0, waiting for transfers between devices: 332 us -> none  [the longest x7 149 us: out_body(): doc_cur = lax.ppermute(doc_cur, 'cp', to_next)]
    pallas_call x0 -> x1, Pallas kernels: none -> 210 us  [per_device(): pl.pallas_call(functools.partial(attention_kernel, n_dev, n_heads), name=...]
    reduce_sum x8 -> x0, other arithmetic: 111 us -> none  [stats_update(): jnp.sum(exp_scores, axis=-1)]
    ppermute x72 -> x0, starting transfers between devices: 76.2 us -> none  [the longest x7 17.7 us: stats_body(): key_cur = lax.ppermute(key_cur, 'cp', to_next)]
    while x119 -> x0, local copies, waits for them, and re-layouts: 51.6 us -> none
    unnamed x35 -> x10, local copies, waits for them, and re-layouts: 49.8 us -> 25.1 us
    dot_general x1 -> x0, other arithmetic: 22 us -> none  [per_device(): jnp.einsum('bqhd,bqhd->bqh', grad_out, attn_out, preferred_element_type=j...]
  transfers between devices with their start and end apart: 72 -> 0, of which waited for: 22 -> 0; matrix products, arithmetic and copies ran while one was open for 36% -> 0% of each run, Pallas kernels for 0% -> 0%
where the time goes in v1:
time: 236 us
  Pallas kernels  210 us (89%)
  local copies, waits for them, and re-layouts  25.1 us (11%)
    pallas_call x1, Pallas kernels, per_device(): pl.pallas_call(functools.partial(attention_kernel, n_dev, n_heads), name=...  210 us
    unnamed x10, local copies, waits for them, and re-layouts  25.1 us

profile of v1, /device:TPU:113, one launch (start us, length us, event | category | flops | bytes accessed | tf_op | source)
XLA Modules:
  0.0 236.0 jit_solution(376037721658433676)
XLA Ops:
  0.6 210.3 %attention.1 = (bf16[32,1024,256]{2,1,0:T(8,128)(2,1)}, bf16[32,1024,256]{2,1,0:T(8,128)(2,1)}, bf16[32,64,256]{2,1,0:T(8,128)(2,1)}, bf16[32,64,256]{2,1,0:T(8,128)(2,1)}) custom-call(bf16[32,1024,256]{2,1,0:T(8,128)(2,1)} %bitcast.12, bf16[32,1024,256]{2,1,0:T(8,128)(2,1)} %bitcast.13, bf16[32,64,256]{2,1,0:T(8,128)(2,1)} %bitcast.16, ...), custom_call_target="tpu_custom_call" | custom-call | tf_op jit(solution)/shard_map/attention/pallas_call | solution.py:412
  210.9 0.0 copy-start
  210.9 14.6 %copy.15 = bf16[32,64,16,256]{3,2,1,0:T(8,128)(2,1)} copy(bf16[32,64,16,256]{3,2,1,0:T(8,128)(2,1)} %bitcast.15) | data formatting | bytes 33554432
  225.5 2.3 copy-done
  227.8 0.0 copy-start.2
  227.8 0.0 copy-start.1
  227.8 6.3 %copy.16 = bf16[32,64,16,256]{3,2,1,0:T(8,128)(2,1)} copy(bf16[32,64,16,256]{3,2,1,0:T(8,128)(2,1)S(1)} %bitcast.14) | data formatting | bytes 33554432
  234.1 0.0 copy-done.2
  234.1 1.0 copy.17
  235.0 0.0 copy-done.1
  235.0 1.0 copy.18
Async XLA Ops:
  210.9 16.9 %copy-start = (bf16[32,1024,256]{2,1,0:T(8,128)(2,1)S(1)}, bf16[32,1024,256]{2,1,0:T(8,128)(2,1)}, u32[]{:S(2)}) copy-start(bf16[32,1024,256]{2,1,0:T(8,128)(2,1)} %get-tuple-element.9) | copy-start | bytes 50331652
  227.8 6.3 %copy-start.2 = (bf16[32,64,256]{2,1,0:T(8,128)(2,1)S(1)}, bf16[32,64,256]{2,1,0:T(8,128)(2,1)}, u32[]{:S(2)}) copy-start(bf16[32,64,256]{2,1,0:T(8,128)(2,1)} %get-tuple-element.10) | copy-start | bytes 3145732
  227.8 7.3 %copy-start.1 = (bf16[32,64,256]{2,1,0:T(8,128)(2,1)S(1)}, bf16[32,64,256]{2,1,0:T(8,128)(2,1)}, u32[]{:S(2)}) copy-start(bf16[32,64,256]{2,1,0:T(8,128)(2,1)} %get-tuple-element.11) | copy-start | bytes 3145732

commit v2 on v1

--- a/solution.py
+++ b/solution.py
@@ -10,14 +10,17 @@
 MESH = pl.DeviceIdType.MESH
 LOG2E = 1.4426950408889634
 HIDDEN = -3.0e38
-NACC = 8
+NACC = 12
 NPRX = 4
-PUSH = 4
-TAKE = 2
+PUSH = {0: 12, 1: 10, 2: 8, 3: 4}
+TAKE = {0: 9, 1: 8, 2: 6, 3: 2}
+LAG_DK = {3: None, 2: 4, 1: 6, 0: 8}
+LAG_DV = {3: 4, 2: 4, 1: 9, 0: 6}
+LAG_MAX = 9
 N_ROWCHUNK = 4
 
-OWN_TO = {0: (1, 3), 1: (2,), 2: (3,), 3: ()}
-PASS_TO = {(1, 0): (2,), (2, 1): (3,)}
+HOPS = ((0, 0, 1, None), (0, 0, 3, None), (1, 0, 2, None), (1, 1, 2, None), (1, 1, 0, 1), (0, 1, 3, 1),
+        (2, 1, 3, 0), (2, 2, 3, None))
 
 
 def attention_kernel(n_dev, n_heads, *refs):
@@ -95,37 +98,56 @@
             rows = pl.ds(pl.multiple_of((src * 2 + src_core) * piece, piece), piece)
             return kv.at[b, :, rows, :]
 
-        flows = [(c, to) for to in OWN_TO[c]]
-        for src in range(c):
-            flows += [(src, to) for to in PASS_TO.get((c, src), ())]
-
-        def kv_copy(src, to, b):
+        flows = [hop[1:] for hop in HOPS if hop[0] == c]
+        through = [src for src, _, _ in flows if src > c]
+
+        def by_core(who, fn):
+            if who is None:
+                fn()
+            else:
+                pl.when(core == who)(fn)
+
+        def kv_copy(i, b):
+            src, to, _ = flows[i]
             blk = kv_block(src, core, b)
-            return remote(blk, blk, kv_tx.at[flows.index((src, to))], kv_rx.at[src, b], dev(to))
+            return remote(blk, blk, kv_tx.at[i], kv_rx.at[src, b], dev(to))
+
+        def send_on(src, b):
+            for i, (s, _, who) in enumerate(flows):
+                if s == src:
+                    by_core(who, lambda: kv_copy(i, b).start())
 
         def kvp_copy(src, b):
             blk = kv_block(src, core, b)
             return remote(blk, blk, kvp_tx.at[src], kvp_rx.at[src, b], {'cp': partner})
 
         def push(b):
-            for to in OWN_TO[c]:
-                kv_copy(c, to, b).start()
+            send_on(c, b)
             kvp_copy(c, b).start()
 
         def take(b):
             for src in range(c):
                 local_wait(kv_block(src, core, b), kv_rx.at[src, b])
-                for to in PASS_TO.get((c, src), ()):
-                    kv_copy(src, to, b).start()
+                send_on(src, b)
                 kvp_copy(src, b).start()
+            for src in through:
+                who = [w for s, _, w in flows if s == src][0]
+
+                def pass_on():
+                    local_wait(kv_block(src, core, b), kv_rx.at[src, b])
+                    for i, (s, _, _) in enumerate(flows):
+                        if s == src:
+                            kv_copy(i, b).start()
+
+                by_core(who, pass_on)
 
         def arrived(b):
             for src in range(c + 1):
                 local_wait(kv_block(src, 1 - core, b), kvp_rx.at[src, b])
 
-        for b in range(PUSH):
+        for b in range(PUSH[c]):
             push(b)
-        for b in range(TAKE):
+        for b in range(TAKE[c]):
             take(b)
 
         n_doc = 2 * c + 1
@@ -288,9 +310,8 @@
                 got('y', b, 0, two)
                 finish(b, [(rxx, two), (rxy, 0)])
 
-        lag_dk = {3: None, 2: 3, 1: 5, 0: 7}[c]
-        lag_dv = {3: 3, 2: 3, 1: 7, 0: 5}[c]
-        n_step = n_seq + 7
+        lag_dk, lag_dv = LAG_DK[c], LAG_DV[c]
+        n_step = n_seq + LAG_MAX
 
         def when_seq(b, fn):
             pl.when((b >= 0) & (b < n_seq))(lambda: fn(b))
@@ -298,8 +319,8 @@
         def step(t, carry):
             @pl.when(t < n_seq)
             def _():
-                when_seq(t + PUSH, push)
-                when_seq(t + TAKE, take)
+                when_seq(t + PUSH[c], push)
+                when_seq(t + TAKE[c], take)
 
                 @pl.when(t + 1 < n_seq)
                 def _():
@@ -359,8 +380,8 @@
                 for i in range(len(dv_sends)):
                     dv_send(b, i).wait_send()
         whole = kv.at[:, :, pl.ds(0, piece), :]
-        for i in range(len(flows)):
-            local_wait(whole, kv_tx.at[i])
+        for i, (_, _, who) in enumerate(flows):
+            by_core(who, lambda: local_wait(whole, kv_tx.at[i]))
         for src in range(c + 1):
             local_wait(whole, kvp_tx.at[src])
         for to in doc_dests:
@@ -436,7 +457,7 @@
                 pltpu.VMEM((n_seq, 1, piece), i32),
                 pltpu.VMEM((piece, n_key), f32),
                 dma((3,)), dma, dma,
-                dma((2,)), dma((n_chip, n_seq)), dma((n_chip,)), dma((n_chip, n_seq)),
+                dma((4,)), dma((n_chip, n_seq)), dma((n_chip,)), dma((n_chip, n_seq)),
                 dma((2,)), dma((2,)), dma((2,)), dma((2,)),
                 dma((2,)), dma((NPRX,)), dma((n_seq,)), dma((n_seq,)), dma((2, NACC)), dma, dma, dma,
             ],

time: 236 us -> 219 us (0.928)
  Pallas kernels: 210 us -> 193 us
    pallas_call x1, Pallas kernels: 210 us -> 193 us  [per_device(): pl.pallas_call(functools.partial(attention_kernel, n_dev, n_heads), name=...]
where the time goes in v2:
time: 219 us; the launch traced here: 218 us
  Pallas kernels  193 us (88%)
  local copies, waits for them, and re-layouts  25.1 us (11%)
    pallas_call x1, Pallas kernels, per_device(): pl.pallas_call(functools.partial(attention_kernel, n_dev, n_heads), name=...  193 us
    unnamed x10, local copies, waits for them, and re-layouts  25.1 us

profile of v2, /device:TPU:113, one launch (start us, length us, event | category | flops | bytes accessed | tf_op | source)
XLA Modules:
  0.0 218.4 jit_solution(969587962706952622)
XLA Ops:
  0.6 192.7 %attention.1 = (bf16[32,1024,256]{2,1,0:T(8,128)(2,1)}, bf16[32,1024,256]{2,1,0:T(8,128)(2,1)}, bf16[32,64,256]{2,1,0:T(8,128)(2,1)}, bf16[32,64,256]{2,1,0:T(8,128)(2,1)}) custom-call(bf16[32,1024,256]{2,1,0:T(8,128)(2,1)} %bitcast.12, bf16[32,1024,256]{2,1,0:T(8,128)(2,1)} %bitcast.13, bf16[32,64,256]{2,1,0:T(8,128)(2,1)} %bitcast.16, ...), custom_call_target="tpu_custom_call" | custom-call | tf_op jit(solution)/shard_map/attention/pallas_call | solution.py:433
  193.3 0.0 copy-start
  193.3 14.6 %copy.15 = bf16[32,64,16,256]{3,2,1,0:T(8,128)(2,1)} copy(bf16[32,64,16,256]{3,2,1,0:T(8,128)(2,1)} %bitcast.15) | data formatting | bytes 33554432
  207.9 2.3 %copy-done = bf16[32,1024,256]{2,1,0:T(8,128)(2,1)S(1)} copy-done((bf16[32,1024,256]{2,1,0:T(8,128)(2,1)S(1)}, bf16[32,1024,256]{2,1,0:T(8,128)(2,1)}, u32[]{:S(2)}) %copy-start) | copy-done | bytes 16777240
  210.2 0.0 copy-start.2
  210.2 0.0 copy-start.1
  210.2 6.3 %copy.16 = bf16[32,64,16,256]{3,2,1,0:T(8,128)(2,1)} copy(bf16[32,64,16,256]{3,2,1,0:T(8,128)(2,1)S(1)} %bitcast.14) | data formatting | bytes 33554432
  216.5 0.0 copy-done.2
  216.5 1.0 copy.17
  217.5 0.0 copy-done.1
  217.5 1.0 copy.18
Async XLA Ops:
  193.3 16.9 %copy-start = (bf16[32,1024,256]{2,1,0:T(8,128)(2,1)S(1)}, bf16[32,1024,256]{2,1,0:T(8,128)(2,1)}, u32[]{:S(2)}) copy-start(bf16[32,1024,256]{2,1,0:T(8,128)(2,1)} %get-tuple-element.9) | copy-start | bytes 50331652
  210.2 6.3 %copy-start.2 = (bf16[32,64,256]{2,1,0:T(8,128)(2,1)S(1)}, bf16[32,64,256]{2,1,0:T(8,128)(2,1)}, u32[]{:S(2)}) copy-start(bf16[32,64,256]{2,1,0:T(8,128)(2,1)} %get-tuple-element.10) | copy-start | bytes 3145732
  210.2 7.3 %copy-start.1 = (bf16[32,64,256]{2,1,0:T(8,128)(2,1)S(1)}, bf16[32,64,256]{2,1,0:T(8,128)(2,1)}, u32[]{:S(2)}) copy-start(bf16[32,64,256]{2,1,0:T(8,128)(2,1)} %get-tuple-element.11) | copy-start | bytes 3145732

commit v3 on v2

v3 whole, which is shorter than its diff:
```python
import functools

import jax
import jax.numpy as jnp
from jax import lax
from jax.experimental import pallas as pl
from jax.experimental.pallas import tpu as pltpu
from jax.sharding import PartitionSpec as P

MESH = pl.DeviceIdType.MESH
LOG2E = 1.4426950408889634
HIDDEN = -3.0e38
NACC = 12
NPRX = 4
N_ROWCHUNK = 4


HOPS = ((1, 1, 2, None), (1, 1, 0, 1), (2, 1, 3, 0), (0, 1, 3, 1), (1, 0, 2, None), (2, 2, 3, None), (0, 0, 1, None),
        (0, 0, 3, None))
PUSH = {0: (1, 7), 1: (3, 9), 2: (3, 2), 3: (2, 5)}
TAKE = {0: (0, 8), 1: (4, 4), 2: (2, 2), 3: (0, 1)}
SENDS = {(3, 0): ((1, 2, 0, False), (0, 0, 1, False), (2, 2, 1, False)),
         (3, 1): ((2, 2, 0, False), (0, 0, 0, True), (1, 0, 2, False)),
         (2, 0): ((0, 1, 0, False), (1, 1, 1, True)),
         (2, 1): ((0, 3, 0, False), (1, 1, 0, False)),
         (1, 0): ((0, 0, 0, True),),
         (1, 1): ((0, 0, 1, False),)}
RELAY = {(3, 1): (2, 0), (2, 0): (2, 0), (1, 0): (3, 0), (0, 1): (4, 2)}
FINISH = {(3, 0): (1, ()), (3, 1): (1, ()), (2, 0): (5, (1,)), (2, 1): (5, (0,)), (1, 0): (8, (1,)), (1, 1): (6, (0, 1)),
          (0, 0): (8, (0, 1)), (0, 1): (8, (0, 1))}
LAG_MAX = 8


def row_plan(n):
    out = [('A', 0), ('A', 1)]
    for i in range(n + 2):
        if i + 2 < n:
            out.append(('A', i + 2))
        if i < n:
            out.append(('B', i))
        if 0 <= i - 1 < n:
            out.append(('D', i - 1))
            out.append(('E', i - 1))
        if i < n:
            out.append(('C', i))
        if i == n - 1:
            out.append(('V', 0))
    return out


def attention_kernel(n_dev, n_heads, *refs):
    (q_ref, g_ref, k_ref, v_ref, doc_ref, o_ref, dq_ref, dk_ref, dv_ref,
     kv, rx0, rx1, rx2, acc, part, prx, qb, gb, ob, dqb, pb, dsb, fin_k, fin_v, docs, kdoc, odoc, vis,
     load_sem, doc_tx, doc_rx, kv_tx, kv_rx, kvp_tx, kvp_rx, q_sem, g_sem, o_sem, dq_sem,
     part_tx, prx_sem, rx_sem, tx_sem, fwd_tx) = refs
    rx = (rx0, rx1, rx2)
    n_seq, n_rows, head_dim = q_ref.shape
    piece = k_ref.shape[1]
    two = 2 * piece
    n_chip = n_dev // 2
    scale = head_dim ** -0.5
    me = lax.axis_index('cp')
    chip = me // 2
    core = me % 2
    partner = chip * 2 + (1 - core)
    my_rows = pl.ds(pl.multiple_of(me * piece, piece), piece)

    def dev(c):
        return {'cp': c * 2 + core}

    def remote(src, dst, tx, rx, to):
        return pltpu.make_async_remote_copy(src_ref=src, dst_ref=dst, send_sem=tx, recv_sem=rx,
                                            device_id=to, device_id_type=MESH)

    def local_wait(ref, sem):
        pltpu.make_async_copy(ref, ref, sem).wait()

    barrier = pltpu.get_barrier_semaphore()
    for hop in range(1, n_dev):
        pl.semaphore_signal(barrier, inc=1, device_id={'cp': (me + hop) % n_dev}, device_id_type=MESH)

    own_k = pltpu.make_async_copy(k_ref, kv.at[:, 0, my_rows, :], load_sem.at[0])
    own_v = pltpu.make_async_copy(v_ref, kv.at[:, 1, my_rows, :], load_sem.at[1])
    own_d = pltpu.make_async_copy(doc_ref, docs.at[me], load_sem.at[2])
    own_k.start()
    own_v.start()
    own_d.start()

    def q_copy(b):
        return pltpu.make_async_copy(q_ref.at[b], qb.at[b % 2], q_sem.at[b % 2])

    def g_copy(b):
        return pltpu.make_async_copy(g_ref.at[b], gb.at[b % 2], g_sem.at[b % 2])

    def o_copy(b):
        return pltpu.make_async_copy(ob.at[b % 2], o_ref.at[b], o_sem.at[b % 2])

    def dq_copy(b):
        return pltpu.make_async_copy(dqb.at[b % 2], dq_ref.at[b], dq_sem.at[b % 2])

    q_copy(0).start()
    g_copy(0).start()
    own_k.wait()
    own_v.wait()
    own_d.wait()
    odoc[...] = docs[me].reshape(n_seq, 1, piece)
    pl.semaphore_wait(barrier, n_dev - 1)

    def run_chip(c):
        n_key = two * (c + 1)
        here = pl.ds(0, c + 1)

        def doc_copy(to):
            return remote(docs.at[me], docs.at[me], doc_tx, doc_rx, to)

        doc_dests = [{'cp': partner}] + [{'cp': d} for d in range(two // piece * (c + 1), n_dev)]
        for to in doc_dests:
            doc_copy(to).start()

        def kv_block(src, src_core, b):
            rows = pl.ds(pl.multiple_of((src * 2 + src_core) * piece, piece), piece)
            return kv.at[b, :, rows, :]

        flows = [hop[1:] for hop in HOPS if hop[0] == c]
        through = [src for src, _, _ in flows if src > c]

        def by_core(who, fn):
            if who is None:
                fn()
            else:
                pl.when(core == who)(fn)

        def kv_copy(i, b):
            src, to, _ = flows[i]
            blk = kv_block(src, core, b)
            return remote(blk, blk, kv_tx.at[i], kv_rx.at[src, b], dev(to))

        def send_on(src, b):
            for i, (s, _, who) in enumerate(flows):
                if s == src:
                    by_core(who, lambda: kv_copy(i, b).start())

        def kvp_copy(src, b):
            blk = kv_block(src, core, b)
            return remote(blk, blk, kvp_tx.at[src], kvp_rx.at[src, b], {'cp': partner})

        def push(b):
            send_on(c, b)
            kvp_copy(c, b).start()

        def take(b):
            for src in range(c - 1, -1, -1):
                local_wait(kv_block(src, core, b), kv_rx.at[src, b])
                send_on(src, b)
                kvp_copy(src, b).start()
            for src in through:
                who = [w for s, _, w in flows if s == src][0]

                def pass_on():
                    local_wait(kv_block(src, core, b), kv_rx.at[src, b])
                    for i, (s, _, _) in enumerate(flows):
                        if s == src:
                            kv_copy(i, b).start()

                by_core(who, pass_on)

        def ramp(lead, fn):
            first, most = lead
            start = min(first, most)

            def at_step(t):
                b = jnp.minimum(start + 2 * t, t + most)
                pl.when(b < n_seq)(lambda: fn(b))
                if most - start > 0:
                    pl.when(t < most - start)(lambda: fn(b + 1))

            return start, at_step

        def arrived(b):
            for src in range(c + 1):
                local_wait(kv_block(src, 1 - core, b), kvp_rx.at[src, b])

        n_push, push_at = ramp(PUSH[c], push)
        n_take, take_at = ramp(TAKE[c], take)
        for b in range(n_push):
            push(b)
        for b in range(n_take):
            take(b)

        n_doc = 2 * c + 1
        pltpu.make_async_copy(docs.at[pl.ds(0, n_doc)], docs.at[pl.ds(0, n_doc)], doc_rx).wait()
        for p in range(2 * c + 2):
            kdoc[:, :, p * piece:(p + 1) * piece] = docs[p].reshape(n_seq, 1, piece)

        def compute(b):
            slot = b % 2
            keys = kv[b, 0, 0:n_key, :]
            vals = kv[b, 1, 0:n_key, :]
            tok = lax.broadcasted_iota(jnp.int32, (piece, piece), 0)
            tok_t = lax.broadcasted_iota(jnp.int32, (piece, piece), 1)
            own_doc = odoc[b]
            q_doc = jnp.sum(jnp.where(tok == tok_t, own_doc, 0), axis=1, keepdims=True)
            key_doc = kdoc[b, :, 0:n_key]
            q_pos = me * piece + lax.broadcasted_iota(jnp.int32, (piece, n_key), 0)
            k_pos = lax.broadcasted_iota(jnp.int32, (piece, n_key), 1)
            seen = (q_doc == key_doc) & (k_pos <= q_pos)
            vis[:, 0:n_key] = jnp.where(seen, 1.0, 0.0)
            rc = n_rows // N_ROWCHUNK
            tc = rc // n_heads
            nt = (((1,), (1,)), ((), ()))
            tn = (((0,), (0,)), ((), ()))
            live = {}

            def span(ch):
                return slice(ch * rc, (ch + 1) * rc)

            def scores(ch):
                live['s', ch] = lax.dot_general(qb[slot, span(ch), :], keys, nt, preferred_element_type=jnp.float32)
                live['dp', ch] = lax.dot_general(gb[slot, span(ch), :], vals, nt, preferred_element_type=jnp.float32)

            def softmax(ch):
                seen_c = vis[ch * tc:(ch + 1) * tc, 0:n_key].reshape(tc, 1, n_key)
                s3 = live.pop(('s', ch)).reshape(tc, n_heads, n_key)
                s = jnp.where(seen_c > 0.5, s3 * (scale * LOG2E), HIDDEN).reshape(rc, n_key)
                e = jnp.exp2(s - jnp.max(s, axis=1, keepdims=True))
                p = e * (1.0 / jnp.sum(e, axis=1, keepdims=True))
                live['p', ch] = p
                pb[span(ch), 0:n_key] = p.astype(jnp.bfloat16)

            def attend(ch):
                o = jnp.dot(pb[span(ch), 0:n_key], vals, preferred_element_type=jnp.float32)
                live['o', ch] = o.astype(jnp.bfloat16)

            def dscores(ch):
                o16 = live.pop(('o', ch))
                ob[slot, span(ch), :] = o16
                gc = gb[slot, span(ch), :].astype(jnp.float32)
                delta = jnp.sum(gc * o16.astype(jnp.float32), axis=1, keepdims=True)
                dsb[span(ch), 0:n_key] = (live.pop(('p', ch)) * (live.pop(('dp', ch)) - delta)).astype(jnp.bfloat16)

            def dquery(ch):
                dq = jnp.dot(dsb[span(ch), 0:n_key], keys, preferred_element_type=jnp.float32)
                dqb[slot, span(ch), :] = (dq * scale).astype(jnp.bfloat16)

            def key_sums():
                live['dv'] = lax.dot_general(pb[:, 0:n_key], gb[slot], tn, preferred_element_type=jnp.float32)

            stages = row_plan(N_ROWCHUNK)
            for name, ch in stages:
                if name == 'A':
                    scores(ch)
                elif name == 'B':
                    softmax(ch)
                elif name == 'C':
                    attend(ch)
                elif name == 'D':
                    dscores(ch)
                elif name == 'E':
                    dquery(ch)
                elif name == 'V':
                    key_sums()
            dv = live['dv']
            dk = lax.dot_general(dsb[:, 0:n_key], qb[slot], tn, preferred_element_type=jnp.float32)

            for a in range(c + 1):
                for p in range(2):
                    rows = slice((2 * a + p) * piece, (2 * a + p + 1) * piece)
                    part[slot, p, a, 0:piece, :] = dk[rows]
                    part[slot, p, a, piece:two, :] = dv[rows]

        def part_copy(b):
            return remote(part.at[b % 2, 1 - core, here], prx.at[b % NPRX, here], part_tx.at[b % 2],
                          prx_sem.at[b % NPRX], {'cp': partner})

        def unit_copy(b, core_, i):
            a, to, buf, _ = SENDS[c, core_][i]
            return remote(acc.at[b % NACC, a], rx[buf].at[b], tx_sem.at[i, b % NACC], rx_sem.at[buf, b], dev(to))

        def got(buf, b):
            local_wait(rx[buf].at[b], rx_sem.at[buf, b])

        def merge_partner(b):
            local_wait(prx.at[b % NPRX, here], prx_sem.at[b % NPRX])
            acc[b % NACC, here] = part[b % 2, core, here] + prx[b % NPRX, here]
            for e in range(2):
                sends = [i for i, s in enumerate(SENDS.get((c, e), ())) if not s[3]]
                if sends:
                    @pl.when(core == e)
                    def _():
                        for i in sends:
                            unit_copy(b, e, i).start()

        def relay(b, e):
            buf = RELAY[c, e][1]
            got(buf, b)
            if c == 0:
                fwd_copy(b).start()
                return
            for i, (a, _, _, after) in enumerate(SENDS[c, e]):
                if after:
                    acc[b % NACC, a] = acc[b % NACC, a] + rx[buf][b]
                    unit_copy(b, e, i).start()

        def fwd_copy(b):
            return remote(rx2.at[b], rx1.at[b], fwd_tx, rx_sem.at[1, b], dev(1))

        def finish(b, e):
            total = acc[b % NACC, c]
            for buf in FINISH[c, e][1]:
                got(buf, b)
                total = total + rx[buf][b]
            fin_k[b] = (total[0:piece] * scale).astype(jnp.bfloat16)
            fin_v[b] = total[piece:two].astype(jnp.bfloat16)

        n_step = n_seq + LAG_MAX

        def when_seq(b, fn):
            pl.when((b >= 0) & (b < n_seq))(lambda: fn(b))

        def sent(b):
            for e in range(2):
                if (c, e) in SENDS:
                    @pl.when(core == e)
                    def _():
                        for i in range(len(SENDS[c, e])):
                            unit_copy(b, e, i).wait_send()

        def step(t, carry):
            @pl.when(t < n_seq)
            def _():
                push_at(t)
                take_at(t)

                @pl.when(t + 1 < n_seq)
                def _():
                    q_copy(t + 1).start()
                    g_copy(t + 1).start()

                @pl.when(t >= 2)
                def _():
                    o_copy(t - 2).wait()
                    dq_copy(t - 2).wait()
                    part_copy(t - 2).wait_send()

                pl.when(t >= NACC)(lambda: sent(t - NACC))
                arrived(t)
                q_copy(t).wait()
                g_copy(t).wait()
                compute(t)
                o_copy(t).start()
                dq_copy(t).start()
                part_copy(t).start()

            when_seq(t - 1, merge_partner)
            for e in range(2):
                @pl.when(core == e)
                def _():
                    if (c, e) in RELAY:
                        when_seq(t - RELAY[c, e][0], lambda b: relay(b, e))
                    when_seq(t - FINISH[c, e][0], lambda b: finish(b, e))
            return carry

        lax.fori_loop(0, n_step, step, 0)

        for b in (n_seq - 2, n_seq - 1):
            o_copy(b).wait()
            dq_copy(b).wait()
            part_copy(b).wait_send()
        for b in range(n_seq - NACC, n_seq):
            sent(b)
        whole = kv.at[:, :, pl.ds(0, piece), :]
        for i, (_, _, who) in enumerate(flows):
            by_core(who, lambda: local_wait(whole, kv_tx.at[i]))
        for src in range(c + 1):
            local_wait(whole, kvp_tx.at[src])
        for to in doc_dests:
            doc_copy(to).wait_send()
        if c == 0:
            pl.when(core == 1)(lambda: local_wait(rx2, fwd_tx))

    for c in range(n_chip):
        pl.when(chip == c)(functools.partial(run_chip, c))

    out_k = pltpu.make_async_copy(fin_k, dk_ref, load_sem.at[0])
    out_v = pltpu.make_async_copy(fin_v, dv_ref, load_sem.at[1])
    out_k.start()
    out_v.start()
    out_k.wait()
    out_v.wait()


def solution(mesh):
    n_dev = mesh.shape['cp']
    seq_spec = P('dp', 'cp', None, None)

    def per_device(query, keys, values, grad_out, doc_id):
        n_seq, piece, n_heads, head_dim = query.shape
        n_rows = piece * n_heads
        n_key = piece * n_dev
        two = 2 * piece
        rows_shape = (n_seq, n_rows, head_dim)
        kv_shape = (n_seq, piece, head_dim)
        bf16, f32, i32 = jnp.bfloat16, jnp.float32, jnp.int32
        dma = pltpu.SemaphoreType.DMA
        any_spec = pl.BlockSpec(memory_space=pl.ANY)
        n_chip = n_dev // 2
        out = pl.pallas_call(
            functools.partial(attention_kernel, n_dev, n_heads),
            name='attention',
            out_shape=[jax.ShapeDtypeStruct(rows_shape, bf16)] * 2 + [jax.ShapeDtypeStruct(kv_shape, bf16)] * 2,
            in_specs=[any_spec] * 5,
            out_specs=[any_spec] * 4,
            scratch_shapes=[
                pltpu.VMEM((n_seq, 2, n_key, head_dim), bf16),
                pltpu.VMEM((n_seq, two, head_dim), f32),
                pltpu.VMEM((n_seq, two, head_dim), f32),
                pltpu.VMEM((n_seq, two, head_dim), f32),
                pltpu.VMEM((NACC, n_chip, two, head_dim), f32),
                pltpu.VMEM((2, 2, n_chip, two, head_dim), f32),
                pltpu.VMEM((NPRX, n_chip, two, head_dim), f32),
                pltpu.VMEM((2, n_rows, head_dim), bf16),
                pltpu.VMEM((2, n_rows, head_dim), bf16),
                pltpu.VMEM((2, n_rows, head_dim), bf16),
                pltpu.VMEM((2, n_rows, head_dim), bf16),
                pltpu.VMEM((n_rows, n_key), bf16),
                pltpu.VMEM((n_rows, n_key), bf16),
                pltpu.VMEM(kv_shape, bf16),
                pltpu.VMEM(kv_shape, bf16),
                pltpu.VMEM((n_dev, n_seq, piece), i32),
                pltpu.VMEM((n_seq, 1, n_key), i32),
                pltpu.VMEM((n_seq, 1, piece), i32),
                pltpu.VMEM((piece, n_key), f32),
                dma((3,)), dma, dma,
                dma((4,)), dma((n_chip, n_seq)), dma((n_chip,)), dma((n_chip, n_seq)),
                dma((2,)), dma((2,)), dma((2,)), dma((2,)),
                dma((2,)), dma((NPRX,)), dma((3, n_seq)), dma((3, NACC)), dma,
            ],
            compiler_params=pltpu.CompilerParams(collective_id=0, has_side_effects=True, vmem_limit_bytes=63 * 1024 * 1024),
        )(query.reshape(rows_shape), grad_out.reshape(rows_shape), keys.reshape(kv_shape), values.reshape(kv_shape), doc_id)
        attn_out, grad_query, grad_keys, grad_values = out
        return (attn_out.reshape(query.shape), grad_query.reshape(query.shape),
                grad_keys.reshape(keys.shape), grad_values.reshape(values.shape))

    return jax.shard_map(per_device, mesh=mesh, in_specs=(seq_spec,) * 4 + (P('dp', 'cp'),), out_specs=(seq_spec,) * 4, check_vma=False)
```

time: 219 us -> 191 us (0.87)
  Pallas kernels: 193 us -> 165 us
    pallas_call x1, Pallas kernels: 193 us -> 165 us  [per_device(): pl.pallas_call(functools.partial(attention_kernel, n_dev, n_heads), name=...]
where the time goes in v3:
time: 191 us; the launch traced here: 190 us
  Pallas kernels  165 us (86%)
  local copies, waits for them, and re-layouts  25.1 us (13%)
    pallas_call x1, Pallas kernels, per_device(): pl.pallas_call(functools.partial(attention_kernel, n_dev, n_heads), name=...  165 us
    unnamed x10, local copies, waits for them, and re-layouts  25.1 us

profile of v3, /device:TPU:113, one launch (start us, length us, event | category | flops | bytes accessed | tf_op | source)
XLA Modules:
  0.0 190.5 jit_solution(14527873516519604796)
XLA Ops:
  0.6 164.7 %attention.1 = (bf16[32,1024,256]{2,1,0:T(8,128)(2,1)}, bf16[32,1024,256]{2,1,0:T(8,128)(2,1)}, bf16[32,64,256]{2,1,0:T(8,128)(2,1)}, bf16[32,64,256]{2,1,0:T(8,128)(2,1)}) custom-call(bf16[32,1024,256]{2,1,0:T(8,128)(2,1)} %bitcast.12, bf16[32,1024,256]{2,1,0:T(8,128)(2,1)} %bitcast.13, bf16[32,64,256]{2,1,0:T(8,128)(2,1)} %bitcast.16, ...), custom_call_target="tpu_custom_call" | custom-call | tf_op jit(solution)/shard_map/attention/pallas_call | solution.py:407
  165.4 0.0 copy-start
  165.4 14.6 %copy.15 = bf16[32,64,16,256]{3,2,1,0:T(8,128)(2,1)} copy(bf16[32,64,16,256]{3,2,1,0:T(8,128)(2,1)} %bitcast.15) | data formatting | bytes 33554432
  180.0 2.3 %copy-done = bf16[32,1024,256]{2,1,0:T(8,128)(2,1)S(1)} copy-done((bf16[32,1024,256]{2,1,0:T(8,128)(2,1)S(1)}, bf16[32,1024,256]{2,1,0:T(8,128)(2,1)}, u32[]{:S(2)}) %copy-start) | copy-done | bytes 16777240
  182.2 0.0 copy-start.2
  182.2 0.0 copy-start.1
  182.2 6.3 %copy.16 = bf16[32,64,16,256]{3,2,1,0:T(8,128)(2,1)} copy(bf16[32,64,16,256]{3,2,1,0:T(8,128)(2,1)S(1)} %bitcast.14) | data formatting | bytes 33554432
  188.5 0.0 copy-done.2
  188.5 1.0 copy.17
  189.5 0.0 copy-done.1
  189.5 1.0 copy.18
Async XLA Ops:
  165.4 16.9 %copy-start = (bf16[32,1024,256]{2,1,0:T(8,128)(2,1)S(1)}, bf16[32,1024,256]{2,1,0:T(8,128)(2,1)}, u32[]{:S(2)}) copy-start(bf16[32,1024,256]{2,1,0:T(8,128)(2,1)} %get-tuple-element.9) | copy-start | bytes 50331652
  182.2 6.3 %copy-start.2 = (bf16[32,64,256]{2,1,0:T(8,128)(2,1)S(1)}, bf16[32,64,256]{2,1,0:T(8,128)(2,1)}, u32[]{:S(2)}) copy-start(bf16[32,64,256]{2,1,0:T(8,128)(2,1)} %get-tuple-element.10) | copy-start | bytes 3145732
  182.2 7.3 %copy-start.1 = (bf16[32,64,256]{2,1,0:T(8,128)(2,1)S(1)}, bf16[32,64,256]{2,1,0:T(8,128)(2,1)}, u32[]{:S(2)}) copy-start(bf16[32,64,256]{2,1,0:T(8,128)(2,1)} %get-tuple-element.11) | copy-start | bytes 3145732

commit v4 on v3

--- a/solution.py
+++ b/solution.py
@@ -13,22 +13,25 @@
 NACC = 12
 NPRX = 4
 N_ROWCHUNK = 4
+N_COPY = 16
+N_LATE = 6
 
 
 HOPS = ((1, 1, 2, None), (1, 1, 0, 1), (2, 1, 3, 0), (0, 1, 3, 1), (1, 0, 2, None), (2, 2, 3, None), (0, 0, 1, None),
         (0, 0, 3, None))
 PUSH = {0: (1, 7), 1: (3, 9), 2: (3, 2), 3: (2, 5)}
 TAKE = {0: (0, 8), 1: (4, 4), 2: (2, 2), 3: (0, 1)}
-SENDS = {(3, 0): ((1, 2, 0, False), (0, 0, 1, False), (2, 2, 1, False)),
-         (3, 1): ((2, 2, 0, False), (0, 0, 0, True), (1, 0, 2, False)),
-         (2, 0): ((0, 1, 0, False), (1, 1, 1, True)),
-         (2, 1): ((0, 3, 0, False), (1, 1, 0, False)),
-         (1, 0): ((0, 0, 0, True),),
-         (1, 1): ((0, 0, 1, False),)}
+SENDS = {(3, 0): ((1, 2, 0, False, None), (0, 0, 1, False, 1), (2, 2, 1, False, 0)),
+         (3, 1): ((2, 2, 0, False, 0), (0, 0, 0, True, 1), (1, 0, 2, False, None)),
+         (2, 0): ((0, 1, 0, False, None), (1, 1, 1, True, 0)),
+         (2, 1): ((0, 3, 0, False, None), (1, 1, 0, False, 0)),
+         (1, 0): ((0, 0, 0, True, 0),),
+         (1, 1): ((0, 0, 1, False, 0),)}
 RELAY = {(3, 1): (2, 0), (2, 0): (2, 0), (1, 0): (3, 0), (0, 1): (4, 2)}
 FINISH = {(3, 0): (1, ()), (3, 1): (1, ()), (2, 0): (5, (1,)), (2, 1): (5, (0,)), (1, 0): (8, (1,)), (1, 1): (6, (0, 1)),
           (0, 0): (8, (0, 1)), (0, 1): (8, (0, 1))}
 LAG_MAX = 8
+FINISH_LATE = {(1, 1): (1,)}
 
 
 def row_plan(n):
@@ -49,10 +52,10 @@
 
 
 def attention_kernel(n_dev, n_heads, *refs):
-    (q_ref, g_ref, k_ref, v_ref, doc_ref, o_ref, dq_ref, dk_ref, dv_ref,
-     kv, rx0, rx1, rx2, acc, part, prx, qb, gb, ob, dqb, pb, dsb, fin_k, fin_v, docs, kdoc, odoc, vis,
+    (q_ref, g_ref, k_ref, v_ref, doc_ref, o_ref, dq_ref, dk_ref, dv_ref, near_ref, far_ref, own_ref,
+     kv, rx0, rx1, rx2, acc, part, prx, qb, gb, ob, dqb, pb, dsb, fin_k, fin_v, own, docs, kdoc, odoc, vis,
      load_sem, doc_tx, doc_rx, kv_tx, kv_rx, kvp_tx, kvp_rx, q_sem, g_sem, o_sem, dq_sem,
-     part_tx, prx_sem, rx_sem, tx_sem, fwd_tx) = refs
+     part_tx, prx_sem, rx_sem, tx_sem, fwd_tx, late_sem) = refs
     rx = (rx0, rx1, rx2)
     n_seq, n_rows, head_dim = q_ref.shape
     piece = k_ref.shape[1]
@@ -109,6 +112,7 @@
     def run_chip(c):
         n_key = two * (c + 1)
         here = pl.ds(0, c + 1)
+        first_late = n_seq - N_LATE
 
         def doc_copy(to):
             return remote(docs.at[me], docs.at[me], doc_tx, doc_rx, to)
@@ -272,9 +276,22 @@
             return remote(part.at[b % 2, 1 - core, here], prx.at[b % NPRX, here], part_tx.at[b % 2],
                           prx_sem.at[b % NPRX], {'cp': partner})
 
-        def unit_copy(b, core_, i):
-            a, to, buf, _ = SENDS[c, core_][i]
-            return remote(acc.at[b % NACC, a], rx[buf].at[b], tx_sem.at[i, b % NACC], rx_sem.at[buf, b], dev(to))
+        def unit_send(b, e, i):
+            a, to, buf, _, late = SENDS[c, e][i]
+            unit = acc.at[b % NACC, a]
+            sem = tx_sem.at[i, b % NACC]
+
+            def now():
+                remote(unit, rx[buf].at[b], sem, rx_sem.at[buf, b], dev(to)).start()
+
+            if late is None:
+                now()
+            else:
+                pl.when(b < first_late)(now)
+
+                @pl.when(b >= first_late)
+                def _():
+                    pltpu.make_async_copy(unit, (near_ref, far_ref)[late].at[b - first_late], sem).start()
 
         def got(buf, b):
             local_wait(rx[buf].at[b], rx_sem.at[buf, b])
@@ -288,7 +305,7 @@
                     @pl.when(core == e)
                     def _():
                         for i in sends:
-                            unit_copy(b, e, i).start()
+                            unit_send(b, e, i)
 
         def relay(b, e):
             buf = RELAY[c, e][1]
@@ -296,21 +313,31 @@
             if c == 0:
                 fwd_copy(b).start()
                 return
-            for i, (a, _, _, after) in enumerate(SENDS[c, e]):
+            for i, (a, _, _, after, _) in enumerate(SENDS[c, e]):
                 if after:
                     acc[b % NACC, a] = acc[b % NACC, a] + rx[buf][b]
-                    unit_copy(b, e, i).start()
+                    unit_send(b, e, i)
 
         def fwd_copy(b):
             return remote(rx2.at[b], rx1.at[b], fwd_tx, rx_sem.at[1, b], dev(1))
 
         def finish(b, e):
-            total = acc[b % NACC, c]
-            for buf in FINISH[c, e][1]:
-                got(buf, b)
-                total = total + rx[buf][b]
-            fin_k[b] = (total[0:piece] * scale).astype(jnp.bfloat16)
-            fin_v[b] = total[piece:two].astype(jnp.bfloat16)
+            def total(bufs):
+                out = acc[b % NACC, c]
+                for buf in bufs:
+                    got(buf, b)
+                    out = out + rx[buf][b]
+                return out
+
+            @pl.when(b < first_late)
+            def _():
+                out = total(FINISH[c, e][1])
+                fin_k[b] = (out[0:piece] * scale).astype(jnp.bfloat16)
+                fin_v[b] = out[piece:two].astype(jnp.bfloat16)
+
+            @pl.when(b >= first_late)
+            def _():
+                own[b - first_late] = total(FINISH_LATE.get((c, e), ()))
 
         n_step = n_seq + LAG_MAX
 
@@ -323,7 +350,7 @@
                     @pl.when(core == e)
                     def _():
                         for i in range(len(SENDS[c, e])):
-                            unit_copy(b, e, i).wait_send()
+                            local_wait(acc.at[b % NACC, SENDS[c, e][i][0]], tx_sem.at[i, b % NACC])
 
         def step(t, carry):
             @pl.when(t < n_seq)
@@ -383,10 +410,47 @@
 
     out_k = pltpu.make_async_copy(fin_k, dk_ref, load_sem.at[0])
     out_v = pltpu.make_async_copy(fin_v, dv_ref, load_sem.at[1])
+    out_own = pltpu.make_async_copy(own, own_ref, late_sem)
     out_k.start()
     out_v.start()
+    out_own.start()
     out_k.wait()
     out_v.wait()
+    out_own.wait()
+
+
+def copy_kernel(a_ref, b_ref, a_out, b_out, buf, in_sem, out_sem):
+    n_seq = a_ref.shape[0]
+    n_buf = buf.shape[0]
+    ahead = n_buf // 2
+
+    def pick(i, fn):
+        fn(a_ref, a_out, i // 2) if i % 2 == 0 else fn(b_ref, b_out, i // 2)
+
+    def read(i):
+        pick(i, lambda src, dst, j: pltpu.make_async_copy(src.at[j], buf.at[i % n_buf], in_sem.at[i % n_buf]).start())
+
+    def read_done(i):
+        pick(i, lambda src, dst, j: pltpu.make_async_copy(src.at[j], buf.at[i % n_buf], in_sem.at[i % n_buf]).wait())
+
+    def write(i):
+        pick(i, lambda src, dst, j: pltpu.make_async_copy(buf.at[i % n_buf], dst.at[j], out_sem.at[i % n_buf]).start())
+
+    def write_done(i):
+        pick(i, lambda src, dst, j: pltpu.make_async_copy(buf.at[i % n_buf], dst.at[j], out_sem.at[i % n_buf]).wait())
+
+    total = 2 * n_seq
+    for i in range(ahead):
+        read(i)
+    for i in range(total):
+        if i + ahead < total:
+            if i + ahead - n_buf >= 0:
+                write_done(i + ahead - n_buf)
+            read(i + ahead)
+        read_done(i)
+        write(i)
+    for i in range(total - n_buf, total):
+        write_done(i)
 
 
 def solution(mesh):
@@ -400,6 +464,7 @@
         two = 2 * piece
         rows_shape = (n_seq, n_rows, head_dim)
         kv_shape = (n_seq, piece, head_dim)
+        late_shape = (N_LATE, two, head_dim)
         bf16, f32, i32 = jnp.bfloat16, jnp.float32, jnp.int32
         dma = pltpu.SemaphoreType.DMA
         any_spec = pl.BlockSpec(memory_space=pl.ANY)
@@ -407,9 +472,10 @@
         out = pl.pallas_call(
             functools.partial(attention_kernel, n_dev, n_heads),
             name='attention',
-            out_shape=[jax.ShapeDtypeStruct(rows_shape, bf16)] * 2 + [jax.ShapeDtypeStruct(kv_shape, bf16)] * 2,
+            out_shape=[jax.ShapeDtypeStruct(rows_shape, bf16)] * 2 + [jax.ShapeDtypeStruct(kv_shape, bf16)] * 2
+            + [jax.ShapeDtypeStruct(late_shape, f32)] * 3,
             in_specs=[any_spec] * 5,
-            out_specs=[any_spec] * 4,
+            out_specs=[any_spec] * 7,
             scratch_shapes=[
                 pltpu.VMEM((n_seq, 2, n_key, head_dim), bf16),
                 pltpu.VMEM((n_seq, two, head_dim), f32),
@@ -426,6 +492,7 @@
                 pltpu.VMEM((n_rows, n_key), bf16),
                 pltpu.VMEM(kv_shape, bf16),
                 pltpu.VMEM(kv_shape, bf16),
+                pltpu.VMEM(late_shape, f32),
                 pltpu.VMEM((n_dev, n_seq, piece), i32),
                 pltpu.VMEM((n_seq, 1, n_key), i32),
                 pltpu.VMEM((n_seq, 1, piece), i32),
@@ -433,11 +500,29 @@
                 dma((3,)), dma, dma,
                 dma((4,)), dma((n_chip, n_seq)), dma((n_chip,)), dma((n_chip, n_seq)),
                 dma((2,)), dma((2,)), dma((2,)), dma((2,)),
-                dma((2,)), dma((NPRX,)), dma((3, n_seq)), dma((3, NACC)), dma,
+                dma((2,)), dma((NPRX,)), dma((3, n_seq)), dma((3, NACC)), dma, dma,
             ],
             compiler_params=pltpu.CompilerParams(collective_id=0, has_side_effects=True, vmem_limit_bytes=63 * 1024 * 1024),
         )(query.reshape(rows_shape), grad_out.reshape(rows_shape), keys.reshape(kv_shape), values.reshape(kv_shape), doc_id)
-        attn_out, grad_query, grad_keys, grad_values = out
+        attn_out, grad_query, grad_keys, grad_values, near, far, own = out
+        attn_out, grad_query = pl.pallas_call(
+            copy_kernel,
+            name='results',
+            out_shape=[jax.ShapeDtypeStruct(rows_shape, bf16)] * 2,
+            in_specs=[any_spec] * 2,
+            out_specs=[any_spec] * 2,
+            scratch_shapes=[pltpu.VMEM((N_COPY, n_rows, head_dim), bf16), dma((N_COPY,)), dma((N_COPY,))],
+            compiler_params=pltpu.CompilerParams(vmem_limit_bytes=48 * 1024 * 1024),
+            cost_estimate=pl.CostEstimate(flops=12_000_000_000, bytes_accessed=8 * n_seq * n_rows * head_dim,
+                                          transcendentals=0),
+        )(attn_out, grad_query)
+        to_near = [(d, d - 2) for d in range(2, n_dev)]
+        to_far = [(n_dev - 2 + e, e) for e in range(2)]
+        late = own + lax.ppermute(near, 'cp', to_near) + lax.ppermute(far, 'cp', to_far)
+        late_keys = (late[:, 0:piece] * head_dim ** -0.5).astype(bf16)
+        late_values = late[:, piece:two].astype(bf16)
+        grad_keys = jnp.concatenate([grad_keys[:n_seq - N_LATE], late_keys])
+        grad_values = jnp.concatenate([grad_values[:n_seq - N_LATE], late_values])
         return (attn_out.reshape(query.shape), grad_query.reshape(query.shape),
                 grad_keys.reshape(keys.shape), grad_values.reshape(values.shape))
 

time: 191 us -> 190 us (level)
  local copies, waits for them, and re-layouts: 25.1 us -> 2.49 us
  Pallas kernels: 165 us -> 182 us
  starting transfers between devices: 0 us -> 2.62 us
    unnamed x10 -> x2, local copies, waits for them, and re-layouts: 25.1 us -> 0.01 us
    pallas_call x0 -> x1, Pallas kernels: none -> 22.6 us  [per_device(): pl.pallas_call(copy_kernel, name='results', out_shape=[jax.ShapeDtypeStru...]
    pallas_call x1, Pallas kernels: 165 us -> 160 us  [per_device(): pl.pallas_call(functools.partial(attention_kernel, n_dev, n_heads), name=...]
    ppermute x0 -> x2, starting transfers between devices: none -> 2.62 us  [the longest x1 1.31 us: per_device(): lax.ppermute(far, 'cp', to_far)]
    slice x0 -> x3, local copies, waits for them, and re-layouts: none -> 2.48 us  [the longest x1 1.23 us: per_device(): grad_values = jnp.concatenate([grad_values[:n_seq - N_LATE], late_values])]
  transfers between devices with their start and end apart: 0 -> 2, of which waited for: 0 -> 0; matrix products, arithmetic and copies ran while one was open for 0% -> 1% of each run, Pallas kernels for 0% -> 12%
where the time goes in v4:
time: 190 us
  Pallas kernels  182 us (96%)
  starting transfers between devices  2.62 us (1%)
  local copies, waits for them, and re-layouts  2.49 us (1%)
    pallas_call x1, Pallas kernels, per_device(): pl.pallas_call(functools.partial(attention_kernel, n_dev, n_heads), name=...  160 us
    pallas_call x1, Pallas kernels, per_device(): pl.pallas_call(copy_kernel, name='results', out_shape=[jax.ShapeDtypeStru...  22.6 us
  transfers between devices with their start and end apart: 2, of which 0 were waited for; matrix products, arithmetic and copies ran while one was open for 1% of the time, Pallas kernels for 12%

profile of v4, /device:TPU:113, one launch (start us, length us, event | category | flops | bytes accessed | tf_op | source)
XLA Modules:
  0.0 189.7 jit_solution(9011586292155978498)
XLA Ops:
  0.6 159.6 %attention.1 = (bf16[32,1024,256]{2,1,0:T(8,128)(2,1)}, bf16[32,1024,256]{2,1,0:T(8,128)(2,1)}, bf16[32,64,256]{2,1,0:T(8,128)(2,1)}, bf16[32,64,256]{2,1,0:T(8,...) custom-call(bf16[32,1024,256]{2,1,0:T(8,128)(2,1)} %bitcast.14, ...), custom_call_target="tpu_custom_call" | custom-call | tf_op jit(solution)/shard_map/attention/pallas_call | solution.py:472
  160.2 1.3 collective-permute-start
  161.5 1.3 collective-permute-start.1
  162.8 1.2 slice.13
  164.1 1.2 slice.15
  165.3 0.0 copy-start
  165.3 22.6 %results.1 = (bf16[32,1024,256]{2,1,0:T(8,128)(2,1)}, bf16[32,1024,256]{2,1,0:T(8,128)(2,1)}) custom-call(bf16[32,1024,256]{2,1,0:T(8,128)(2,1)} %get-tuple-element.13.a_ref, bf16[32,1024,256]{2,1,0:T(8,128)(2,1)} %get-tuple-element.14.b_ref), custom_call_target="tpu_custom_call" | custom-call | flops 12000000000 | bytes 67108864 | tf_op jit(solution)/shard_map/results/pallas_call | solution.py:508
  188.0 0.0 collective-permute-done
  188.0 0.0 collective-permute-done.1
  188.0 0.0 copy-done
  188.0 0.2 add_add_fusion
  188.2 1.5 maximum_bitcast_fusion
  (2 shorter events, 0.0 us)
Async XLA Ops:
  160.2 27.8 %collective-permute-start = (f32[6,128,256]{2,1,0:T(8,128)}, f32[6,128,256]{2,1,0:T(8,128)S(1)}, u32[]{:S(2)}, u32[]{:S(2)}) collective-permute-start(f32[6,128,256]{2,1,0:T(8,128)} %get-tuple-element.19), channel_id=1, source_target_pairs={{2,0},{3,1},{4,2},{5,3},{6,4},{7,5},{10,8},{11,9},{12,10},{13,11},... | collective-permute-start | bytes 2359304 | tf_op jit(solution)/shard_map/ppermute | solution.py:521
  161.5 26.4 %collective-permute-start.1 = (f32[6,128,256]{2,1,0:T(8,128)}, f32[6,128,256]{2,1,0:T(8,128)S(1)}, u32[]{:S(2)}, u32[]{:S(2)}) collective-permute-start(f32[6,128,256]{2,1,0:T(8,128)} %get-tuple-element.20), channel_id=1, source_target_pairs={{6,0},{7,1},{14,8},{15,9}} | collective-permute-start | bytes 2359304 | tf_op jit(solution)/shard_map/ppermute | solution.py:521
  165.3 22.7 %copy-start = (f32[6,128,256]{2,1,0:T(8,128)S(1)}, f32[6,128,256]{2,1,0:T(8,128)}, u32[]{:S(2)}) copy-start(f32[6,128,256]{2,1,0:T(8,128)} %get-tuple-element.18) | copy-start | bytes 2359300

commit v5 on v4

--- a/solution.py
+++ b/solution.py
@@ -12,7 +12,6 @@
 HIDDEN = -3.0e38
 NACC = 12
 NPRX = 4
-N_ROWCHUNK = 4
 N_COPY = 16
 N_LATE = 6
 
@@ -34,27 +33,10 @@
 FINISH_LATE = {(1, 1): (1,)}
 
 
-def row_plan(n):
-    out = [('A', 0), ('A', 1)]
-    for i in range(n + 2):
-        if i + 2 < n:
-            out.append(('A', i + 2))
-        if i < n:
-            out.append(('B', i))
-        if 0 <= i - 1 < n:
-            out.append(('D', i - 1))
-            out.append(('E', i - 1))
-        if i < n:
-            out.append(('C', i))
-        if i == n - 1:
-            out.append(('V', 0))
-    return out
-
-
 def attention_kernel(n_dev, n_heads, *refs):
     (q_ref, g_ref, k_ref, v_ref, doc_ref, o_ref, dq_ref, dk_ref, dv_ref, near_ref, far_ref, own_ref,
-     kv, rx0, rx1, rx2, acc, part, prx, qb, gb, ob, dqb, pb, dsb, fin_k, fin_v, own, docs, kdoc, odoc, vis,
-     load_sem, doc_tx, doc_rx, kv_tx, kv_rx, kvp_tx, kvp_rx, q_sem, g_sem, o_sem, dq_sem,
+     kv, rx0, rx1, rx2, acc, part, prx, qg, odq, pb, dsb, fin_k, fin_v, own, docs, kdoc, odoc, vis,
+     load_sem, doc_tx, doc_rx, kv_tx, kv_rx, kvp_tx, kvp_rx, qg_sem, odq_sem,
      part_tx, prx_sem, rx_sem, tx_sem, fwd_tx, late_sem) = refs
     rx = (rx0, rx1, rx2)
     n_seq, n_rows, head_dim = q_ref.shape
@@ -66,7 +48,6 @@
     chip = me // 2
     core = me % 2
     partner = chip * 2 + (1 - core)
-    my_rows = pl.ds(pl.multiple_of(me * piece, piece), piece)
 
     def dev(c):
         return {'cp': c * 2 + core}
@@ -82,27 +63,25 @@
     for hop in range(1, n_dev):
         pl.semaphore_signal(barrier, inc=1, device_id={'cp': (me + hop) % n_dev}, device_id_type=MESH)
 
-    own_k = pltpu.make_async_copy(k_ref, kv.at[:, 0, my_rows, :], load_sem.at[0])
-    own_v = pltpu.make_async_copy(v_ref, kv.at[:, 1, my_rows, :], load_sem.at[1])
+    own_k = pltpu.make_async_copy(k_ref, kv.at[:, 0, chip, core], load_sem.at[0])
+    own_v = pltpu.make_async_copy(v_ref, kv.at[:, 1, chip, core], load_sem.at[1])
     own_d = pltpu.make_async_copy(doc_ref, docs.at[me], load_sem.at[2])
     own_k.start()
     own_v.start()
     own_d.start()
 
-    def q_copy(b):
-        return pltpu.make_async_copy(q_ref.at[b], qb.at[b % 2], q_sem.at[b % 2])
-
-    def g_copy(b):
-        return pltpu.make_async_copy(g_ref.at[b], gb.at[b % 2], g_sem.at[b % 2])
-
-    def o_copy(b):
-        return pltpu.make_async_copy(ob.at[b % 2], o_ref.at[b], o_sem.at[b % 2])
-
-    def dq_copy(b):
-        return pltpu.make_async_copy(dqb.at[b % 2], dq_ref.at[b], dq_sem.at[b % 2])
-
-    q_copy(0).start()
-    g_copy(0).start()
+    def qg_start(b):
+        pltpu.make_async_copy(q_ref.at[b], qg.at[b % 2, 0], qg_sem.at[b % 2]).start()
+        pltpu.make_async_copy(g_ref.at[b], qg.at[b % 2, 1], qg_sem.at[b % 2]).start()
+
+    def odq_start(b):
+        pltpu.make_async_copy(odq.at[b % 2, 0], o_ref.at[b], odq_sem.at[b % 2]).start()
+        pltpu.make_async_copy(odq.at[b % 2, 1], dq_ref.at[b], odq_sem.at[b % 2]).start()
+
+    def odq_wait(b):
+        local_wait(odq.at[b % 2], odq_sem.at[b % 2])
+
+    qg_start(0)
     own_k.wait()
     own_v.wait()
     own_d.wait()
@@ -121,10 +100,6 @@
         for to in doc_dests:
             doc_copy(to).start()
 
-        def kv_block(src, src_core, b):
-            rows = pl.ds(pl.multiple_of((src * 2 + src_core) * piece, piece), piece)
-            return kv.at[b, :, rows, :]
-
         flows = [hop[1:] for hop in HOPS if hop[0] == c]
         through = [src for src, _, _ in flows if src > c]
 
@@ -134,34 +109,39 @@
             else:
                 pl.when(core == who)(fn)
 
+        def kv_sem(src, to, b):
+            return kv_rx.at[0 if to == n_chip - 1 else src, b]
+
         def kv_copy(i, b):
             src, to, _ = flows[i]
-            blk = kv_block(src, core, b)
-            return remote(blk, blk, kv_tx.at[i], kv_rx.at[src, b], dev(to))
+            blk = kv.at[b, :, src, core]
+            return remote(blk, blk, kv_tx.at[i], kv_sem(src, to, b), dev(to))
+
+        def kvp_copy(b):
+            blk = kv.at[b, :, here, core]
+            return remote(blk, blk, kvp_tx, kvp_rx.at[b], {'cp': partner})
 
         def send_on(src, b):
             for i, (s, _, who) in enumerate(flows):
                 if s == src:
                     by_core(who, lambda: kv_copy(i, b).start())
 
-        def kvp_copy(src, b):
-            blk = kv_block(src, core, b)
-            return remote(blk, blk, kvp_tx.at[src], kvp_rx.at[src, b], {'cp': partner})
-
         def push(b):
             send_on(c, b)
-            kvp_copy(c, b).start()
 
         def take(b):
-            for src in range(c - 1, -1, -1):
-                local_wait(kv_block(src, core, b), kv_rx.at[src, b])
-                send_on(src, b)
-                kvp_copy(src, b).start()
+            if c == n_chip - 1:
+                local_wait(kv.at[b, :, pl.ds(0, c), core], kv_rx.at[0, b])
+            else:
+                for src in range(c - 1, -1, -1):
+                    local_wait(kv.at[b, :, src, core], kv_rx.at[src, b])
+                    send_on(src, b)
+            kvp_copy(b).start()
             for src in through:
                 who = [w for s, _, w in flows if s == src][0]
 
                 def pass_on():
-                    local_wait(kv_block(src, core, b), kv_rx.at[src, b])
+                    local_wait(kv.at[b, :, src, core], kv_rx.at[src, b])
                     for i, (s, _, _) in enumerate(flows):
                         if s == src:
                             kv_copy(i, b).start()
@@ -181,8 +161,7 @@
             return start, at_step
 
         def arrived(b):
-            for src in range(c + 1):
-                local_wait(kv_block(src, 1 - core, b), kvp_rx.at[src, b])
+            local_wait(kv.at[b, :, here, 1 - core], kvp_rx.at[b])
 
         n_push, push_at = ramp(PUSH[c], push)
         n_take, take_at = ramp(TAKE[c], take)
@@ -198,8 +177,8 @@
 
         def compute(b):
             slot = b % 2
-            keys = kv[b, 0, 0:n_key, :]
-            vals = kv[b, 1, 0:n_key, :]
+            keys = kv[b, 0, here].reshape(n_key, head_dim)
+            vals = kv[b, 1, here].reshape(n_key, head_dim)
             tok = lax.broadcasted_iota(jnp.int32, (piece, piece), 0)
             tok_t = lax.broadcasted_iota(jnp.int32, (piece, piece), 1)
             own_doc = odoc[b]
@@ -208,64 +187,25 @@
             q_pos = me * piece + lax.broadcasted_iota(jnp.int32, (piece, n_key), 0)
             k_pos = lax.broadcasted_iota(jnp.int32, (piece, n_key), 1)
             seen = (q_doc == key_doc) & (k_pos <= q_pos)
-            vis[:, 0:n_key] = jnp.where(seen, 1.0, 0.0)
-            rc = n_rows // N_ROWCHUNK
-            tc = rc // n_heads
+            vis[:, 0:n_key] = jnp.where(seen, 0.0, HIDDEN)
             nt = (((1,), (1,)), ((), ()))
             tn = (((0,), (0,)), ((), ()))
-            live = {}
-
-            def span(ch):
-                return slice(ch * rc, (ch + 1) * rc)
-
-            def scores(ch):
-                live['s', ch] = lax.dot_general(qb[slot, span(ch), :], keys, nt, preferred_element_type=jnp.float32)
-                live['dp', ch] = lax.dot_general(gb[slot, span(ch), :], vals, nt, preferred_element_type=jnp.float32)
-
-            def softmax(ch):
-                seen_c = vis[ch * tc:(ch + 1) * tc, 0:n_key].reshape(tc, 1, n_key)
-                s3 = live.pop(('s', ch)).reshape(tc, n_heads, n_key)
-                s = jnp.where(seen_c > 0.5, s3 * (scale * LOG2E), HIDDEN).reshape(rc, n_key)
-                e = jnp.exp2(s - jnp.max(s, axis=1, keepdims=True))
-                p = e * (1.0 / jnp.sum(e, axis=1, keepdims=True))
-                live['p', ch] = p
-                pb[span(ch), 0:n_key] = p.astype(jnp.bfloat16)
-
-            def attend(ch):
-                o = jnp.dot(pb[span(ch), 0:n_key], vals, preferred_element_type=jnp.float32)
-                live['o', ch] = o.astype(jnp.bfloat16)
-
-            def dscores(ch):
-                o16 = live.pop(('o', ch))
-                ob[slot, span(ch), :] = o16
-                gc = gb[slot, span(ch), :].astype(jnp.float32)
-                delta = jnp.sum(gc * o16.astype(jnp.float32), axis=1, keepdims=True)
-                dsb[span(ch), 0:n_key] = (live.pop(('p', ch)) * (live.pop(('dp', ch)) - delta)).astype(jnp.bfloat16)
-
-            def dquery(ch):
-                dq = jnp.dot(dsb[span(ch), 0:n_key], keys, preferred_element_type=jnp.float32)
-                dqb[slot, span(ch), :] = (dq * scale).astype(jnp.bfloat16)
-
-            def key_sums():
-                live['dv'] = lax.dot_general(pb[:, 0:n_key], gb[slot], tn, preferred_element_type=jnp.float32)
-
-            stages = row_plan(N_ROWCHUNK)
-            for name, ch in stages:
-                if name == 'A':
-                    scores(ch)
-                elif name == 'B':
-                    softmax(ch)
-                elif name == 'C':
-                    attend(ch)
-                elif name == 'D':
-                    dscores(ch)
-                elif name == 'E':
-                    dquery(ch)
-                elif name == 'V':
-                    key_sums()
-            dv = live['dv']
-            dk = lax.dot_general(dsb[:, 0:n_key], qb[slot], tn, preferred_element_type=jnp.float32)
-
+            f32 = jnp.float32
+            s = lax.dot_general(qg[slot, 0], keys, nt, preferred_element_type=f32)
+            dp = lax.dot_general(qg[slot, 1], vals, nt, preferred_element_type=f32)
+            s = s.reshape(piece, n_heads, n_key) * (scale * LOG2E) + vis[:, 0:n_key].reshape(piece, 1, n_key)
+            s = s.reshape(n_rows, n_key)
+            e = jnp.exp2(s - jnp.max(s, axis=1, keepdims=True))
+            p = e * (1.0 / jnp.sum(e, axis=1, keepdims=True))
+            pb[:, 0:n_key] = p.astype(jnp.bfloat16)
+            o16 = jnp.dot(pb[:, 0:n_key], vals, preferred_element_type=f32).astype(jnp.bfloat16)
+            dv = lax.dot_general(pb[:, 0:n_key], qg[slot, 1], tn, preferred_element_type=f32)
+            odq[slot, 0] = o16
+            delta = jnp.sum(qg[slot, 1].astype(f32) * o16.astype(f32), axis=1, keepdims=True)
+            dsb[:, 0:n_key] = (p * (dp - delta)).astype(jnp.bfloat16)
+            dq = jnp.dot(dsb[:, 0:n_key], keys, preferred_element_type=f32)
+            odq[slot, 1] = (dq * scale).astype(jnp.bfloat16)
+            dk = lax.dot_general(dsb[:, 0:n_key], qg[slot, 0], tn, preferred_element_type=f32)
             for a in range(c + 1):
                 for p in range(2):
                     rows = slice((2 * a + p) * piece, (2 * a + p + 1) * piece)
@@ -279,7 +219,7 @@
         def unit_send(b, e, i):
             a, to, buf, _, late = SENDS[c, e][i]
             unit = acc.at[b % NACC, a]
-            sem = tx_sem.at[i, b % NACC]
+            sem = tx_sem.at[b % NACC]
 
             def now():
                 remote(unit, rx[buf].at[b], sem, rx_sem.at[buf, b], dev(to)).start()
@@ -346,11 +286,9 @@
 
         def sent(b):
             for e in range(2):
-                if (c, e) in SENDS:
-                    @pl.when(core == e)
-                    def _():
-                        for i in range(len(SENDS[c, e])):
-                            local_wait(acc.at[b % NACC, SENDS[c, e][i][0]], tx_sem.at[i, b % NACC])
+                n = len(SENDS.get((c, e), ()))
+                if n:
+                    pl.when(core == e)(lambda: local_wait(acc.at[b % NACC, pl.ds(0, n)], tx_sem.at[b % NACC]))
 
         def step(t, carry):
             @pl.when(t < n_seq)
@@ -360,22 +298,18 @@
 
                 @pl.when(t + 1 < n_seq)
                 def _():
-                    q_copy(t + 1).start()
-                    g_copy(t + 1).start()
+                    qg_start(t + 1)
 
                 @pl.when(t >= 2)
                 def _():
-                    o_copy(t - 2).wait()
-                    dq_copy(t - 2).wait()
+                    odq_wait(t - 2)
                     part_copy(t - 2).wait_send()
 
                 pl.when(t >= NACC)(lambda: sent(t - NACC))
                 arrived(t)
-                q_copy(t).wait()
-                g_copy(t).wait()
+                local_wait(qg.at[t % 2], qg_sem.at[t % 2])
                 compute(t)
-                o_copy(t).start()
-                dq_copy(t).start()
+                odq_start(t)
                 part_copy(t).start()
 
             when_seq(t - 1, merge_partner)
@@ -390,16 +324,14 @@
         lax.fori_loop(0, n_step, step, 0)
 
         for b in (n_seq - 2, n_seq - 1):
-            o_copy(b).wait()
-            dq_copy(b).wait()
+            odq_wait(b)
             part_copy(b).wait_send()
         for b in range(n_seq - NACC, n_seq):
             sent(b)
-        whole = kv.at[:, :, pl.ds(0, piece), :]
+        whole = kv.at[:, :, 0, 0]
         for i, (_, _, who) in enumerate(flows):
             by_core(who, lambda: local_wait(whole, kv_tx.at[i]))
-        for src in range(c + 1):
-            local_wait(whole, kvp_tx.at[src])
+        local_wait(kv.at[:, :, here, 0], kvp_tx)
         for to in doc_dests:
             doc_copy(to).wait_send()
         if c == 0:
@@ -465,6 +397,7 @@
         rows_shape = (n_seq, n_rows, head_dim)
         kv_shape = (n_seq, piece, head_dim)
         late_shape = (N_LATE, two, head_dim)
+        main_shape = (n_seq - N_LATE, piece, head_dim)
         bf16, f32, i32 = jnp.bfloat16, jnp.float32, jnp.int32
         dma = pltpu.SemaphoreType.DMA
         any_spec = pl.BlockSpec(memory_space=pl.ANY)
@@ -472,35 +405,33 @@
         out = pl.pallas_call(
             functools.partial(attention_kernel, n_dev, n_heads),
             name='attention',
-            out_shape=[jax.ShapeDtypeStruct(rows_shape, bf16)] * 2 + [jax.ShapeDtypeStruct(kv_shape, bf16)] * 2
+            out_shape=[jax.ShapeDtypeStruct(rows_shape, bf16)] * 2 + [jax.ShapeDtypeStruct(main_shape, bf16)] * 2
             + [jax.ShapeDtypeStruct(late_shape, f32)] * 3,
             in_specs=[any_spec] * 5,
             out_specs=[any_spec] * 7,
             scratch_shapes=[
-                pltpu.VMEM((n_seq, 2, n_key, head_dim), bf16),
+                pltpu.VMEM((n_seq, 2, n_chip, 2, piece, head_dim), bf16),
                 pltpu.VMEM((n_seq, two, head_dim), f32),
                 pltpu.VMEM((n_seq, two, head_dim), f32),
                 pltpu.VMEM((n_seq, two, head_dim), f32),
                 pltpu.VMEM((NACC, n_chip, two, head_dim), f32),
                 pltpu.VMEM((2, 2, n_chip, two, head_dim), f32),
                 pltpu.VMEM((NPRX, n_chip, two, head_dim), f32),
-                pltpu.VMEM((2, n_rows, head_dim), bf16),
-                pltpu.VMEM((2, n_rows, head_dim), bf16),
-                pltpu.VMEM((2, n_rows, head_dim), bf16),
-                pltpu.VMEM((2, n_rows, head_dim), bf16),
+                pltpu.VMEM((2, 2, n_rows, head_dim), bf16),
+                pltpu.VMEM((2, 2, n_rows, head_dim), bf16),
                 pltpu.VMEM((n_rows, n_key), bf16),
                 pltpu.VMEM((n_rows, n_key), bf16),
-                pltpu.VMEM(kv_shape, bf16),
-                pltpu.VMEM(kv_shape, bf16),
+                pltpu.VMEM(main_shape, bf16),
+                pltpu.VMEM(main_shape, bf16),
                 pltpu.VMEM(late_shape, f32),
                 pltpu.VMEM((n_dev, n_seq, piece), i32),
                 pltpu.VMEM((n_seq, 1, n_key), i32),
                 pltpu.VMEM((n_seq, 1, piece), i32),
                 pltpu.VMEM((piece, n_key), f32),
                 dma((3,)), dma, dma,
-                dma((4,)), dma((n_chip, n_seq)), dma((n_chip,)), dma((n_chip, n_seq)),
-                dma((2,)), dma((2,)), dma((2,)), dma((2,)),
-                dma((2,)), dma((NPRX,)), dma((3, n_seq)), dma((3, NACC)), dma, dma,
+                dma((4,)), dma((n_chip, n_seq)), dma, dma((n_seq,)),
+                dma((2,)), dma((2,)),
+                dma((2,)), dma((NPRX,)), dma((3, n_seq)), dma((NACC,)), dma, dma,
             ],
             compiler_params=pltpu.CompilerParams(collective_id=0, has_side_effects=True, vmem_limit_bytes=63 * 1024 * 1024),
         )(query.reshape(rows_shape), grad_out.reshape(rows_shape), keys.reshape(kv_shape), values.reshape(kv_shape), doc_id)
@@ -521,8 +452,8 @@
         late = own + lax.ppermute(near, 'cp', to_near) + lax.ppermute(far, 'cp', to_far)
         late_keys = (late[:, 0:piece] * head_dim ** -0.5).astype(bf16)
         late_values = late[:, piece:two].astype(bf16)
-        grad_keys = jnp.concatenate([grad_keys[:n_seq - N_LATE], late_keys])
-        grad_values = jnp.concatenate([grad_values[:n_seq - N_LATE], late_values])
+        grad_keys = jnp.concatenate([grad_keys, late_keys])
+        grad_values = jnp.concatenate([grad_values, late_values])
         return (attn_out.reshape(query.shape), grad_query.reshape(query.shape),
                 grad_keys.reshape(keys.shape), grad_values.reshape(values.shape))
 

time: 190 us -> 186 us (0.979)
  local copies, waits for them, and re-layouts: 2.49 us -> 0.04 us
    pallas_call x1, Pallas kernels: 160 us -> 157 us  [per_device(): pl.pallas_call(functools.partial(attention_kernel, n_dev, n_heads), name=...]
    slice x2 -> x0, local copies, waits for them, and re-layouts: 2.46 us -> none  [the longest x1 1.23 us: per_device(): grad_values = jnp.concatenate([grad_values[:n_seq - N_LATE], late_values])]
  transfers between devices with their start and end apart: 2 -> 2, of which waited for: 0 -> 0; matrix products, arithmetic and copies ran while one was open for 1% -> 0% of each run, Pallas kernels for 12% -> 13%
where the time goes in v5:
time: 186 us
  Pallas kernels  181 us (97%)
  starting transfers between devices  2.62 us (1%)
    pallas_call x1, Pallas kernels, per_device(): pl.pallas_call(functools.partial(attention_kernel, n_dev, n_heads), name=...  157 us
    pallas_call x1, Pallas kernels, per_device(): pl.pallas_call(copy_kernel, name='results', out_shape=[jax.ShapeDtypeStru...  23.9 us
  transfers between devices with their start and end apart: 2, of which 0 were waited for; matrix products, arithmetic and copies ran while one was open for 0% of the time, Pallas kernels for 13%

profile of v5, /device:TPU:113, one launch (start us, length us, event | category | flops | bytes accessed | tf_op | source)
XLA Modules:
  0.0 185.9 jit_solution(10254467563614742518)
XLA Ops:
  0.6 156.9 %attention.1 = (bf16[32,1024,256]{2,1,0:T(8,128)(2,1)}, bf16[32,1024,256]{2,1,0:T(8,128)(2,1)}, bf16[26,64,256]{2,1,0:T(8,128)(2,1)}, bf16[26,64,256]{2,1,0:T(8,...) custom-call(bf16[32,1024,256]{2,1,0:T(8,128)(2,1)} %bitcast.14, ...), custom_call_target="tpu_custom_call" | custom-call | tf_op jit(solution)/shard_map/attention/pallas_call | solution.py:405
  157.5 1.3 collective-permute-start
  158.9 1.3 collective-permute-start.1
  160.2 0.0 copy-start.2
  160.2 0.0 copy-start
  160.2 0.0 copy-start.1
  160.2 23.9 %results.1 = (bf16[32,1024,256]{2,1,0:T(8,128)(2,1)}, bf16[32,1024,256]{2,1,0:T(8,128)(2,1)}) custom-call(bf16[32,1024,256]{2,1,0:T(8,128)(2,1)} %get-tuple-element.13.a_ref, bf16[32,1024,256]{2,1,0:T(8,128)(2,1)} %get-tuple-element.14.b_ref), custom_call_target="tpu_custom_call" | custom-call | flops 12000000000 | bytes 67108864 | tf_op jit(solution)/shard_map/results/pallas_call | solution.py:439
  184.1 0.0 collective-permute-done
  184.1 0.0 collective-permute-done.1
  184.1 0.0 copy-done.2
  184.1 0.2 add_add_fusion
  184.3 0.0 copy-done
  184.3 0.0 copy-done.1
  184.3 1.5 maximum_bitcast_fusion
  (2 shorter events, 0.0 us)
Async XLA Ops:
  157.5 26.5 %collective-permute-start = (f32[6,128,256]{2,1,0:T(8,128)}, f32[6,128,256]{2,1,0:T(8,128)S(1)}, u32[]{:S(2)}, u32[]{:S(2)}) collective-permute-start(f32[6,128,256]{2,1,0:T(8,128)} %get-tuple-element.19), channel_id=1, source_target_pairs={{2,0},{3,1},{4,2},{5,3},{6,4},{7,5},{10,8},{11,9},{12,10},{13,11},... | collective-permute-start | bytes 2359304 | tf_op jit(solution)/shard_map/ppermute | solution.py:452
  158.9 25.2 %collective-permute-start.1 = (f32[6,128,256]{2,1,0:T(8,128)}, f32[6,128,256]{2,1,0:T(8,128)S(1)}, u32[]{:S(2)}, u32[]{:S(2)}) collective-permute-start(f32[6,128,256]{2,1,0:T(8,128)} %get-tuple-element.20), channel_id=1, source_target_pairs={{6,0},{7,1},{14,8},{15,9}} | collective-permute-start | bytes 2359304 | tf_op jit(solution)/shard_map/ppermute | solution.py:452
  160.2 23.9 %copy-start.2 = (f32[6,128,256]{2,1,0:T(8,128)S(1)}, f32[6,128,256]{2,1,0:T(8,128)}, u32[]{:S(2)}) copy-start(f32[6,128,256]{2,1,0:T(8,128)} %get-tuple-element.18) | copy-start | bytes 2359300
  160.2 24.2 %copy-start = (bf16[26,64,256]{2,1,0:T(8,128)(2,1)S(1)}, bf16[26,64,256]{2,1,0:T(8,128)(2,1)}, u32[]{:S(2)}) copy-start(bf16[26,64,256]{2,1,0:T(8,128)(2,1)} %get-tuple-element.17) | copy-start | bytes 2555908
  160.2 24.2 %copy-start.1 = (bf16[26,64,256]{2,1,0:T(8,128)(2,1)S(1)}, bf16[26,64,256]{2,1,0:T(8,128)(2,1)}, u32[]{:S(2)}) copy-start(bf16[26,64,256]{2,1,0:T(8,128)(2,1)} %get-tuple-element.21) | copy-start | bytes 2555908

commit v6 on v5

--- a/solution.py
+++ b/solution.py
@@ -13,23 +13,16 @@
 NACC = 12
 NPRX = 4
 N_COPY = 16
-N_LATE = 6
-
-
-HOPS = ((1, 1, 2, None), (1, 1, 0, 1), (2, 1, 3, 0), (0, 1, 3, 1), (1, 0, 2, None), (2, 2, 3, None), (0, 0, 1, None),
-        (0, 0, 3, None))
-PUSH = {0: (1, 7), 1: (3, 9), 2: (3, 2), 3: (2, 5)}
-TAKE = {0: (0, 8), 1: (4, 4), 2: (2, 2), 3: (0, 1)}
-SENDS = {(3, 0): ((1, 2, 0, False, None), (0, 0, 1, False, 1), (2, 2, 1, False, 0)),
-         (3, 1): ((2, 2, 0, False, 0), (0, 0, 0, True, 1), (1, 0, 2, False, None)),
-         (2, 0): ((0, 1, 0, False, None), (1, 1, 1, True, 0)),
-         (2, 1): ((0, 3, 0, False, None), (1, 1, 0, False, 0)),
-         (1, 0): ((0, 0, 0, True, 0),),
-         (1, 1): ((0, 0, 1, False, 0),)}
-RELAY = {(3, 1): (2, 0), (2, 0): (2, 0), (1, 0): (3, 0), (0, 1): (4, 2)}
-FINISH = {(3, 0): (1, ()), (3, 1): (1, ()), (2, 0): (5, (1,)), (2, 1): (5, (0,)), (1, 0): (8, (1,)), (1, 1): (6, (0, 1)),
-          (0, 0): (8, (0, 1)), (0, 1): (8, (0, 1))}
-LAG_MAX = 8
+N_LATE = 9
+
+
+HOPS = ((1, 0, 2, None), (1, 1, 0, 1), (2, 2, 3, None), (0, 1, 3, 1), (1, 1, 2, None), (2, 1, 3, 0), (0, 0, 1, None), (0, 0, 3, None))
+PUSH = {0: (1, 6), 1: (2, 12), 2: (3, 4), 3: (2, 5)}
+TAKE = {0: (0, 10), 1: (3, 5), 2: (2, 2), 3: (0, 1)}
+SENDS = {(3, 0): ((1, 2, 0, False, None), (0, 0, 1, False, 1), (2, 2, 1, False, 0)), (3, 1): ((2, 2, 0, False, 0), (0, 0, 0, True, 1), (1, 0, 2, False, None)), (2, 0): ((1, 1, 1, True, 0), (0, 1, 0, False, None)), (2, 1): ((0, 3, 0, False, None), (1, 1, 0, False, 0)), (1, 0): ((0, 0, 0, True, 0),), (1, 1): ((0, 0, 1, False, 0),)}
+RELAY = {(3, 1): (3, 0), (2, 0): (7, 0), (1, 0): (5, 0), (0, 1): (6, 2)}
+FINISH = {(3, 0): (1, ()), (3, 1): (1, ()), (2, 0): (9, (1,)), (2, 1): (5, (0,)), (1, 0): (10, (1,)), (1, 1): (6, (0, 1)), (0, 0): (8, (0, 1)), (0, 1): (9, (0, 1))}
+LAG_MAX = 10
 FINISH_LATE = {(1, 1): (1,)}
 
 

time: 186 us -> 175 us (0.941)
  Pallas kernels: 181 us -> 164 us
  waiting for transfers between devices: 0.01 us -> 5.43 us
    pallas_call x1, Pallas kernels: 157 us -> 141 us  [per_device(): pl.pallas_call(functools.partial(attention_kernel, n_dev, n_heads), name=...]
    ppermute x1, waiting for transfers between devices: 0.01 us -> 4.31 us  [per_device(): lax.ppermute(near, 'cp', to_near)]
  transfers between devices with their start and end apart: 2 -> 2, of which waited for: 0 -> 2; matrix products, arithmetic and copies ran while one was open for 0% -> 0% of each run, Pallas kernels for 13% -> 13%
where the time goes in v6:
time: 175 us
  Pallas kernels  164 us (94%)
  waiting for transfers between devices  5.43 us (3%)
  starting transfers between devices  2.62 us (1%)
  other arithmetic  1.78 us (1%)
    pallas_call x1, Pallas kernels, per_device(): pl.pallas_call(functools.partial(attention_kernel, n_dev, n_heads), name=...  141 us
    pallas_call x1, Pallas kernels, per_device(): pl.pallas_call(copy_kernel, name='results', out_shape=[jax.ShapeDtypeStru...  22.6 us
    ppermute x1, waiting for transfers between devices, per_device(): lax.ppermute(near, 'cp', to_near)  4.31 us
  transfers between devices with their start and end apart: 2, of which 2 were waited for; matrix products, arithmetic and copies ran while one was open for 0% of the time, Pallas kernels for 13%

profile of v6, /device:TPU:113, one launch (start us, length us, event | category | flops | bytes accessed | tf_op | source)
XLA Modules:
  0.0 175.3 jit_solution(11534732463893092505)
XLA Ops:
  0.6 141.0 %attention.1 = (bf16[32,1024,256]{2,1,0:T(8,128)(2,1)}, bf16[32,1024,256]{2,1,0:T(8,128)(2,1)}, bf16[23,64,256]{2,1,0:T(8,128)(2,1)}, bf16[23,64,256]{2,1,0:T(8,...) custom-call(bf16[32,1024,256]{2,1,0:T(8,128)(2,1)} %bitcast.14, ...), custom_call_target="tpu_custom_call" | custom-call | tf_op jit(solution)/shard_map/attention/pallas_call | solution.py:398
  141.6 1.3 collective-permute-start
  143.0 1.3 collective-permute-start.1
  144.3 0.0 copy-start
  144.3 22.6 %results.1 = (bf16[32,1024,256]{2,1,0:T(8,128)(2,1)}, bf16[32,1024,256]{2,1,0:T(8,128)(2,1)}) custom-call(bf16[32,1024,256]{2,1,0:T(8,128)(2,1)} %get-tuple-element.13.a_ref, bf16[32,1024,256]{2,1,0:T(8,128)(2,1)} %get-tuple-element.14.b_ref), custom_call_target="tpu_custom_call" | custom-call | flops 12000000000 | bytes 67108864 | tf_op jit(solution)/shard_map/results/pallas_call | solution.py:432
  166.9 4.3 %collective-permute-done = f32[9,128,256]{2,1,0:T(8,128)S(1)} collective-permute-done((f32[9,128,256]{2,1,0:T(8,128)}, f32[9,128,256]{2,1,0:T(8,128)S(1)}, u32[]{:S(2)}, u32[]{:S(2)}) %collective-permute-start) | collective-permute-done | bytes 1179680 | tf_op jit(solution)/shard_map/ppermute | solution.py:445
  171.2 1.1 collective-permute-done.1
  172.4 0.0 copy-done
  172.4 0.0 copy-start.2
  172.4 0.2 add_add_fusion
  172.6 0.0 copy-start.1
  172.6 0.1 fusion
  172.7 0.8 copy-done.2
  173.5 0.3 copy-done.1
  173.8 1.5 maximum_bitcast_fusion
  (1 shorter events, 0.0 us)
Async XLA Ops:
  141.6 29.6 %collective-permute-start = (f32[9,128,256]{2,1,0:T(8,128)}, f32[9,128,256]{2,1,0:T(8,128)S(1)}, u32[]{:S(2)}, u32[]{:S(2)}) collective-permute-start(f32[9,128,256]{2,1,0:T(8,128)} %get-tuple-element.19), channel_id=1, source_target_pairs={{2,0},{3,1},{4,2},{5,3},{6,4},{7,5},{10,8},{11,9},{12,10},{13,11},... | collective-permute-start | bytes 3538952 | tf_op jit(solution)/shard_map/ppermute | solution.py:445
  143.0 29.4 %collective-permute-start.1 = (f32[9,128,256]{2,1,0:T(8,128)}, f32[9,128,256]{2,1,0:T(8,128)S(1)}, u32[]{:S(2)}, u32[]{:S(2)}) collective-permute-start(f32[9,128,256]{2,1,0:T(8,128)} %get-tuple-element.20), channel_id=1, source_target_pairs={{6,0},{7,1},{14,8},{15,9}} | collective-permute-start | bytes 3538952 | tf_op jit(solution)/shard_map/ppermute | solution.py:445
  144.3 28.1 %copy-start = (f32[9,128,256]{2,1,0:T(8,128)S(1)}, f32[9,128,256]{2,1,0:T(8,128)}, u32[]{:S(2)}) copy-start(f32[9,128,256]{2,1,0:T(8,128)} %get-tuple-element.18) | copy-start | bytes 3538948
  172.4 1.1 copy-start.2
  172.6 1.2 copy-start.1

commit v7 on v6

--- a/solution.py
+++ b/solution.py
@@ -13,15 +13,16 @@
 NACC = 12
 NPRX = 4
 N_COPY = 16
-N_LATE = 9
-
-
-HOPS = ((1, 0, 2, None), (1, 1, 0, 1), (2, 2, 3, None), (0, 1, 3, 1), (1, 1, 2, None), (2, 1, 3, 0), (0, 0, 1, None), (0, 0, 3, None))
+N_FIRST = 1
+N_LATE = 8
+
+
+HOPS = ((2, 1, 3, 0), (1, 0, 2, None), (2, 2, 3, None), (1, 1, 0, 1), (1, 1, 2, None), (0, 0, 3, None), (0, 0, 1, None), (0, 1, 3, 1))
 PUSH = {0: (1, 6), 1: (2, 12), 2: (3, 4), 3: (2, 5)}
-TAKE = {0: (0, 10), 1: (3, 5), 2: (2, 2), 3: (0, 1)}
-SENDS = {(3, 0): ((1, 2, 0, False, None), (0, 0, 1, False, 1), (2, 2, 1, False, 0)), (3, 1): ((2, 2, 0, False, 0), (0, 0, 0, True, 1), (1, 0, 2, False, None)), (2, 0): ((1, 1, 1, True, 0), (0, 1, 0, False, None)), (2, 1): ((0, 3, 0, False, None), (1, 1, 0, False, 0)), (1, 0): ((0, 0, 0, True, 0),), (1, 1): ((0, 0, 1, False, 0),)}
-RELAY = {(3, 1): (3, 0), (2, 0): (7, 0), (1, 0): (5, 0), (0, 1): (6, 2)}
-FINISH = {(3, 0): (1, ()), (3, 1): (1, ()), (2, 0): (9, (1,)), (2, 1): (5, (0,)), (1, 0): (10, (1,)), (1, 1): (6, (0, 1)), (0, 0): (8, (0, 1)), (0, 1): (9, (0, 1))}
+TAKE = {0: (0, 10), 1: (3, 6), 2: (2, 2), 3: (0, 1)}
+SENDS = {(3, 0): ((1, 2, 0, False, None), (0, 0, 1, False, 1), (2, 2, 1, False, 0)), (3, 1): ((2, 2, 0, False, 0), (0, 0, 0, True, 1), (1, 0, 2, False, None)), (2, 0): ((1, 1, 1, True, 0), (0, 1, 0, False, None)), (2, 1): ((1, 1, 0, False, 0), (0, 3, 0, False, None)), (1, 0): ((0, 0, 0, True, 0),), (1, 1): ((0, 0, 1, False, 0),)}
+RELAY = {(3, 1): (3, 0), (2, 0): (6, 0), (1, 0): (8, 0), (0, 1): (6, 2)}
+FINISH = {(3, 0): (1, ()), (3, 1): (1, ()), (2, 0): (9, (1,)), (2, 1): (5, (0,)), (1, 0): (10, (1,)), (1, 1): (10, (0, 1)), (0, 0): (10, (0, 1)), (0, 1): (9, (0, 1))}
 LAG_MAX = 10
 FINISH_LATE = {(1, 1): (1,)}
 
@@ -56,12 +57,16 @@
     for hop in range(1, n_dev):
         pl.semaphore_signal(barrier, inc=1, device_id={'cp': (me + hop) % n_dev}, device_id_type=MESH)
 
-    own_k = pltpu.make_async_copy(k_ref, kv.at[:, 0, chip, core], load_sem.at[0])
-    own_v = pltpu.make_async_copy(v_ref, kv.at[:, 1, chip, core], load_sem.at[1])
-    own_d = pltpu.make_async_copy(doc_ref, docs.at[me], load_sem.at[2])
-    own_k.start()
-    own_v.start()
-    own_d.start()
+    def own_copies(lo, n, sem):
+        seqs = pl.ds(lo, n)
+        return (pltpu.make_async_copy(k_ref.at[seqs], kv.at[seqs, 0, chip, core], load_sem.at[sem]),
+                pltpu.make_async_copy(v_ref.at[seqs], kv.at[seqs, 1, chip, core], load_sem.at[sem + 1]))
+
+    own_d = pltpu.make_async_copy(doc_ref, docs.at[me], load_sem.at[4])
+    own_first = own_copies(0, N_FIRST, 0)
+    own_rest = own_copies(N_FIRST, n_seq - N_FIRST, 2)
+    for copy in (*own_first, own_d, *own_rest):
+        copy.start()
 
     def qg_start(b):
         pltpu.make_async_copy(q_ref.at[b], qg.at[b % 2, 0], qg_sem.at[b % 2]).start()
@@ -75,9 +80,8 @@
         local_wait(odq.at[b % 2], odq_sem.at[b % 2])
 
     qg_start(0)
-    own_k.wait()
-    own_v.wait()
-    own_d.wait()
+    for copy in (*own_first, own_d):
+        copy.wait()
     odoc[...] = docs[me].reshape(n_seq, 1, piece)
     pl.semaphore_wait(barrier, n_dev - 1)
 
@@ -90,8 +94,6 @@
             return remote(docs.at[me], docs.at[me], doc_tx, doc_rx, to)
 
         doc_dests = [{'cp': partner}] + [{'cp': d} for d in range(two // piece * (c + 1), n_dev)]
-        for to in doc_dests:
-            doc_copy(to).start()
 
         flows = [hop[1:] for hop in HOPS if hop[0] == c]
         through = [src for src, _, _ in flows if src > c]
@@ -159,7 +161,15 @@
         n_push, push_at = ramp(PUSH[c], push)
         n_take, take_at = ramp(TAKE[c], take)
         for b in range(n_push):
+            if b == N_FIRST:
+                for copy in own_rest:
+                    copy.wait()
             push(b)
+        if n_push <= N_FIRST:
+            for copy in own_rest:
+                copy.wait()
+        for to in doc_dests:
+            doc_copy(to).start()
         for b in range(n_take):
             take(b)
 
@@ -421,7 +431,7 @@
                 pltpu.VMEM((n_seq, 1, n_key), i32),
                 pltpu.VMEM((n_seq, 1, piece), i32),
                 pltpu.VMEM((piece, n_key), f32),
-                dma((3,)), dma, dma,
+                dma((5,)), dma, dma,
                 dma((4,)), dma((n_chip, n_seq)), dma, dma((n_seq,)),
                 dma((2,)), dma((2,)),
                 dma((2,)), dma((NPRX,)), dma((3, n_seq)), dma((NACC,)), dma, dma,

time: 175 us -> 174 us (level)
  waiting for transfers between devices: 5.43 us -> 1.37 us
  Pallas kernels: 164 us -> 168 us
    ppermute x1, waiting for transfers between devices: 4.31 us -> 0.01 us  [per_device(): lax.ppermute(near, 'cp', to_near)]
    pallas_call x1, Pallas kernels: 141 us -> 144 us  [per_device(): pl.pallas_call(functools.partial(attention_kernel, n_dev, n_heads), name=...]
  transfers between devices with their start and end apart: 2 -> 2, of which waited for: 2 -> 1; matrix products, arithmetic and copies ran while one was open for 0% -> 0% of each run, Pallas kernels for 13% -> 14%
where the time goes in v7:
time: 174 us
  Pallas kernels  168 us (97%)
  starting transfers between devices  2.62 us (2%)
  other arithmetic  1.75 us (1%)
    pallas_call x1, Pallas kernels, per_device(): pl.pallas_call(functools.partial(attention_kernel, n_dev, n_heads), name=...  144 us
    pallas_call x1, Pallas kernels, per_device(): pl.pallas_call(copy_kernel, name='results', out_shape=[jax.ShapeDtypeStru...  23.9 us
  transfers between devices with their start and end apart: 2, of which 1 were waited for; matrix products, arithmetic and copies ran while one was open for 0% of the time, Pallas kernels for 14%

profile of v7, /device:TPU:113, one launch (start us, length us, event | category | flops | bytes accessed | tf_op | source)
XLA Modules:
  0.0 174.1 jit_solution(11009570435996580128)
XLA Ops:
  0.6 143.7 %attention.1 = (bf16[32,1024,256]{2,1,0:T(8,128)(2,1)}, bf16[32,1024,256]{2,1,0:T(8,128)(2,1)}, bf16[24,64,256]{2,1,0:T(8,128)(2,1)}, bf16[24,64,256]{2,1,0:T(8,...) custom-call(bf16[32,1024,256]{2,1,0:T(8,128)(2,1)} %bitcast.14, ...), custom_call_target="tpu_custom_call" | custom-call | tf_op jit(solution)/shard_map/attention/pallas_call | solution.py:408
  144.4 1.3 collective-permute-start
  145.7 1.3 collective-permute-start.1
  147.0 0.0 copy-start
  147.0 0.0 copy-start.1
  147.0 0.0 copy-start.2
  147.0 23.9 %results.1 = (bf16[32,1024,256]{2,1,0:T(8,128)(2,1)}, bf16[32,1024,256]{2,1,0:T(8,128)(2,1)}) custom-call(bf16[32,1024,256]{2,1,0:T(8,128)(2,1)} %get-tuple-element.13.a_ref, bf16[32,1024,256]{2,1,0:T(8,128)(2,1)} %get-tuple-element.14.b_ref), custom_call_target="tpu_custom_call" | custom-call | flops 12000000000 | bytes 67108864 | tf_op jit(solution)/shard_map/results/pallas_call | solution.py:442
  170.9 0.0 collective-permute-done
  170.9 1.4 collective-permute-done.1
  172.3 0.0 copy-done
  172.3 0.2 add_add_fusion
  172.6 0.0 copy-done.1
  172.6 0.0 copy-done.2
  172.6 1.5 maximum_bitcast_fusion
  (2 shorter events, 0.1 us)
Async XLA Ops:
  144.4 26.6 %collective-permute-start = (f32[8,128,256]{2,1,0:T(8,128)}, f32[8,128,256]{2,1,0:T(8,128)S(1)}, u32[]{:S(2)}, u32[]{:S(2)}) collective-permute-start(f32[8,128,256]{2,1,0:T(8,128)} %get-tuple-element.19), channel_id=1, source_target_pairs={{2,0},{3,1},{4,2},{5,3},{6,4},{7,5},{10,8},{11,9},{12,10},{13,11},... | collective-permute-start | bytes 3145736 | tf_op jit(solution)/shard_map/ppermute | solution.py:455
  145.7 26.6 %collective-permute-start.1 = (f32[8,128,256]{2,1,0:T(8,128)}, f32[8,128,256]{2,1,0:T(8,128)S(1)}, u32[]{:S(2)}, u32[]{:S(2)}) collective-permute-start(f32[8,128,256]{2,1,0:T(8,128)} %get-tuple-element.20), channel_id=1, source_target_pairs={{6,0},{7,1},{14,8},{15,9}} | collective-permute-start | bytes 3145736 | tf_op jit(solution)/shard_map/ppermute | solution.py:455
  147.0 25.3 %copy-start = (f32[8,128,256]{2,1,0:T(8,128)S(1)}, f32[8,128,256]{2,1,0:T(8,128)}, u32[]{:S(2)}) copy-start(f32[8,128,256]{2,1,0:T(8,128)} %get-tuple-element.18) | copy-start | bytes 3145732
  147.0 25.6 %copy-start.1 = (bf16[24,64,256]{2,1,0:T(8,128)(2,1)S(1)}, bf16[24,64,256]{2,1,0:T(8,128)(2,1)}, u32[]{:S(2)}) copy-start(bf16[24,64,256]{2,1,0:T(8,128)(2,1)} %get-tuple-element.17) | copy-start | bytes 2359300
  147.0 25.6 %copy-start.2 = (bf16[24,64,256]{2,1,0:T(8,128)(2,1)S(1)}, bf16[24,64,256]{2,1,0:T(8,128)(2,1)}, u32[]{:S(2)}) copy-start(bf16[24,64,256]{2,1,0:T(8,128)(2,1)} %get-tuple-element.21) | copy-start | bytes 2359300

commit v8 on v7

--- a/solution.py
+++ b/solution.py
@@ -14,17 +14,19 @@
 NPRX = 4
 N_COPY = 16
 N_FIRST = 1
+N_TURN = 3
 N_LATE = 8
 
 
-HOPS = ((2, 1, 3, 0), (1, 0, 2, None), (2, 2, 3, None), (1, 1, 0, 1), (1, 1, 2, None), (0, 0, 3, None), (0, 0, 1, None), (0, 1, 3, 1))
-PUSH = {0: (1, 6), 1: (2, 12), 2: (3, 4), 3: (2, 5)}
-TAKE = {0: (0, 10), 1: (3, 6), 2: (2, 2), 3: (0, 1)}
+HOPS = ((1, 1, 2, None), (1, 0, 2, None), (2, 1, 3, 0), (2, 2, 3, None), (0, 1, 3, 1), (1, 1, 0, 1), (0, 0, 3, None), (0, 0, 1, None))
+PUSH = {0: (0, 8), 1: (2, 12), 2: (3, 3), 3: (2, 5)}
+TAKE = {0: (0, 10), 1: (2, 6), 2: (2, 2), 3: (0, 1)}
 SENDS = {(3, 0): ((1, 2, 0, False, None), (0, 0, 1, False, 1), (2, 2, 1, False, 0)), (3, 1): ((2, 2, 0, False, 0), (0, 0, 0, True, 1), (1, 0, 2, False, None)), (2, 0): ((1, 1, 1, True, 0), (0, 1, 0, False, None)), (2, 1): ((1, 1, 0, False, 0), (0, 3, 0, False, None)), (1, 0): ((0, 0, 0, True, 0),), (1, 1): ((0, 0, 1, False, 0),)}
-RELAY = {(3, 1): (3, 0), (2, 0): (6, 0), (1, 0): (8, 0), (0, 1): (6, 2)}
-FINISH = {(3, 0): (1, ()), (3, 1): (1, ()), (2, 0): (9, (1,)), (2, 1): (5, (0,)), (1, 0): (10, (1,)), (1, 1): (10, (0, 1)), (0, 0): (10, (0, 1)), (0, 1): (9, (0, 1))}
+RELAY = {(3, 1): (3, 0), (2, 0): (8, 0), (1, 0): (8, 0), (0, 1): (7, 2)}
+FINISH = {(3, 0): (1, ()), (3, 1): (1, ()), (2, 0): (7, (1,)), (2, 1): (5, (0,)), (1, 0): (10, (1,)), (1, 1): (10, (0, 1)), (0, 0): (10, (0, 1)), (0, 1): (9, (0, 1))}
 LAG_MAX = 10
 FINISH_LATE = {(1, 1): (1,)}
+TURNED, TURN, TURN_LAG = (3, 1, 1), (2, 1), 4
 
 
 def attention_kernel(n_dev, n_heads, *refs):
@@ -89,6 +91,7 @@
         n_key = two * (c + 1)
         here = pl.ds(0, c + 1)
         first_late = n_seq - N_LATE
+        first_turn = n_seq - N_TURN
 
         def doc_copy(to):
             return remote(docs.at[me], docs.at[me], doc_tx, doc_rx, to)
@@ -224,10 +227,13 @@
             unit = acc.at[b % NACC, a]
             sem = tx_sem.at[b % NACC]
 
-            def now():
+            def now(to=to, buf=buf):
                 remote(unit, rx[buf].at[b], sem, rx_sem.at[buf, b], dev(to)).start()
 
-            if late is None:
+            if (c, e, a) == TURNED:
+                pl.when(b < first_turn)(now)
+                pl.when(b >= first_turn)(lambda: now(*TURN))
+            elif late is None:
                 now()
             else:
                 pl.when(b < first_late)(now)
@@ -248,18 +254,34 @@
                     @pl.when(core == e)
                     def _():
                         for i in sends:
-                            unit_send(b, e, i)
+                            if (c, e, SENDS[c, e][i][0]) == (TURN[0], TURNED[1], TURNED[2]):
+                                pl.when(b < first_turn)(lambda: unit_send(b, e, i))
+                            else:
+                                unit_send(b, e, i)
 
         def relay(b, e):
             buf = RELAY[c, e][1]
-            got(buf, b)
+
+            def take_in():
+                got(buf, b)
+                if c == 0:
+                    fwd_copy(b).start()
+                    return
+                for i, (a, _, _, after, _) in enumerate(SENDS[c, e]):
+                    if after:
+                        acc[b % NACC, a] = acc[b % NACC, a] + rx[buf][b]
+                        unit_send(b, e, i)
+
             if c == 0:
-                fwd_copy(b).start()
-                return
-            for i, (a, _, _, after, _) in enumerate(SENDS[c, e]):
-                if after:
-                    acc[b % NACC, a] = acc[b % NACC, a] + rx[buf][b]
-                    unit_send(b, e, i)
+                pl.when(b < first_turn)(take_in)
+            else:
+                take_in()
+
+        def add_turned(b):
+            got(TURN[1], b)
+            a = TURNED[2]
+            acc[b % NACC, a] = acc[b % NACC, a] + rx[TURN[1]][b]
+            unit_send(b, TURNED[1], [s[0] for s in SENDS[c, TURNED[1]]].index(a))
 
         def fwd_copy(b):
             return remote(rx2.at[b], rx1.at[b], fwd_tx, rx_sem.at[1, b], dev(1))
@@ -278,9 +300,13 @@
                 fin_k[b] = (out[0:piece] * scale).astype(jnp.bfloat16)
                 fin_v[b] = out[piece:two].astype(jnp.bfloat16)
 
-            @pl.when(b >= first_late)
+            @pl.when((b >= first_late) & (b < first_turn))
             def _():
                 own[b - first_late] = total(FINISH_LATE.get((c, e), ()))
+
+            @pl.when(b >= first_turn)
+            def _():
+                own[b - first_late] = total(())
 
         n_step = n_seq + LAG_MAX
 
@@ -321,6 +347,9 @@
                 def _():
                     if (c, e) in RELAY:
                         when_seq(t - RELAY[c, e][0], lambda b: relay(b, e))
+                    if (c, e) == (TURN[0], TURNED[1]):
+                        b_turn = t - TURN_LAG
+                        pl.when((b_turn >= first_turn) & (b_turn < n_seq))(lambda: add_turned(b_turn))
                     when_seq(t - FINISH[c, e][0], lambda b: finish(b, e))
             return carry
 
@@ -338,7 +367,7 @@
         for to in doc_dests:
             doc_copy(to).wait_send()
         if c == 0:
-            pl.when(core == 1)(lambda: local_wait(rx2, fwd_tx))
+            pl.when(core == 1)(lambda: local_wait(rx2.at[pl.ds(0, first_turn)], fwd_tx))
 
     for c in range(n_chip):
         pl.when(chip == c)(functools.partial(run_chip, c))

time: 174 us -> 174 us (level)
  the two profiles are of different devices: /device:TPU:113 before, /device:TPU:118 now
where the time goes in v8:
time: 174 us
  Pallas kernels  165 us (95%)
  starting transfers between devices  6.54 us (4%)
  other arithmetic  1.75 us (1%)
    pallas_call x1, Pallas kernels, per_device(): pl.pallas_call(functools.partial(attention_kernel, n_dev, n_heads), name=...  141 us
    pallas_call x1, Pallas kernels, per_device(): pl.pallas_call(copy_kernel, name='results', out_shape=[jax.ShapeDtypeStru...  23.9 us
    ppermute x1, starting transfers between devices, per_device(): lax.ppermute(near, 'cp', to_near)  5.17 us
  transfers between devices with their start and end apart: 2, of which 0 were waited for; matrix products, arithmetic and copies ran while one was open for 0% of the time, Pallas kernels for 14%

profile of v8, /device:TPU:118, one launch (start us, length us, event | category | flops | bytes accessed | tf_op | source)
XLA Modules:
  0.0 174.0 jit_solution(2479567129780378756)
XLA Ops:
  0.6 141.0 %attention.1 = (bf16[32,1024,256]{2,1,0:T(8,128)(2,1)}, bf16[32,1024,256]{2,1,0:T(8,128)(2,1)}, bf16[24,64,256]{2,1,0:T(8,128)(2,1)}, bf16[24,64,256]{2,1,0:T(8,...) custom-call(bf16[32,1024,256]{2,1,0:T(8,128)(2,1)} %bitcast.14, ...), custom_call_target="tpu_custom_call" | custom-call | tf_op jit(solution)/shard_map/attention/pallas_call | solution.py:437
  141.7 5.2 %collective-permute-start = (f32[8,128,256]{2,1,0:T(8,128)}, f32[8,128,256]{2,1,0:T(8,128)S(1)}, u32[]{:S(2)}, u32[]{:S(2)}) collective-permute-start(f32[8,128,256]{2,1,0:T(8,128)} %get-tuple-element.19), channel_id=1, source_target_pairs={{2,0},{3,1},{4,2},{5,3},{6,4},{7,5},{10,8},{11,9},{12,10},{13,11},... | collective-permute-start | bytes 3145736 | tf_op jit(solution)/shard_map/ppermute | solution.py:484
  146.8 1.4 collective-permute-start.1
  148.2 0.0 copy-start
  148.2 0.0 copy-start.1
  148.2 0.0 copy-start.2
  148.2 23.9 %results.1 = (bf16[32,1024,256]{2,1,0:T(8,128)(2,1)}, bf16[32,1024,256]{2,1,0:T(8,128)(2,1)}) custom-call(bf16[32,1024,256]{2,1,0:T(8,128)(2,1)} %get-tuple-element.13.a_ref, bf16[32,1024,256]{2,1,0:T(8,128)(2,1)} %get-tuple-element.14.b_ref), custom_call_target="tpu_custom_call" | custom-call | flops 12000000000 | bytes 67108864 | tf_op jit(solution)/shard_map/results/pallas_call | solution.py:471
  172.2 0.0 collective-permute-done
  172.2 0.0 collective-permute-done.1
  172.2 0.0 copy-done
  172.2 0.2 add_add_fusion
  172.5 0.0 copy-done.1
  172.5 0.0 copy-done.2
  172.5 1.5 maximum_bitcast_fusion
  (2 shorter events, 0.1 us)
Async XLA Ops:
  141.7 30.5 %collective-permute-start = (f32[8,128,256]{2,1,0:T(8,128)}, f32[8,128,256]{2,1,0:T(8,128)S(1)}, u32[]{:S(2)}, u32[]{:S(2)}) collective-permute-start(f32[8,128,256]{2,1,0:T(8,128)} %get-tuple-element.19), channel_id=1, source_target_pairs={{2,0},{3,1},{4,2},{5,3},{6,4},{7,5},{10,8},{11,9},{12,10},{13,11},... | collective-permute-start | bytes 3145736 | tf_op jit(solution)/shard_map/ppermute | solution.py:484
  146.8 25.3 %collective-permute-start.1 = (f32[8,128,256]{2,1,0:T(8,128)}, f32[8,128,256]{2,1,0:T(8,128)S(1)}, u32[]{:S(2)}, u32[]{:S(2)}) collective-permute-start(f32[8,128,256]{2,1,0:T(8,128)} %get-tuple-element.20), channel_id=1, source_target_pairs={{6,0},{7,1},{14,8},{15,9}} | collective-permute-start | bytes 3145736 | tf_op jit(solution)/shard_map/ppermute | solution.py:484
  148.2 24.0 %copy-start = (f32[8,128,256]{2,1,0:T(8,128)S(1)}, f32[8,128,256]{2,1,0:T(8,128)}, u32[]{:S(2)}) copy-start(f32[8,128,256]{2,1,0:T(8,128)} %get-tuple-element.18) | copy-start | bytes 3145732
  148.2 24.3 %copy-start.1 = (bf16[24,64,256]{2,1,0:T(8,128)(2,1)S(1)}, bf16[24,64,256]{2,1,0:T(8,128)(2,1)}, u32[]{:S(2)}) copy-start(bf16[24,64,256]{2,1,0:T(8,128)(2,1)} %get-tuple-element.17) | copy-start | bytes 2359300
  148.2 24.3 %copy-start.2 = (bf16[24,64,256]{2,1,0:T(8,128)(2,1)S(1)}, bf16[24,64,256]{2,1,0:T(8,128)(2,1)}, u32[]{:S(2)}) copy-start(bf16[24,64,256]{2,1,0:T(8,128)(2,1)} %get-tuple-element.21) | copy-start | bytes 2359300

commit v9 on v8

--- a/solution.py
+++ b/solution.py
@@ -12,7 +12,8 @@
 HIDDEN = -3.0e38
 NACC = 12
 NPRX = 4
-N_COPY = 16
+COPY_BLOCK = 2
+N_COPY = 32
 N_FIRST = 1
 N_TURN = 3
 N_LATE = 8
@@ -384,37 +385,29 @@
 
 
 def copy_kernel(a_ref, b_ref, a_out, b_out, buf, in_sem, out_sem):
-    n_seq = a_ref.shape[0]
-    n_buf = buf.shape[0]
+    n_buf, n_block = buf.shape[:2]
+    total = 2 * a_ref.shape[0] // n_block
     ahead = n_buf // 2
 
-    def pick(i, fn):
-        fn(a_ref, a_out, i // 2) if i % 2 == 0 else fn(b_ref, b_out, i // 2)
-
     def read(i):
-        pick(i, lambda src, dst, j: pltpu.make_async_copy(src.at[j], buf.at[i % n_buf], in_sem.at[i % n_buf]).start())
-
-    def read_done(i):
-        pick(i, lambda src, dst, j: pltpu.make_async_copy(src.at[j], buf.at[i % n_buf], in_sem.at[i % n_buf]).wait())
+        src = (a_ref, b_ref)[i % 2].at[pl.ds(i // 2 * n_block, n_block)]
+        return pltpu.make_async_copy(src, buf.at[i % n_buf], in_sem.at[i % n_buf])
 
     def write(i):
-        pick(i, lambda src, dst, j: pltpu.make_async_copy(buf.at[i % n_buf], dst.at[j], out_sem.at[i % n_buf]).start())
-
-    def write_done(i):
-        pick(i, lambda src, dst, j: pltpu.make_async_copy(buf.at[i % n_buf], dst.at[j], out_sem.at[i % n_buf]).wait())
-
-    total = 2 * n_seq
+        dst = (a_out, b_out)[i % 2].at[pl.ds(i // 2 * n_block, n_block)]
+        return pltpu.make_async_copy(buf.at[i % n_buf], dst, out_sem.at[i % n_buf])
+
     for i in range(ahead):
-        read(i)
+        read(i).start()
     for i in range(total):
         if i + ahead < total:
-            if i + ahead - n_buf >= 0:
-                write_done(i + ahead - n_buf)
-            read(i + ahead)
-        read_done(i)
-        write(i)
-    for i in range(total - n_buf, total):
-        write_done(i)
+            if i + ahead >= n_buf:
+                write(i + ahead - n_buf).wait()
+            read(i + ahead).start()
+        read(i).wait()
+        write(i).start()
+    for i in range(max(total - n_buf, 0), total):
+        write(i).wait()
 
 
 def solution(mesh):
@@ -474,8 +467,8 @@
             out_shape=[jax.ShapeDtypeStruct(rows_shape, bf16)] * 2,
             in_specs=[any_spec] * 2,
             out_specs=[any_spec] * 2,
-            scratch_shapes=[pltpu.VMEM((N_COPY, n_rows, head_dim), bf16), dma((N_COPY,)), dma((N_COPY,))],
-            compiler_params=pltpu.CompilerParams(vmem_limit_bytes=48 * 1024 * 1024),
+            scratch_shapes=[pltpu.VMEM((N_COPY, COPY_BLOCK, n_rows, head_dim), bf16), dma((N_COPY,)), dma((N_COPY,))],
+            compiler_params=pltpu.CompilerParams(vmem_limit_bytes=52 * 1024 * 1024),
             cost_estimate=pl.CostEstimate(flops=12_000_000_000, bytes_accessed=8 * n_seq * n_rows * head_dim,
                                           transcendentals=0),
         )(attn_out, grad_query)

time: 174 us -> 174 us (level)
  no operation moved by 1% of the time
where the time goes in v9:
time: 174 us
  Pallas kernels  165 us (95%)
  starting transfers between devices  6.54 us (4%)
  other arithmetic  1.75 us (1%)
    pallas_call x1, Pallas kernels, per_device(): pl.pallas_call(functools.partial(attention_kernel, n_dev, n_heads), name=...  141 us
    pallas_call x1, Pallas kernels, per_device(): pl.pallas_call(copy_kernel, name='results', out_shape=[jax.ShapeDtypeStru...  23.6 us
    ppermute x1, starting transfers between devices, per_device(): lax.ppermute(near, 'cp', to_near)  5.17 us
  transfers between devices with their start and end apart: 2, of which 0 were waited for; matrix products, arithmetic and copies ran while one was open for 0% of the time, Pallas kernels for 14%

profile of v9, /device:TPU:118, one launch (start us, length us, event | category | flops | bytes accessed | tf_op | source)
XLA Modules:
  0.0 173.8 jit_solution(4656414730056721058)
XLA Ops:
  0.6 141.0 %attention.1 = (bf16[32,1024,256]{2,1,0:T(8,128)(2,1)}, bf16[32,1024,256]{2,1,0:T(8,128)(2,1)}, bf16[24,64,256]{2,1,0:T(8,128)(2,1)}, bf16[24,64,256]{2,1,0:T(8,...) custom-call(bf16[32,1024,256]{2,1,0:T(8,128)(2,1)} %bitcast.14, ...), custom_call_target="tpu_custom_call" | custom-call | tf_op jit(solution)/shard_map/attention/pallas_call | solution.py:430
  141.7 5.2 %collective-permute-start = (f32[8,128,256]{2,1,0:T(8,128)}, f32[8,128,256]{2,1,0:T(8,128)S(1)}, u32[]{:S(2)}, u32[]{:S(2)}) collective-permute-start(f32[8,128,256]{2,1,0:T(8,128)} %get-tuple-element.19), channel_id=1, source_target_pairs={{2,0},{3,1},{4,2},{5,3},{6,4},{7,5},{10,8},{11,9},{12,10},{13,11},... | collective-permute-start | bytes 3145736 | tf_op jit(solution)/shard_map/ppermute | solution.py:477
  146.8 1.4 collective-permute-start.1
  148.2 0.0 copy-start
  148.2 0.0 copy-start.1
  148.2 0.0 copy-start.2
  148.2 23.6 %results.1 = (bf16[32,1024,256]{2,1,0:T(8,128)(2,1)}, bf16[32,1024,256]{2,1,0:T(8,128)(2,1)}) custom-call(bf16[32,1024,256]{2,1,0:T(8,128)(2,1)} %get-tuple-element.13.a_ref, bf16[32,1024,256]{2,1,0:T(8,128)(2,1)} %get-tuple-element.14.b_ref), custom_call_target="tpu_custom_call" | custom-call | flops 12000000000 | bytes 67108864 | tf_op jit(solution)/shard_map/results/pallas_call | solution.py:464
  171.9 0.0 collective-permute-done
  171.9 0.0 collective-permute-done.1
  171.9 0.0 copy-done
  171.9 0.2 add_add_fusion
  172.2 0.0 copy-done.1
  172.2 0.0 copy-done.2
  172.3 1.5 maximum_bitcast_fusion
  (2 shorter events, 0.1 us)
Async XLA Ops:
  141.7 30.2 %collective-permute-start = (f32[8,128,256]{2,1,0:T(8,128)}, f32[8,128,256]{2,1,0:T(8,128)S(1)}, u32[]{:S(2)}, u32[]{:S(2)}) collective-permute-start(f32[8,128,256]{2,1,0:T(8,128)} %get-tuple-element.19), channel_id=1, source_target_pairs={{2,0},{3,1},{4,2},{5,3},{6,4},{7,5},{10,8},{11,9},{12,10},{13,11},... | collective-permute-start | bytes 3145736 | tf_op jit(solution)/shard_map/ppermute | solution.py:477
  146.8 25.1 %collective-permute-start.1 = (f32[8,128,256]{2,1,0:T(8,128)}, f32[8,128,256]{2,1,0:T(8,128)S(1)}, u32[]{:S(2)}, u32[]{:S(2)}) collective-permute-start(f32[8,128,256]{2,1,0:T(8,128)} %get-tuple-element.20), channel_id=1, source_target_pairs={{6,0},{7,1},{14,8},{15,9}} | collective-permute-start | bytes 3145736 | tf_op jit(solution)/shard_map/ppermute | solution.py:477
  148.2 23.7 %copy-start = (f32[8,128,256]{2,1,0:T(8,128)S(1)}, f32[8,128,256]{2,1,0:T(8,128)}, u32[]{:S(2)}) copy-start(f32[8,128,256]{2,1,0:T(8,128)} %get-tuple-element.18) | copy-start | bytes 3145732
  148.2 24.0 %copy-start.1 = (bf16[24,64,256]{2,1,0:T(8,128)(2,1)S(1)}, bf16[24,64,256]{2,1,0:T(8,128)(2,1)}, u32[]{:S(2)}) copy-start(bf16[24,64,256]{2,1,0:T(8,128)(2,1)} %get-tuple-element.17) | copy-start | bytes 2359300
  148.2 24.0 %copy-start.2 = (bf16[24,64,256]{2,1,0:T(8,128)(2,1)S(1)}, bf16[24,64,256]{2,1,0:T(8,128)(2,1)}, u32[]{:S(2)}) copy-start(bf16[24,64,256]{2,1,0:T(8,128)(2,1)} %get-tuple-element.21) | copy-start | bytes 2359300

commit v10 on v9

--- a/solution.py
+++ b/solution.py
@@ -16,7 +16,7 @@
 N_COPY = 32
 N_FIRST = 1
 N_TURN = 3
-N_LATE = 8
+N_LATE = 9
 
 
 HOPS = ((1, 1, 2, None), (1, 0, 2, None), (2, 1, 3, 0), (2, 2, 3, None), (0, 1, 3, 1), (1, 1, 0, 1), (0, 0, 3, None), (0, 0, 1, None))

time: 174 us -> 176 us (1.011)
  the two profiles are of different devices: /device:TPU:118 before, /device:TPU:113 now
where the time goes in v10:
time: 176 us; the launch traced here: 173 us
  Pallas kernels  161 us (91%)
  waiting for transfers between devices  5.17 us (3%)
  starting transfers between devices  2.62 us (1%)
  other arithmetic  1.78 us (1%)
    pallas_call x1, Pallas kernels, per_device(): pl.pallas_call(functools.partial(attention_kernel, n_dev, n_heads), name=...  138 us
    pallas_call x1, Pallas kernels, per_device(): pl.pallas_call(copy_kernel, name='results', out_shape=[jax.ShapeDtypeStru...  23.6 us
    ppermute x1, waiting for transfers between devices, per_device(): lax.ppermute(near, 'cp', to_near)  3.55 us
  transfers between devices with their start and end apart: 2, of which 2 were waited for; matrix products, arithmetic and copies ran while one was open for 0% of the time, Pallas kernels for 14%

profile of v10, /device:TPU:113, one launch (start us, length us, event | category | flops | bytes accessed | tf_op | source)
XLA Modules:
  0.0 172.6 jit_solution(284043579616833145)
XLA Ops:
  0.6 137.6 %attention.1 = (bf16[32,1024,256]{2,1,0:T(8,128)(2,1)}, bf16[32,1024,256]{2,1,0:T(8,128)(2,1)}, bf16[23,64,256]{2,1,0:T(8,128)(2,1)}, bf16[23,64,256]{2,1,0:T(8,...) custom-call(bf16[32,1024,256]{2,1,0:T(8,128)(2,1)} %bitcast.14, ...), custom_call_target="tpu_custom_call" | custom-call | tf_op jit(solution)/shard_map/attention/pallas_call | solution.py:430
  138.3 1.3 collective-permute-start
  139.6 1.3 collective-permute-start.1
  140.9 0.0 copy-start
  140.9 23.6 %results.1 = (bf16[32,1024,256]{2,1,0:T(8,128)(2,1)}, bf16[32,1024,256]{2,1,0:T(8,128)(2,1)}) custom-call(bf16[32,1024,256]{2,1,0:T(8,128)(2,1)} %get-tuple-element.13.a_ref, bf16[32,1024,256]{2,1,0:T(8,128)(2,1)} %get-tuple-element.14.b_ref), custom_call_target="tpu_custom_call" | custom-call | flops 12000000000 | bytes 67108864 | tf_op jit(solution)/shard_map/results/pallas_call | solution.py:464
  164.5 3.6 %collective-permute-done = f32[9,128,256]{2,1,0:T(8,128)S(1)} collective-permute-done((f32[9,128,256]{2,1,0:T(8,128)}, f32[9,128,256]{2,1,0:T(8,128)S(1)}, u32[]{:S(2)}, u32[]{:S(2)}) %collective-permute-start) | collective-permute-done | bytes 1179680 | tf_op jit(solution)/shard_map/ppermute | solution.py:477
  168.1 1.6 collective-permute-done.1
  169.7 0.0 copy-done
  169.7 0.0 copy-start.2
  169.7 0.2 add_add_fusion
  169.9 0.0 copy-start.1
  169.9 0.1 fusion
  170.0 0.8 copy-done.2
  170.8 0.3 copy-done.1
  171.1 1.5 maximum_bitcast_fusion
  (1 shorter events, 0.0 us)
Async XLA Ops:
  138.3 29.8 %collective-permute-start = (f32[9,128,256]{2,1,0:T(8,128)}, f32[9,128,256]{2,1,0:T(8,128)S(1)}, u32[]{:S(2)}, u32[]{:S(2)}) collective-permute-start(f32[9,128,256]{2,1,0:T(8,128)} %get-tuple-element.19), channel_id=1, source_target_pairs={{2,0},{3,1},{4,2},{5,3},{6,4},{7,5},{10,8},{11,9},{12,10},{13,11},... | collective-permute-start | bytes 3538952 | tf_op jit(solution)/shard_map/ppermute | solution.py:477
  139.6 30.1 %collective-permute-start.1 = (f32[9,128,256]{2,1,0:T(8,128)}, f32[9,128,256]{2,1,0:T(8,128)S(1)}, u32[]{:S(2)}, u32[]{:S(2)}) collective-permute-start(f32[9,128,256]{2,1,0:T(8,128)} %get-tuple-element.20), channel_id=1, source_target_pairs={{6,0},{7,1},{14,8},{15,9}} | collective-permute-start | bytes 3538952 | tf_op jit(solution)/shard_map/ppermute | solution.py:477
  140.9 28.8 %copy-start = (f32[9,128,256]{2,1,0:T(8,128)S(1)}, f32[9,128,256]{2,1,0:T(8,128)}, u32[]{:S(2)}) copy-start(f32[9,128,256]{2,1,0:T(8,128)} %get-tuple-element.18) | copy-start | bytes 3538948
  169.7 1.1 copy-start.2
  169.9 1.2 copy-start.1

commit v11 on v10

--- a/solution.py
+++ b/solution.py
@@ -474,7 +474,9 @@
         )(attn_out, grad_query)
         to_near = [(d, d - 2) for d in range(2, n_dev)]
         to_far = [(n_dev - 2 + e, e) for e in range(2)]
-        late = own + lax.ppermute(near, 'cp', to_near) + lax.ppermute(far, 'cp', to_far)
+        from_far = lax.ppermute(far, 'cp', to_far)
+        from_near = lax.ppermute(near, 'cp', to_near)
+        late = own + from_far + from_near
         late_keys = (late[:, 0:piece] * head_dim ** -0.5).astype(bf16)
         late_values = late[:, piece:two].astype(bf16)
         grad_keys = jnp.concatenate([grad_keys, late_keys])

time: 176 us -> 173 us (0.983); the launches traced: 173 us -> 172 us
  no operation moved by 1% of the time
where the time goes in v11:
time: 173 us; the launch traced here: 172 us
  Pallas kernels  161 us (93%)
  waiting for transfers between devices  4.3 us (2%)
  starting transfers between devices  2.62 us (2%)
  other arithmetic  1.78 us (1%)
    pallas_call x1, Pallas kernels, per_device(): pl.pallas_call(functools.partial(attention_kernel, n_dev, n_heads), name=...  138 us
    pallas_call x1, Pallas kernels, per_device(): pl.pallas_call(copy_kernel, name='results', out_shape=[jax.ShapeDtypeStru...  23.6 us
  transfers between devices with their start and end apart: 2, of which 2 were waited for; matrix products, arithmetic and copies ran while one was open for 0% of the time, Pallas kernels for 14%

profile of v11, /device:TPU:113, one launch (start us, length us, event | category | flops | bytes accessed | tf_op | source)
XLA Modules:
  0.0 171.7 jit_solution(8917127806382619400)
XLA Ops:
  0.6 137.6 %attention.1 = (bf16[32,1024,256]{2,1,0:T(8,128)(2,1)}, bf16[32,1024,256]{2,1,0:T(8,128)(2,1)}, bf16[23,64,256]{2,1,0:T(8,128)(2,1)}, bf16[23,64,256]{2,1,0:T(8,...) custom-call(bf16[32,1024,256]{2,1,0:T(8,128)(2,1)} %bitcast.14, ...), custom_call_target="tpu_custom_call" | custom-call | tf_op jit(solution)/shard_map/attention/pallas_call | solution.py:430
  138.3 1.3 collective-permute-start
  139.6 1.3 collective-permute-start.1
  140.9 0.0 copy-start
  140.9 23.6 %results.1 = (bf16[32,1024,256]{2,1,0:T(8,128)(2,1)}, bf16[32,1024,256]{2,1,0:T(8,128)(2,1)}) custom-call(bf16[32,1024,256]{2,1,0:T(8,128)(2,1)} %get-tuple-element.13.a_ref, bf16[32,1024,256]{2,1,0:T(8,128)(2,1)} %get-tuple-element.14.b_ref), custom_call_target="tpu_custom_call" | custom-call | flops 12000000000 | bytes 67108864 | tf_op jit(solution)/shard_map/results/pallas_call | solution.py:464
  164.5 3.0 %collective-permute-done = f32[9,128,256]{2,1,0:T(8,128)S(1)} collective-permute-done((f32[9,128,256]{2,1,0:T(8,128)}, f32[9,128,256]{2,1,0:T(8,128)S(1)}, u32[]{:S(2)}, u32[]{:S(2)}) %collective-permute-start) | collective-permute-done | bytes 1179680 | tf_op jit(solution)/shard_map/ppermute | solution.py:477
  167.5 1.3 collective-permute-done.1
  168.8 0.0 copy-done
  168.8 0.0 copy-start.2
  168.8 0.2 add_add_fusion
  169.1 0.0 copy-start.1
  169.1 0.1 fusion
  169.2 0.8 copy-done.2
  169.9 0.3 copy-done.1
  170.2 1.5 maximum_bitcast_fusion
  (1 shorter events, 0.0 us)
Async XLA Ops:
  138.3 29.3 %collective-permute-start = (f32[9,128,256]{2,1,0:T(8,128)}, f32[9,128,256]{2,1,0:T(8,128)S(1)}, u32[]{:S(2)}, u32[]{:S(2)}) collective-permute-start(f32[9,128,256]{2,1,0:T(8,128)} %get-tuple-element.19), channel_id=1, source_target_pairs={{6,0},{7,1},{14,8},{15,9}} | collective-permute-start | bytes 3538952 | tf_op jit(solution)/shard_map/ppermute | solution.py:477
  139.6 29.2 %collective-permute-start.1 = (f32[9,128,256]{2,1,0:T(8,128)}, f32[9,128,256]{2,1,0:T(8,128)S(1)}, u32[]{:S(2)}, u32[]{:S(2)}) collective-permute-start(f32[9,128,256]{2,1,0:T(8,128)} %get-tuple-element.20), channel_id=1, source_target_pairs={{2,0},{3,1},{4,2},{5,3},{6,4},{7,5},{10,8},{11,9},{12,10},{13,11},... | collective-permute-start | bytes 3538952 | tf_op jit(solution)/shard_map/ppermute | solution.py:478
  140.9 27.9 %copy-start = (f32[9,128,256]{2,1,0:T(8,128)S(1)}, f32[9,128,256]{2,1,0:T(8,128)}, u32[]{:S(2)}) copy-start(f32[9,128,256]{2,1,0:T(8,128)} %get-tuple-element.18) | copy-start | bytes 3538948
  168.8 1.1 copy-start.2
  169.1 1.2 copy-start.1

commit v12 on v11

--- a/solution.py
+++ b/solution.py
@@ -13,7 +13,7 @@
 NACC = 12
 NPRX = 4
 COPY_BLOCK = 2
-N_COPY = 32
+N_COPY = 28
 N_FIRST = 1
 N_TURN = 3
 N_LATE = 9
@@ -384,7 +384,7 @@
     out_own.wait()
 
 
-def copy_kernel(a_ref, b_ref, a_out, b_out, buf, in_sem, out_sem):
+def copy_kernel(a_ref, b_ref, k_ref, v_ref, a_out, b_out, k_out, v_out, buf, in_sem, out_sem, k_buf, v_buf, kv_sem):
     n_buf, n_block = buf.shape[:2]
     total = 2 * a_ref.shape[0] // n_block
     ahead = n_buf // 2
@@ -397,8 +397,15 @@
         dst = (a_out, b_out)[i % 2].at[pl.ds(i // 2 * n_block, n_block)]
         return pltpu.make_async_copy(buf.at[i % n_buf], dst, out_sem.at[i % n_buf])
 
+    rows = pl.ds(0, k_ref.shape[0])
+    small_in = [pltpu.make_async_copy(k_ref, k_buf, kv_sem.at[0]), pltpu.make_async_copy(v_ref, v_buf, kv_sem.at[1])]
+    small_out = [pltpu.make_async_copy(k_buf, k_out.at[rows], kv_sem.at[0]),
+                 pltpu.make_async_copy(v_buf, v_out.at[rows], kv_sem.at[1])]
+
     for i in range(ahead):
         read(i).start()
+    for copy in small_in:
+        copy.start()
     for i in range(total):
         if i + ahead < total:
             if i + ahead >= n_buf:
@@ -406,8 +413,15 @@
             read(i + ahead).start()
         read(i).wait()
         write(i).start()
+        if i == ahead:
+            for copy in small_in:
+                copy.wait()
+            for copy in small_out:
+                copy.start()
     for i in range(max(total - n_buf, 0), total):
         write(i).wait()
+    for copy in small_out:
+        copy.wait()
 
 
 def solution(mesh):
@@ -461,17 +475,18 @@
             compiler_params=pltpu.CompilerParams(collective_id=0, has_side_effects=True, vmem_limit_bytes=63 * 1024 * 1024),
         )(query.reshape(rows_shape), grad_out.reshape(rows_shape), keys.reshape(kv_shape), values.reshape(kv_shape), doc_id)
         attn_out, grad_query, grad_keys, grad_values, near, far, own = out
-        attn_out, grad_query = pl.pallas_call(
+        attn_out, grad_query, grad_keys, grad_values = pl.pallas_call(
             copy_kernel,
             name='results',
-            out_shape=[jax.ShapeDtypeStruct(rows_shape, bf16)] * 2,
-            in_specs=[any_spec] * 2,
-            out_specs=[any_spec] * 2,
-            scratch_shapes=[pltpu.VMEM((N_COPY, COPY_BLOCK, n_rows, head_dim), bf16), dma((N_COPY,)), dma((N_COPY,))],
-            compiler_params=pltpu.CompilerParams(vmem_limit_bytes=52 * 1024 * 1024),
+            out_shape=[jax.ShapeDtypeStruct(rows_shape, bf16)] * 2 + [jax.ShapeDtypeStruct(kv_shape, bf16)] * 2,
+            in_specs=[pl.BlockSpec(memory_space=pltpu.HBM)] * 4,
+            out_specs=[pl.BlockSpec(memory_space=pltpu.HBM)] * 4,
+            scratch_shapes=[pltpu.VMEM((N_COPY, COPY_BLOCK, n_rows, head_dim), bf16), dma((N_COPY,)), dma((N_COPY,)),
+                            pltpu.VMEM(main_shape, bf16), pltpu.VMEM(main_shape, bf16), dma((2,))],
+            compiler_params=pltpu.CompilerParams(vmem_limit_bytes=40 * 1024 * 1024),
             cost_estimate=pl.CostEstimate(flops=12_000_000_000, bytes_accessed=8 * n_seq * n_rows * head_dim,
                                           transcendentals=0),
-        )(attn_out, grad_query)
+        )(attn_out, grad_query, grad_keys, grad_values)
         to_near = [(d, d - 2) for d in range(2, n_dev)]
         to_far = [(n_dev - 2 + e, e) for e in range(2)]
         from_far = lax.ppermute(far, 'cp', to_far)
@@ -479,8 +494,8 @@
         late = own + from_far + from_near
         late_keys = (late[:, 0:piece] * head_dim ** -0.5).astype(bf16)
         late_values = late[:, piece:two].astype(bf16)
-        grad_keys = jnp.concatenate([grad_keys, late_keys])
-        grad_values = jnp.concatenate([grad_values, late_values])
+        grad_keys = lax.dynamic_update_slice(grad_keys, late_keys, (n_seq - N_LATE, 0, 0))
+        grad_values = lax.dynamic_update_slice(grad_values, late_values, (n_seq - N_LATE, 0, 0))
         return (attn_out.reshape(query.shape), grad_query.reshape(query.shape),
                 grad_keys.reshape(keys.shape), grad_values.reshape(values.shape))
 

time: 173 us -> 172 us (level)
  waiting for transfers between devices: 4.3 us -> 2.09 us
    ppermute x1, waiting for transfers between devices: 3.02 us -> 0.81 us  [per_device(): from_far = lax.ppermute(far, 'cp', to_far)]
where the time goes in v12:
time: 172 us; the launch traced here: 170 us
  Pallas kernels  161 us (94%)
  starting transfers between devices  2.62 us (2%)
  local copies, waits for them, and re-layouts  2.24 us (1%)
  waiting for transfers between devices  2.09 us (1%)
    pallas_call x1, Pallas kernels, per_device(): pl.pallas_call(functools.partial(attention_kernel, n_dev, n_heads), name=...  138 us
    pallas_call x1, Pallas kernels, per_device(): pl.pallas_call(copy_kernel, name='results', out_shape=[jax.ShapeDtypeStru...  23.6 us
  transfers between devices with their start and end apart: 2, of which 2 were waited for; matrix products, arithmetic and copies ran while one was open for 0% of the time, Pallas kernels for 14%

profile of v12, /device:TPU:113, one launch (start us, length us, event | category | flops | bytes accessed | tf_op | source)
XLA Modules:
  0.0 170.0 jit_solution(866749743166612265)
XLA Ops:
  0.6 137.6 %attention.1 = (bf16[32,1024,256]{2,1,0:T(8,128)(2,1)}, bf16[32,1024,256]{2,1,0:T(8,128)(2,1)}, bf16[23,64,256]{2,1,0:T(8,128)(2,1)}, bf16[23,64,256]{2,1,0:T(8,...) custom-call(bf16[32,1024,256]{2,1,0:T(8,128)(2,1)} %bitcast.18, ...), custom_call_target="tpu_custom_call" | custom-call | tf_op jit(solution)/shard_map/attention/pallas_call | solution.py:444
  138.3 1.3 collective-permute-start
  139.6 1.3 collective-permute-start.1
  140.9 0.0 copy-start
  140.9 1.1 copy-done
  142.0 0.0 copy-start.1
  142.0 1.1 copy-done.1
  143.1 0.0 copy-start.2
  143.1 23.6 %results.1 = (bf16[32,1024,256]{2,1,0:T(8,128)(2,1)}, bf16[32,1024,256]{2,1,0:T(8,128)(2,1)}, bf16[32,64,256]{2,1,0:T(8,128)(2,1)}, bf16[32,64,256]{2,1,0:T(8,128)(2,1)}) custom-call(bf16[32,1024,256]{2,1,0:T(8,128)(2,1)} %get-tuple-element.15.a_ref, bf16[32,1024,256]{2,1,0:T(8,128)(2,1)} %get-tuple-element.16.b_ref, bf16[23,64,256]{2,1,0:T(8,128)(2,1)S(1)} %copy-done, ...), custom_call_target="tpu_custom_call" | custom-call | flops 12000000000 | bytes 67108864 | tf_op jit(solution)/shard_map/results/pallas_call | solution.py:478
  166.7 0.8 collective-permute-done
  167.5 1.3 collective-permute-done.1
  168.8 0.0 copy-done.2
  168.8 0.2 add_add_fusion
  169.0 0.9 fusion.4
Async XLA Ops:
  138.3 29.3 %collective-permute-start = (f32[9,128,256]{2,1,0:T(8,128)}, f32[9,128,256]{2,1,0:T(8,128)S(1)}, u32[]{:S(2)}, u32[]{:S(2)}) collective-permute-start(f32[9,128,256]{2,1,0:T(8,128)} %get-tuple-element.23), channel_id=1, source_target_pairs={{6,0},{7,1},{14,8},{15,9}} | collective-permute-start | bytes 3538952 | tf_op jit(solution)/shard_map/ppermute | solution.py:492
  139.6 29.2 %collective-permute-start.1 = (f32[9,128,256]{2,1,0:T(8,128)}, f32[9,128,256]{2,1,0:T(8,128)S(1)}, u32[]{:S(2)}, u32[]{:S(2)}) collective-permute-start(f32[9,128,256]{2,1,0:T(8,128)} %get-tuple-element.24), channel_id=1, source_target_pairs={{2,0},{3,1},{4,2},{5,3},{6,4},{7,5},{10,8},{11,9},{12,10},{13,11},... | collective-permute-start | bytes 3538952 | tf_op jit(solution)/shard_map/ppermute | solution.py:493
  140.9 1.1 copy-start
  142.0 1.1 copy-start.1
  143.1 25.7 %copy-start.2 = (f32[9,128,256]{2,1,0:T(8,128)S(1)}, f32[9,128,256]{2,1,0:T(8,128)}, u32[]{:S(2)}) copy-start(f32[9,128,256]{2,1,0:T(8,128)} %get-tuple-element.22) | copy-start | bytes 3538948

commit v13 on v12

--- a/solution.py
+++ b/solution.py
@@ -13,7 +13,7 @@
 NACC = 12
 NPRX = 4
 COPY_BLOCK = 2
-N_COPY = 28
+N_COPY = 32
 N_FIRST = 1
 N_TURN = 3
 N_LATE = 9
@@ -483,7 +483,7 @@
             out_specs=[pl.BlockSpec(memory_space=pltpu.HBM)] * 4,
             scratch_shapes=[pltpu.VMEM((N_COPY, COPY_BLOCK, n_rows, head_dim), bf16), dma((N_COPY,)), dma((N_COPY,)),
                             pltpu.VMEM(main_shape, bf16), pltpu.VMEM(main_shape, bf16), dma((2,))],
-            compiler_params=pltpu.CompilerParams(vmem_limit_bytes=40 * 1024 * 1024),
+            compiler_params=pltpu.CompilerParams(vmem_limit_bytes=56 * 1024 * 1024),
             cost_estimate=pl.CostEstimate(flops=12_000_000_000, bytes_accessed=8 * n_seq * n_rows * head_dim,
                                           transcendentals=0),
         )(attn_out, grad_query, grad_keys, grad_values)

time: 172 us -> 171 us (level)
  local copies, waits for them, and re-layouts: 2.24 us -> 0.01 us
    unnamed x6 -> x2, local copies, waits for them, and re-layouts: 2.24 us -> 0.01 us
where the time goes in v13:
time: 171 us; the launch traced here: 170 us
  Pallas kernels  162 us (95%)
  waiting for transfers between devices  3.62 us (2%)
  starting transfers between devices  2.62 us (2%)
    pallas_call x1, Pallas kernels, per_device(): pl.pallas_call(functools.partial(attention_kernel, n_dev, n_heads), name=...  138 us
    pallas_call x1, Pallas kernels, per_device(): pl.pallas_call(copy_kernel, name='results', out_shape=[jax.ShapeDtypeStru...  24.3 us
  transfers between devices with their start and end apart: 2, of which 2 were waited for; matrix products, arithmetic and copies ran while one was open for 0% of the time, Pallas kernels for 14%

profile of v13, /device:TPU:113, one launch (start us, length us, event | category | flops | bytes accessed | tf_op | source)
XLA Modules:
  0.0 169.9 jit_solution(9524183944928026392)
XLA Ops:
  0.6 137.6 %attention.1 = (bf16[32,1024,256]{2,1,0:T(8,128)(2,1)}, bf16[32,1024,256]{2,1,0:T(8,128)(2,1)}, bf16[23,64,256]{2,1,0:T(8,128)(2,1)}, bf16[23,64,256]{2,1,0:T(8,...) custom-call(bf16[32,1024,256]{2,1,0:T(8,128)(2,1)} %bitcast.18, ...), custom_call_target="tpu_custom_call" | custom-call | tf_op jit(solution)/shard_map/attention/pallas_call | solution.py:444
  138.3 1.3 collective-permute-start
  139.6 1.3 collective-permute-start.1
  140.9 0.0 copy-start
  140.9 24.3 %results.1 = (bf16[32,1024,256]{2,1,0:T(8,128)(2,1)}, bf16[32,1024,256]{2,1,0:T(8,128)(2,1)}, bf16[32,64,256]{2,1,0:T(8,128)(2,1)}, bf16[32,64,256]{2,1,0:T(8,128)(2,1)}) custom-call(bf16[32,1024,256]{2,1,0:T(8,128)(2,1)} %get-tuple-element.15.a_ref, bf16[32,1024,256]{2,1,0:T(8,128)(2,1)} %get-tuple-element.16.b_ref, ...), custom_call_target="tpu_custom_call" | custom-call | flops 12000000000 | bytes 67108864 | tf_op jit(solution)/shard_map/results/pallas_call | solution.py:478
  165.2 2.4 %collective-permute-done = f32[9,128,256]{2,1,0:T(8,128)S(1)} collective-permute-done((f32[9,128,256]{2,1,0:T(8,128)}, f32[9,128,256]{2,1,0:T(8,128)S(1)}, u32[]{:S(2)}, u32[]{:S(2)}) %collective-permute-start) | collective-permute-done | bytes 1179680 | tf_op jit(solution)/shard_map/ppermute | solution.py:492
  167.5 1.3 collective-permute-done.1
  168.8 0.0 copy-done
  168.8 0.2 add_add_fusion
  169.0 0.9 fusion.4
Async XLA Ops:
  138.3 29.3 %collective-permute-start = (f32[9,128,256]{2,1,0:T(8,128)}, f32[9,128,256]{2,1,0:T(8,128)S(1)}, u32[]{:S(2)}, u32[]{:S(2)}) collective-permute-start(f32[9,128,256]{2,1,0:T(8,128)} %get-tuple-element.23), channel_id=1, source_target_pairs={{6,0},{7,1},{14,8},{15,9}} | collective-permute-start | bytes 3538952 | tf_op jit(solution)/shard_map/ppermute | solution.py:492
  139.6 29.2 %collective-permute-start.1 = (f32[9,128,256]{2,1,0:T(8,128)}, f32[9,128,256]{2,1,0:T(8,128)S(1)}, u32[]{:S(2)}, u32[]{:S(2)}) collective-permute-start(f32[9,128,256]{2,1,0:T(8,128)} %get-tuple-element.24), channel_id=1, source_target_pairs={{2,0},{3,1},{4,2},{5,3},{6,4},{7,5},{10,8},{11,9},{12,10},{13,11},... | collective-permute-start | bytes 3538952 | tf_op jit(solution)/shard_map/ppermute | solution.py:493
  140.9 27.9 %copy-start = (f32[9,128,256]{2,1,0:T(8,128)S(1)}, f32[9,128,256]{2,1,0:T(8,128)}, u32[]{:S(2)}) copy-start(f32[9,128,256]{2,1,0:T(8,128)} %get-tuple-element.22) | copy-start | bytes 3538948

commit v14 on v13

--- a/solution.py
+++ b/solution.py
@@ -15,7 +15,7 @@
 COPY_BLOCK = 2
 N_COPY = 32
 N_FIRST = 1
-N_TURN = 3
+N_TURN = 2
 N_LATE = 9
 
 
@@ -87,6 +87,9 @@
         copy.wait()
     odoc[...] = docs[me].reshape(n_seq, 1, piece)
     pl.semaphore_wait(barrier, n_dev - 1)
+
+    def out_copies():
+        return (pltpu.make_async_copy(fin_k, dk_ref, load_sem.at[0]), pltpu.make_async_copy(fin_v, dv_ref, load_sem.at[1]))
 
     def run_chip(c):
         n_key = two * (c + 1)
@@ -301,6 +304,11 @@
                 fin_k[b] = (out[0:piece] * scale).astype(jnp.bfloat16)
                 fin_v[b] = out[piece:two].astype(jnp.bfloat16)
 
+            @pl.when(b == first_late)
+            def _():
+                for copy in out_copies():
+                    copy.start()
+
             @pl.when((b >= first_late) & (b < first_turn))
             def _():
                 own[b - first_late] = total(FINISH_LATE.get((c, e), ()))
@@ -308,6 +316,11 @@
             @pl.when(b >= first_turn)
             def _():
                 own[b - first_late] = total(())
+
+            @pl.when(b >= first_late)
+            def _():
+                late = b - first_late
+                pltpu.make_async_copy(own.at[late], own_ref.at[late], late_sem).start()
 
         n_step = n_seq + LAG_MAX
 
@@ -373,15 +386,9 @@
     for c in range(n_chip):
         pl.when(chip == c)(functools.partial(run_chip, c))
 
-    out_k = pltpu.make_async_copy(fin_k, dk_ref, load_sem.at[0])
-    out_v = pltpu.make_async_copy(fin_v, dv_ref, load_sem.at[1])
-    out_own = pltpu.make_async_copy(own, own_ref, late_sem)
-    out_k.start()
-    out_v.start()
-    out_own.start()
-    out_k.wait()
-    out_v.wait()
-    out_own.wait()
+    for copy in out_copies():
+        copy.wait()
+    local_wait(own, late_sem)
 
 
 def copy_kernel(a_ref, b_ref, k_ref, v_ref, a_out, b_out, k_out, v_out, buf, in_sem, out_sem, k_buf, v_buf, kv_sem):

time: 171 us -> 170 us (level)
  no operation moved by 1% of the time
where the time goes in v14:
time: 170 us
  Pallas kernels  162 us (95%)
  waiting for transfers between devices  3.65 us (2%)
  starting transfers between devices  2.62 us (2%)
    pallas_call x1, Pallas kernels, per_device(): pl.pallas_call(functools.partial(attention_kernel, n_dev, n_heads), name=...  137 us
    pallas_call x1, Pallas kernels, per_device(): pl.pallas_call(copy_kernel, name='results', out_shape=[jax.ShapeDtypeStru...  24.3 us
  transfers between devices with their start and end apart: 2, of which 2 were waited for; matrix products, arithmetic and copies ran while one was open for 0% of the time, Pallas kernels for 14%

profile of v14, /device:TPU:113, one launch (start us, length us, event | category | flops | bytes accessed | tf_op | source)
XLA Modules:
  0.0 169.8 jit_solution(6139673675703569433)
XLA Ops:
  0.6 137.5 %attention.1 = (bf16[32,1024,256]{2,1,0:T(8,128)(2,1)}, bf16[32,1024,256]{2,1,0:T(8,128)(2,1)}, bf16[23,64,256]{2,1,0:T(8,128)(2,1)}, bf16[23,64,256]{2,1,0:T(8,...) custom-call(bf16[32,1024,256]{2,1,0:T(8,128)(2,1)} %bitcast.18, ...), custom_call_target="tpu_custom_call" | custom-call | tf_op jit(solution)/shard_map/attention/pallas_call | solution.py:451
  138.1 1.3 collective-permute-start
  139.4 1.3 collective-permute-start.1
  140.7 0.0 copy-start
  140.7 24.3 %results.1 = (bf16[32,1024,256]{2,1,0:T(8,128)(2,1)}, bf16[32,1024,256]{2,1,0:T(8,128)(2,1)}, bf16[32,64,256]{2,1,0:T(8,128)(2,1)}, bf16[32,64,256]{2,1,0:T(8,128)(2,1)}) custom-call(bf16[32,1024,256]{2,1,0:T(8,128)(2,1)} %get-tuple-element.15.a_ref, bf16[32,1024,256]{2,1,0:T(8,128)(2,1)} %get-tuple-element.16.b_ref, ...), custom_call_target="tpu_custom_call" | custom-call | flops 12000000000 | bytes 67108864 | tf_op jit(solution)/shard_map/results/pallas_call | solution.py:485
  165.0 3.0 %collective-permute-done = f32[9,128,256]{2,1,0:T(8,128)S(1)} collective-permute-done((f32[9,128,256]{2,1,0:T(8,128)}, f32[9,128,256]{2,1,0:T(8,128)S(1)}, u32[]{:S(2)}, u32[]{:S(2)}) %collective-permute-start) | collective-permute-done | bytes 1179680 | tf_op jit(solution)/shard_map/ppermute | solution.py:499
  168.0 0.7 collective-permute-done.1
  168.7 0.0 copy-done
  168.7 0.2 add_add_fusion
  168.9 0.9 fusion.4
Async XLA Ops:
  138.1 29.9 %collective-permute-start = (f32[9,128,256]{2,1,0:T(8,128)}, f32[9,128,256]{2,1,0:T(8,128)S(1)}, u32[]{:S(2)}, u32[]{:S(2)}) collective-permute-start(f32[9,128,256]{2,1,0:T(8,128)} %get-tuple-element.23), channel_id=1, source_target_pairs={{6,0},{7,1},{14,8},{15,9}} | collective-permute-start | bytes 3538952 | tf_op jit(solution)/shard_map/ppermute | solution.py:499
  139.4 29.2 %collective-permute-start.1 = (f32[9,128,256]{2,1,0:T(8,128)}, f32[9,128,256]{2,1,0:T(8,128)S(1)}, u32[]{:S(2)}, u32[]{:S(2)}) collective-permute-start(f32[9,128,256]{2,1,0:T(8,128)} %get-tuple-element.24), channel_id=1, source_target_pairs={{2,0},{3,1},{4,2},{5,3},{6,4},{7,5},{10,8},{11,9},{12,10},{13,11},... | collective-permute-start | bytes 3538952 | tf_op jit(solution)/shard_map/ppermute | solution.py:500
  140.7 27.9 %copy-start = (f32[9,128,256]{2,1,0:T(8,128)S(1)}, f32[9,128,256]{2,1,0:T(8,128)}, u32[]{:S(2)}) copy-start(f32[9,128,256]{2,1,0:T(8,128)} %get-tuple-element.22) | copy-start | bytes 3538948

commit v15 on v14

--- a/solution.py
+++ b/solution.py
@@ -22,7 +22,7 @@
 HOPS = ((1, 1, 2, None), (1, 0, 2, None), (2, 1, 3, 0), (2, 2, 3, None), (0, 1, 3, 1), (1, 1, 0, 1), (0, 0, 3, None), (0, 0, 1, None))
 PUSH = {0: (0, 8), 1: (2, 12), 2: (3, 3), 3: (2, 5)}
 TAKE = {0: (0, 10), 1: (2, 6), 2: (2, 2), 3: (0, 1)}
-SENDS = {(3, 0): ((1, 2, 0, False, None), (0, 0, 1, False, 1), (2, 2, 1, False, 0)), (3, 1): ((2, 2, 0, False, 0), (0, 0, 0, True, 1), (1, 0, 2, False, None)), (2, 0): ((1, 1, 1, True, 0), (0, 1, 0, False, None)), (2, 1): ((1, 1, 0, False, 0), (0, 3, 0, False, None)), (1, 0): ((0, 0, 0, True, 0),), (1, 1): ((0, 0, 1, False, 0),)}
+SENDS = {(3, 0): ((1, 2, 0, False, None), (0, 0, 1, False, 1), (2, 2, 1, False, 0)), (3, 1): ((2, 2, 0, False, 0), (0, 0, 0, True, 1), (1, 0, 2, False, None)), (2, 0): ((1, 1, 1, True, 1), (0, 1, 0, False, None)), (2, 1): ((1, 1, 0, False, 1), (0, 3, 0, False, None)), (1, 0): ((0, 0, 0, True, 0),), (1, 1): ((0, 0, 1, False, 0),)}
 RELAY = {(3, 1): (3, 0), (2, 0): (8, 0), (1, 0): (8, 0), (0, 1): (7, 2)}
 FINISH = {(3, 0): (1, ()), (3, 1): (1, ()), (2, 0): (7, (1,)), (2, 1): (5, (0,)), (1, 0): (10, (1,)), (1, 1): (10, (0, 1)), (0, 0): (10, (0, 1)), (0, 1): (9, (0, 1))}
 LAG_MAX = 10
@@ -31,7 +31,7 @@
 
 
 def attention_kernel(n_dev, n_heads, *refs):
-    (q_ref, g_ref, k_ref, v_ref, doc_ref, o_ref, dq_ref, dk_ref, dv_ref, near_ref, far_ref, own_ref,
+    (q_ref, g_ref, k_ref, v_ref, doc_ref, o_ref, dq_ref, dk_ref, dv_ref, even_ref, odd_ref, own_ref,
      kv, rx0, rx1, rx2, acc, part, prx, qg, odq, pb, dsb, fin_k, fin_v, own, docs, kdoc, odoc, vis,
      load_sem, doc_tx, doc_rx, kv_tx, kv_rx, kvp_tx, kvp_rx, qg_sem, odq_sem,
      part_tx, prx_sem, rx_sem, tx_sem, fwd_tx, late_sem) = refs
@@ -244,7 +244,7 @@
 
                 @pl.when(b >= first_late)
                 def _():
-                    pltpu.make_async_copy(unit, (near_ref, far_ref)[late].at[b - first_late], sem).start()
+                    pltpu.make_async_copy(unit, (even_ref, odd_ref)[late].at[b - first_late], sem).start()
 
         def got(buf, b):
             local_wait(rx[buf].at[b], rx_sem.at[buf, b])
@@ -481,7 +481,7 @@
             ],
             compiler_params=pltpu.CompilerParams(collective_id=0, has_side_effects=True, vmem_limit_bytes=63 * 1024 * 1024),
         )(query.reshape(rows_shape), grad_out.reshape(rows_shape), keys.reshape(kv_shape), values.reshape(kv_shape), doc_id)
-        attn_out, grad_query, grad_keys, grad_values, near, far, own = out
+        attn_out, grad_query, grad_keys, grad_values, even, odd, own = out
         attn_out, grad_query, grad_keys, grad_values = pl.pallas_call(
             copy_kernel,
             name='results',
@@ -494,11 +494,11 @@
             cost_estimate=pl.CostEstimate(flops=12_000_000_000, bytes_accessed=8 * n_seq * n_rows * head_dim,
                                           transcendentals=0),
         )(attn_out, grad_query, grad_keys, grad_values)
-        to_near = [(d, d - 2) for d in range(2, n_dev)]
-        to_far = [(n_dev - 2 + e, e) for e in range(2)]
-        from_far = lax.ppermute(far, 'cp', to_far)
-        from_near = lax.ppermute(near, 'cp', to_near)
-        late = own + from_far + from_near
+        odd_hops = [(n_dev - 2 + e, e) for e in range(2)] + [(d + 2, d) for d in range(2, n_dev - 4)]
+        even_hops = [(d + 2, d) for d in range(2)] + [(d + 2, d) for d in range(n_dev - 4, n_dev - 2)]
+        from_odd = lax.ppermute(odd, 'cp', odd_hops)
+        from_even = lax.ppermute(even, 'cp', even_hops)
+        late = own + from_odd + from_even
         late_keys = (late[:, 0:piece] * head_dim ** -0.5).astype(bf16)
         late_values = late[:, piece:two].astype(bf16)
         grad_keys = lax.dynamic_update_slice(grad_keys, late_keys, (n_seq - N_LATE, 0, 0))

time: 170 us -> 172 us (1.012); the launches traced: 170 us -> 170 us
  no operation moved by 1% of the time
where the time goes in v15:
time: 172 us; the launch traced here: 170 us
  Pallas kernels  162 us (94%)
  waiting for transfers between devices  3.58 us (2%)
  starting transfers between devices  2.62 us (2%)
    pallas_call x1, Pallas kernels, per_device(): pl.pallas_call(functools.partial(attention_kernel, n_dev, n_heads), name=...  137 us
    pallas_call x1, Pallas kernels, per_device(): pl.pallas_call(copy_kernel, name='results', out_shape=[jax.ShapeDtypeStru...  24.3 us
  transfers between devices with their start and end apart: 2, of which 2 were waited for; matrix products, arithmetic and copies ran while one was open for 0% of the time, Pallas kernels for 14%

profile of v15, /device:TPU:113, one launch (start us, length us, event | category | flops | bytes accessed | tf_op | source)
XLA Modules:
  0.0 169.7 jit_solution(3331142335835221958)
XLA Ops:
  0.6 137.5 %attention.1 = (bf16[32,1024,256]{2,1,0:T(8,128)(2,1)}, bf16[32,1024,256]{2,1,0:T(8,128)(2,1)}, bf16[23,64,256]{2,1,0:T(8,128)(2,1)}, bf16[23,64,256]{2,1,0:T(8,...) custom-call(bf16[32,1024,256]{2,1,0:T(8,128)(2,1)} %bitcast.18, ...), custom_call_target="tpu_custom_call" | custom-call | tf_op jit(solution)/shard_map/attention/pallas_call | solution.py:451
  138.1 1.3 collective-permute-start
  139.4 1.3 collective-permute-start.1
  140.7 0.0 copy-start
  140.7 24.3 %results.1 = (bf16[32,1024,256]{2,1,0:T(8,128)(2,1)}, bf16[32,1024,256]{2,1,0:T(8,128)(2,1)}, bf16[32,64,256]{2,1,0:T(8,128)(2,1)}, bf16[32,64,256]{2,1,0:T(8,128)(2,1)}) custom-call(bf16[32,1024,256]{2,1,0:T(8,128)(2,1)} %get-tuple-element.15.a_ref, bf16[32,1024,256]{2,1,0:T(8,128)(2,1)} %get-tuple-element.16.b_ref, ...), custom_call_target="tpu_custom_call" | custom-call | flops 12000000000 | bytes 67108864 | tf_op jit(solution)/shard_map/results/pallas_call | solution.py:485
  165.0 3.0 %collective-permute-done = f32[9,128,256]{2,1,0:T(8,128)S(1)} collective-permute-done((f32[9,128,256]{2,1,0:T(8,128)}, f32[9,128,256]{2,1,0:T(8,128)S(1)}, u32[]{:S(2)}, u32[]{:S(2)}) %collective-permute-start) | collective-permute-done | bytes 1179680 | tf_op jit(solution)/shard_map/ppermute | solution.py:499
  168.0 0.6 collective-permute-done.1
  168.6 0.0 copy-done
  168.6 0.2 add_add_fusion
  168.8 0.9 fusion.4
Async XLA Ops:
  138.1 29.9 %collective-permute-start = (f32[9,128,256]{2,1,0:T(8,128)}, f32[9,128,256]{2,1,0:T(8,128)S(1)}, u32[]{:S(2)}, u32[]{:S(2)}) collective-permute-start(f32[9,128,256]{2,1,0:T(8,128)} %get-tuple-element.23), channel_id=1, source_target_pairs={{6,0},{7,1},{4,2},{5,3},{14,8},{15,9},{12,10},{13,11}} | collective-permute-start | bytes 3538952 | tf_op jit(solution)/shard_map/ppermute | solution.py:499
  139.4 29.2 %collective-permute-start.1 = (f32[9,128,256]{2,1,0:T(8,128)}, f32[9,128,256]{2,1,0:T(8,128)S(1)}, u32[]{:S(2)}, u32[]{:S(2)}) collective-permute-start(f32[9,128,256]{2,1,0:T(8,128)} %get-tuple-element.24), channel_id=1, source_target_pairs={{2,0},{3,1},{6,4},{7,5},{10,8},{11,9},{14,12},{15,13}} | collective-permute-start | bytes 3538952 | tf_op jit(solution)/shard_map/ppermute | solution.py:500
  140.7 27.9 %copy-start = (f32[9,128,256]{2,1,0:T(8,128)S(1)}, f32[9,128,256]{2,1,0:T(8,128)}, u32[]{:S(2)}) copy-start(f32[9,128,256]{2,1,0:T(8,128)} %get-tuple-element.22) | copy-start | bytes 3538948

commit v16 on v14

--- a/solution.py
+++ b/solution.py
@@ -16,7 +16,7 @@
 N_COPY = 32
 N_FIRST = 1
 N_TURN = 2
-N_LATE = 9
+N_LATE = 8
 
 
 HOPS = ((1, 1, 2, None), (1, 0, 2, None), (2, 1, 3, 0), (2, 2, 3, None), (0, 1, 3, 1), (1, 1, 0, 1), (0, 0, 3, None), (0, 0, 1, None))

time: 170 us -> 170 us (level)
  Pallas kernels: 162 us -> 165 us
  waiting for transfers between devices: 3.65 us -> 0.8 us
    ppermute x1, waiting for transfers between devices: 2.98 us -> 0.13 us  [per_device(): from_far = lax.ppermute(far, 'cp', to_far)]
    pallas_call x1, Pallas kernels: 137 us -> 140 us  [per_device(): pl.pallas_call(functools.partial(attention_kernel, n_dev, n_heads), name=...]
where the time goes in v16:
time: 170 us
  Pallas kernels  165 us (97%)
  starting transfers between devices  2.62 us (2%)
    pallas_call x1, Pallas kernels, per_device(): pl.pallas_call(functools.partial(attention_kernel, n_dev, n_heads), name=...  140 us
    pallas_call x1, Pallas kernels, per_device(): pl.pallas_call(copy_kernel, name='results', out_shape=[jax.ShapeDtypeStru...  24.3 us
  transfers between devices with their start and end apart: 2, of which 2 were waited for; matrix products, arithmetic and copies ran while one was open for 0% of the time, Pallas kernels for 14%

profile of v16, /device:TPU:113, one launch (start us, length us, event | category | flops | bytes accessed | tf_op | source)
XLA Modules:
  0.0 169.7 jit_solution(10545920785634684426)
XLA Ops:
  0.6 140.3 %attention.1 = (bf16[32,1024,256]{2,1,0:T(8,128)(2,1)}, bf16[32,1024,256]{2,1,0:T(8,128)(2,1)}, bf16[24,64,256]{2,1,0:T(8,128)(2,1)}, bf16[24,64,256]{2,1,0:T(8,...) custom-call(bf16[32,1024,256]{2,1,0:T(8,128)(2,1)} %bitcast.18, ...), custom_call_target="tpu_custom_call" | custom-call | tf_op jit(solution)/shard_map/attention/pallas_call | solution.py:451
  140.9 1.3 collective-permute-start
  142.2 1.3 collective-permute-start.1
  143.5 0.0 copy-start
  143.6 24.3 %results.1 = (bf16[32,1024,256]{2,1,0:T(8,128)(2,1)}, bf16[32,1024,256]{2,1,0:T(8,128)(2,1)}, bf16[32,64,256]{2,1,0:T(8,128)(2,1)}, bf16[32,64,256]{2,1,0:T(8,128)(2,1)}) custom-call(bf16[32,1024,256]{2,1,0:T(8,128)(2,1)} %get-tuple-element.15.a_ref, bf16[32,1024,256]{2,1,0:T(8,128)(2,1)} %get-tuple-element.16.b_ref, ...), custom_call_target="tpu_custom_call" | custom-call | flops 12000000000 | bytes 67108864 | tf_op jit(solution)/shard_map/results/pallas_call | solution.py:485
  167.9 0.1 collective-permute-done
  168.0 0.7 collective-permute-done.1
  168.7 0.0 copy-done
  168.7 0.2 add_add_fusion
  168.9 0.9 fusion.4
Async XLA Ops:
  140.9 27.1 %collective-permute-start = (f32[8,128,256]{2,1,0:T(8,128)}, f32[8,128,256]{2,1,0:T(8,128)S(1)}, u32[]{:S(2)}, u32[]{:S(2)}) collective-permute-start(f32[8,128,256]{2,1,0:T(8,128)} %get-tuple-element.23), channel_id=1, source_target_pairs={{6,0},{7,1},{14,8},{15,9}} | collective-permute-start | bytes 3145736 | tf_op jit(solution)/shard_map/ppermute | solution.py:499
  142.2 26.4 %collective-permute-start.1 = (f32[8,128,256]{2,1,0:T(8,128)}, f32[8,128,256]{2,1,0:T(8,128)S(1)}, u32[]{:S(2)}, u32[]{:S(2)}) collective-permute-start(f32[8,128,256]{2,1,0:T(8,128)} %get-tuple-element.24), channel_id=1, source_target_pairs={{2,0},{3,1},{4,2},{5,3},{6,4},{7,5},{10,8},{11,9},{12,10},{13,11},... | collective-permute-start | bytes 3145736 | tf_op jit(solution)/shard_map/ppermute | solution.py:500
  143.5 25.1 %copy-start = (f32[8,128,256]{2,1,0:T(8,128)S(1)}, f32[8,128,256]{2,1,0:T(8,128)}, u32[]{:S(2)}) copy-start(f32[8,128,256]{2,1,0:T(8,128)} %get-tuple-element.22) | copy-start | bytes 3145732

commit v17 on v16

--- a/solution.py
+++ b/solution.py
@@ -157,16 +157,18 @@
             def at_step(t):
                 b = jnp.minimum(start + 2 * t, t + most)
                 pl.when(b < n_seq)(lambda: fn(b))
+
+            def at_early_step(t):
                 if most - start > 0:
-                    pl.when(t < most - start)(lambda: fn(b + 1))
-
-            return start, at_step
+                    pl.when(t < most - start)(lambda: fn(start + 2 * t + 1))
+
+            return start, at_step, at_early_step
 
         def arrived(b):
             local_wait(kv.at[b, :, here, 1 - core], kvp_rx.at[b])
 
-        n_push, push_at = ramp(PUSH[c], push)
-        n_take, take_at = ramp(TAKE[c], take)
+        n_push, push_at, push_early = ramp(PUSH[c], push)
+        n_take, take_at, take_early = ramp(TAKE[c], take)
         for b in range(n_push):
             if b == N_FIRST:
                 for copy in own_rest:
@@ -337,7 +339,10 @@
             @pl.when(t < n_seq)
             def _():
                 push_at(t)
+                push_early(t)
                 take_at(t)
+                if c < n_chip - 1:
+                    take_early(t)
 
                 @pl.when(t + 1 < n_seq)
                 def _():
@@ -354,6 +359,8 @@
                 compute(t)
                 odq_start(t)
                 part_copy(t).start()
+                if c == n_chip - 1:
+                    take_early(t)
 
             when_seq(t - 1, merge_partner)
             for e in range(2):

time: 170 us -> 170 us (level)
  no operation moved by 1% of the time
where the time goes in v17:
time: 170 us
  Pallas kernels  165 us (97%)
  starting transfers between devices  2.62 us (2%)
    pallas_call x1, Pallas kernels, per_device(): pl.pallas_call(functools.partial(attention_kernel, n_dev, n_heads), name=...  140 us
    pallas_call x1, Pallas kernels, per_device(): pl.pallas_call(copy_kernel, name='results', out_shape=[jax.ShapeDtypeStru...  24.3 us
  transfers between devices with their start and end apart: 2, of which 2 were waited for; matrix products, arithmetic and copies ran while one was open for 0% of the time, Pallas kernels for 14%

profile of v17, /device:TPU:113, one launch (start us, length us, event | category | flops | bytes accessed | tf_op | source)
XLA Modules:
  0.0 169.7 jit_solution(1776187792670347399)
XLA Ops:
  0.6 140.3 %attention.1 = (bf16[32,1024,256]{2,1,0:T(8,128)(2,1)}, bf16[32,1024,256]{2,1,0:T(8,128)(2,1)}, bf16[24,64,256]{2,1,0:T(8,128)(2,1)}, bf16[24,64,256]{2,1,0:T(8,...) custom-call(bf16[32,1024,256]{2,1,0:T(8,128)(2,1)} %bitcast.18, ...), custom_call_target="tpu_custom_call" | custom-call | tf_op jit(solution)/shard_map/attention/pallas_call | solution.py:458
  140.9 1.3 collective-permute-start
  142.2 1.3 collective-permute-start.1
  143.5 0.0 copy-start
  143.6 24.3 %results.1 = (bf16[32,1024,256]{2,1,0:T(8,128)(2,1)}, bf16[32,1024,256]{2,1,0:T(8,128)(2,1)}, bf16[32,64,256]{2,1,0:T(8,128)(2,1)}, bf16[32,64,256]{2,1,0:T(8,128)(2,1)}) custom-call(bf16[32,1024,256]{2,1,0:T(8,128)(2,1)} %get-tuple-element.15.a_ref, bf16[32,1024,256]{2,1,0:T(8,128)(2,1)} %get-tuple-element.16.b_ref, ...), custom_call_target="tpu_custom_call" | custom-call | flops 12000000000 | bytes 67108864 | tf_op jit(solution)/shard_map/results/pallas_call | solution.py:492
  167.9 0.1 collective-permute-done
  168.0 0.7 collective-permute-done.1
  168.7 0.0 copy-done
  168.7 0.2 add_add_fusion
  168.9 0.9 fusion.4
Async XLA Ops:
  140.9 27.1 %collective-permute-start = (f32[8,128,256]{2,1,0:T(8,128)}, f32[8,128,256]{2,1,0:T(8,128)S(1)}, u32[]{:S(2)}, u32[]{:S(2)}) collective-permute-start(f32[8,128,256]{2,1,0:T(8,128)} %get-tuple-element.23), channel_id=1, source_target_pairs={{6,0},{7,1},{14,8},{15,9}} | collective-permute-start | bytes 3145736 | tf_op jit(solution)/shard_map/ppermute | solution.py:506
  142.2 26.4 %collective-permute-start.1 = (f32[8,128,256]{2,1,0:T(8,128)}, f32[8,128,256]{2,1,0:T(8,128)S(1)}, u32[]{:S(2)}, u32[]{:S(2)}) collective-permute-start(f32[8,128,256]{2,1,0:T(8,128)} %get-tuple-element.24), channel_id=1, source_target_pairs={{2,0},{3,1},{4,2},{5,3},{6,4},{7,5},{10,8},{11,9},{12,10},{13,11},... | collective-permute-start | bytes 3145736 | tf_op jit(solution)/shard_map/ppermute | solution.py:507
  143.5 25.1 %copy-start = (f32[8,128,256]{2,1,0:T(8,128)S(1)}, f32[8,128,256]{2,1,0:T(8,128)}, u32[]{:S(2)}) copy-start(f32[8,128,256]{2,1,0:T(8,128)} %get-tuple-element.22) | copy-start | bytes 3145732
